TPU v7x, 128 devices: a whole 4x4x4 slice. The times are simulated.
128 devices in a mesh: dom: 128 (over x, z, y, core).
Axes of the slice: x: 4, y: 4, z: 4, core: 2. Of those that a mesh axis runs over, the one named last changes fastest.
Arguments:
- features: bfloat16 [32768, 512], P('dom'), may hold values from -6 to 6
- w_one: bfloat16 [9, 512, 512], replicated, may hold values from -0.25 to 0.25
- w_two: bfloat16 [8, 512, 349], replicated, may hold values from -0.25 to 0.25
- self_two: bfloat16 [512, 349], replicated, may hold values from -80 to 80
- edge_src: int32 [8, 256, 256], P(None, 'dom'), may hold values from 0 to 1279, as said below
- edge_dst: int32 [8, 256, 256], P(None, 'dom'), may hold values from -1 to 127, as said below
- send_rows: int32 [128, 128, 8], P('dom'), may hold values from 0 to 255
- send_count: int32 [128, 128], P('dom'), may hold values from 1 to 8, as said below
- labels: int32 [32768], P('dom'), may hold values from -1 to 348
Outputs:
- logits: float32 [32768, 349], P('dom')
- loss: float32 [], replicated
- grad_one: float32 [4608, 512], P('dom')
- grad_two: float32 [4608, 349], P('dom')
Inputs may be any that keep to these rules, and one draw needn't show every extreme that they name: `send_rows`: entry [p, q, s] is a row of partition p's own nodes, rows may repeat. `send_count`: entry [p, q] counts the live slots p sends to q; every row reaches 8 at some q. `edge_src`: index into the destination partition's table: its 256 own rows, then 8 slots from each partition in order. `edge_dst`: -1 marks an empty edge slot.
All inputs are finite; a program needn't handle non-finite values.
Results may differ from a plain program's by a relative error of at most 0.0085.
The roundings to bfloat16 on the way count: a program that leaves them out, or rounds other values in their place, can miss the bound.
Values may be sent and summed in bfloat16 or wider, within the bound.
A program may use at most 128 MiB of HBM per device.

v0:
```python
import jax
import jax.numpy as jnp
from jax import lax
from jax.sharding import Mesh
from jax.sharding import PartitionSpec as P

DOM = ("dom_0", "dom_1", "dom_2", "dom_3")


loss_scale = 256.0


def copy_for_each(value, axis):
    count = lax.axis_size(axis)
    return lax.all_to_all(
        jnp.broadcast_to(value[None], (count, *value.shape)), axis, 0, 0, tiled=True
    )


def taken_together(value, axis):
    everything = copy_for_each(value, axis)
    return jnp.sum(everything, axis=0)


def one_axis_at_a_time(value, axes):
    far, near = axes
    return taken_together(taken_together(value, near), far)


def in_one(arrays, axis):
    ends = [0]
    for a in arrays:
        ends.append(ends[-1] + a.size)
    running = one_axis_at_a_time(jnp.concatenate([a.ravel() for a in arrays]), axis)
    return tuple((running[b:e].reshape(a.shape) for a, b, e in zip(arrays, ends, ends[1:])))


def in_blocks(value, dim, count):
    shape = value.shape
    parts = value.reshape(*shape[:dim], count, shape[dim] // count, *shape[dim + 1 :])
    return jnp.moveaxis(parts, dim, 0)


def summed_on_arrival(value, axis, dim):
    parts = in_blocks(value, dim, lax.axis_size(axis))
    arrived = lax.all_to_all(parts, axis, split_axis=0, concat_axis=0, tiled=True)
    return arrived.astype(jnp.float32).sum(axis=0)


def summed_rows(value, axes, dim):
    far, near = axes
    own = summed_on_arrival(in_blocks(value, dim, lax.axis_size(far)), near, dim + 1)
    return jnp.sum(
        lax.all_to_all(own.astype(jnp.bfloat16), far, 0, 0, tiled=True).astype(jnp.float32), axis=0
    )


def pack_rows(values, picks, live_slot):
    chosen = values[picks]
    return jnp.where(live_slot[:, :, None], chosen, jnp.zeros_like(chosen))


def aggregate(node_table, sources, targets):
    blocks = sources.shape[1]
    block_rows = jnp.arange(128, dtype=jnp.int32)

    def one_relation(edge_pair):
        src_rel, dst_rel = edge_pair
        picked = node_table[src_rel]
        one_hot = dst_rel[:, None, :] == block_rows[None, :, None]
        sums = jnp.einsum(
            "bve,bed->bvd", one_hot.astype(jnp.bfloat16), picked, preferred_element_type=jnp.float32
        )
        counts = jnp.sum(one_hot.astype(jnp.float32), axis=2)
        norm_rows = 1.0 / jnp.maximum(counts, 1.0)
        averaged = (sums * norm_rows[:, :, None]).astype(jnp.bfloat16)
        return (averaged.reshape(blocks * 128, -1), norm_rows.reshape(blocks * 128))

    return lax.map(one_relation, (sources, targets))


def spread_back(spread, sources, targets, table_rows):
    blocks = sources.shape[1]
    block_rows = jnp.arange(128, dtype=jnp.int32)

    def add_relation(total, edge_pack):
        grad_rel, src_rel, dst_rel = edge_pack
        one_hot = (dst_rel[:, None, :] == block_rows[None, :, None]).astype(jnp.bfloat16)
        per_edge = jnp.einsum(
            "bve,bvd->bed",
            one_hot,
            grad_rel.reshape(blocks, 128, -1),
            preferred_element_type=jnp.float32,
        )
        added = jax.ops.segment_sum(
            per_edge.reshape(-1, per_edge.shape[-1]), src_rel.reshape(-1), num_segments=table_rows
        )
        return (total + added, None)

    start = jnp.zeros((table_rows, spread.shape[-1]), jnp.float32)
    total, unused = lax.scan(add_relation, start, (spread, sources, targets))
    return total


def stacked_rows(averaged, own_rows):
    stacked = jnp.concatenate([averaged, own_rows[None]], axis=0)
    return jnp.swapaxes(stacked, 1, 2).reshape(-1, stacked.shape[1])


def on_device(features, w_one, w_two, self_two, edge_src, edge_dst, send_rows, send_count, labels):
    peers = lax.axis_size(DOM)
    node_rows = features.shape[0]
    width = features.shape[1]
    relations = w_two.shape[0]
    picks = send_rows[0]
    slots = picks.shape[1]
    live_slot = jnp.arange(slots, dtype=jnp.int32)[None, :] < send_count[0][:, None]
    table_rows = node_rows + peers * slots
    arrived = lax.all_to_all(
        pack_rows(features, picks, live_slot), DOM, split_axis=0, concat_axis=0, tiled=True
    )
    node_table = jnp.concatenate([features, arrived.reshape(peers * slots, width)], axis=0)
    averaged_one, norm_one = aggregate(node_table, edge_src, edge_dst)
    before_relu = jnp.einsum(
        "rnd,rde->ne", averaged_one, w_one[:relations], preferred_element_type=jnp.float32
    )
    before_relu = before_relu + jnp.dot(
        features, w_one[relations], preferred_element_type=jnp.float32
    )
    hidden = jnp.maximum(before_relu, 0.0).astype(jnp.bfloat16)
    arrived_hidden = lax.all_to_all(
        pack_rows(hidden, picks, live_slot), DOM, split_axis=0, concat_axis=0, tiled=True
    )
    hidden_table = jnp.concatenate([hidden, arrived_hidden.reshape(peers * slots, width)], axis=0)
    averaged_two, norm_two = aggregate(hidden_table, edge_src, edge_dst)
    logits = jnp.einsum("rnd,rdc->nc", averaged_two, w_two, preferred_element_type=jnp.float32)
    logits = logits + jnp.dot(hidden, self_two, preferred_element_type=jnp.float32)
    classes = logits.shape[1]
    labelled = labels >= 0
    log_total = jax.nn.logsumexp(logits, axis=1)
    one_hot = (jnp.arange(classes, dtype=jnp.int32)[None, :] == labels[:, None]).astype(jnp.float32)
    picked = jnp.sum(logits * one_hot, axis=1)
    local_total = jnp.sum(jnp.where(labelled, log_total - picked, 0.0))
    local_count = jnp.sum(labelled.astype(jnp.float32))
    total, label_count = in_one((local_total, local_count), (("dom_0", "dom_1", "dom_2"), "dom_3"))
    loss = total / label_count
    softmax_out = jnp.exp(logits - log_total[:, None])
    grad_logits = (
        loss_scale * (softmax_out - one_hot) * labelled[:, None].astype(jnp.float32) / label_count
    ).astype(jnp.bfloat16)
    left_two = stacked_rows(averaged_two, hidden)
    spread = jnp.einsum("nc,rdc->rnd", grad_logits, w_two, preferred_element_type=jnp.float32)
    spread = (spread * norm_two[:, :, None]).astype(jnp.bfloat16)
    table_grad = spread_back(spread, edge_src, edge_dst, table_rows)
    local_grad = table_grad[:node_rows] + jnp.dot(
        grad_logits, self_two.T, preferred_element_type=jnp.float32
    )
    outgoing = table_grad[node_rows:].astype(jnp.bfloat16).reshape(peers, slots, width)
    returned = lax.all_to_all(outgoing, DOM, split_axis=0, concat_axis=0, tiled=True)
    returned = jnp.where(live_slot[:, :, None], returned.astype(jnp.float32), 0.0)
    grad_hidden = local_grad + jax.ops.segment_sum(
        returned.reshape(peers * slots, width), picks.reshape(-1), num_segments=node_rows
    )
    grad_pre = jnp.where(before_relu > 0.0, grad_hidden, 0.0).astype(jnp.bfloat16)
    left_one = stacked_rows(averaged_one, features)
    joined = summed_rows(
        jnp.concatenate(
            [
                jnp.dot(left_one, grad_pre, preferred_element_type=jnp.float32),
                jnp.dot(left_two, grad_logits, preferred_element_type=jnp.float32),
            ],
            axis=1,
        ).astype(jnp.bfloat16),
        (("dom_0", "dom_1", "dom_2"), "dom_3"),
        0,
    )
    grad_one = joined[:, :width]
    grad_two = joined[:, width:]
    return (logits, loss, grad_one, grad_two)


def solution(mesh):
    split = Mesh(mesh.devices.reshape(4, 4, 4, 2), ("dom_0", "dom_1", "dom_2", "dom_3"))
    return jax.shard_map(
        on_device,
        mesh=split,
        in_specs=(
            P(DOM, None),
            P(),
            P(),
            P(),
            P(None, DOM, None),
            P(None, DOM, None),
            P(DOM, None, None),
            P(DOM, None),
            P(DOM),
        ),
        out_specs=(P(DOM, None), P(), P(DOM, None), P(DOM, None)),
        check_vma=False,
    )
```

profile of v0, /device:TPU:0, one launch (start us, length us, event | category | flops | bytes accessed | tf_op | source)
XLA Modules:
  0.0 482.4 jit_solution(6401178279022526690)
XLA Ops:
  2.4 6.1 %gather_fusion.2 = bf16[1024,512]{1,0:T(8,128)(2,1)} fusion(bf16[256,512]{1,0:T(8,128)(2,1)} %param.15, s32[1024]{0:T(1024)S(1)} %broadcast_clamp_fusion), kind=kCustom, calls=%fused_computation.2 | custom fusion | bytes 2101248 | tf_op jit(solution)/shard_map/gather | solution.py:59
  11.0 11.7 %all-to-all-start = ((bf16[128,8,512]{2,1,0:T(8,128)(2,1)}), bf16[128,8,512]{2,1,0:T(8,128)(2,1)}, u32[]{:S(2)}, u32[]{:S(2)}) async-start(bf16[128,8,512]{2,1,0:T(8,128)(2,1)} %bitcast_select_fusion.1), calls=%async_computation | async-start | bytes 2097152 | tf_op jit(solution)/shard_map/all_to_all | solution.py:119
  22.8 18.7 %all-to-all-done = bf16[128,8,512]{2,1,0:T(8,128)(2,1)} async-done(((bf16[128,8,512]{2,1,0:T(8,128)(2,1)}), bf16[128,8,512]{2,1,0:T(8,128)(2,1)}, u32[]{:S(2)}, u32[]{:S(2)}) %all-to-all-start) | async-done | bytes 1048608 | tf_op jit(solution)/shard_map/all_to_all | solution.py:119
  45.4 61.3 %while.35 = (s32[]{:T(128)}, bf16[8,256,512]{2,1,0:T(8,128)(2,1)}, s32[8,2,256]{2,1,0:T(2,128)}, s32[8,2,256]{2,1,0:T(2,128)}, bf16[1280,512]{1,0:T(8,128)(2,1)}, /*index=5*/s32[]{:T(128)}) while((s32[]{:T(128)}, bf16[8,256,512]{2,1,0:T(8,128)(2,1)}, s32[8,2,256]{2,1,0:T(2,128)}, s32[8,2,256]{2,1,0:T(2,128)}, ...), condition=%wide.region_2.3_spmd.clone, body=%wide.region_0.2_spmd.clone.sunk | while | flops 67635968 | bytes 2388057 | solution.py:79
  46.1 4.1 gather_fusion
  53.7 4.1 gather_fusion
  61.4 4.1 gather_fusion
  69.1 4.1 gather_fusion
  76.7 4.1 gather_fusion
  84.4 4.1 gather_fusion
  92.0 4.1 gather_fusion
  112.9 5.0 %gather_fusion.3 = bf16[1024,512]{1,0:T(8,128)(2,1)} fusion(bf16[256,512]{1,0:T(8,128)(2,1)S(1)} %get-tuple-element.188, s32[1024]{0:T(1024)S(1)} %broadcast_clamp_fusion), kind=kCustom, calls=%fused_computation.3 | custom fusion | bytes 2101248 | tf_op jit(solution)/shard_map/gather | solution.py:59
  120.3 5.8 %all-to-all-start.1 = ((bf16[128,8,512]{2,1,0:T(8,128)(2,1)}), bf16[128,8,512]{2,1,0:T(8,128)(2,1)}, u32[]{:S(2)}, u32[]{:S(2)}) async-start(bf16[128,8,512]{2,1,0:T(8,128)(2,1)} %bitcast_select_fusion), calls=%async_computation.1 | async-start | bytes 2097152 | tf_op jit(solution)/shard_map/all_to_all | solution.py:131
  126.1 18.7 %all-to-all-done.1 = bf16[128,8,512]{2,1,0:T(8,128)(2,1)} async-done(((bf16[128,8,512]{2,1,0:T(8,128)(2,1)}), bf16[128,8,512]{2,1,0:T(8,128)(2,1)}, u32[]{:S(2)}, u32[]{:S(2)}) %all-to-all-start.1) | async-done | bytes 1048608 | tf_op jit(solution)/shard_map/all_to_all | solution.py:131
  148.7 61.6 %while.36 = (s32[]{:T(128)}, bf16[8,256,512]{2,1,0:T(8,128)(2,1)}, f32[8,256]{1,0:T(8,128)S(1)}, s32[8,2,256]{2,1,0:T(2,128)}, s32[8,2,256]{2,1,0:T(2,128)}, /*i...) while((s32[]{:T(128)}, bf16[8,256,512]{2,1,0:T(8,128)(2,1)}, f32[8,256]{1,0:T(8,128)S(1)}, ...), condition=%wide.region_5.6_spmd.clone, body=%wide.region_3.5_spmd.clone.sunk | while | flops 67635968 | bytes 2390125 | solution.py:79
  149.4 4.1 gather_fusion.1
  157.1 4.1 gather_fusion.1
  164.8 4.1 gather_fusion.1
  172.5 4.1 gather_fusion.1
  180.2 4.1 gather_fusion.1
  187.9 4.1 gather_fusion.1
  195.6 4.1 gather_fusion.1
  203.3 4.1 gather_fusion.1
  220.6 14.3 %all_to_all.38 = f32[64,1,2]{2,1,0:T(1,128)S(1)} all-to-all(f32[64,1,2]{2,1,0:T(1,128)S(1)} %broadcast_in_dim.55), channel_id=1, replica_groups=mesh['dom_0'=4,'dom_1'=4,'dom_2'=4,'dom_3'=2] {'dom_0','dom_1','dom_2'}, dimensions={0} | all-to-all | bytes 1024 | tf_op jit(solution)/shard_map/all_to_all | solution.py:15
  235.6 5.1 %fusion.18 = bf16[8,256,512]{2,1,0:T(8,128)(2,1)} fusion(f32[8,256]{1,0:T(8,128)S(1)} %get-tuple-element.108, bf16[8,512,349]{1,0,2:T(8,128)(2,1)S(1)} %copy-done, f32[256,349]{0,1:T(8,128)} %copy-done.5, f32[]{:T(128)} %bitcast.13, f32[256]{0:T(256)S(1)} %get-tuple-element.185, f32[256]{0:T(256)S(1)} %get-tuple-element.184, s32[256]{0:T(256)S(1)} %copy-done.10), kind=kOutput, calls=%fused_computation.42 | convolution fusion | flops 734628608 | bytes 5324804 | tf_op jit(solution)/shard_map/nc,rdc->rnd/dot_general | solution.py:152
  241.1 71.2 %while.37 = (s32[]{:T(128)}, f32[1280,512]{1,0:T(8,128)S(1)}, s32[8,2,256]{2,1,0:T(2,128)}, s32[8,2,256]{2,1,0:T(2,128)}, bf16[8,256,512]{2,1,0:T(8,128)(2,1)}, /*index=5*/s32[]{:T(128)}) while((s32[]{:T(128)}, f32[1280,512]{1,0:T(8,128)S(1)}, s32[8,2,256]{2,1,0:T(2,128)}, s32[8,2,256]{2,1,0:T(2,128)}, ...), condition=%wide.region_15.16_spmd.clone, body=%wide.region_13.15_spmd.clone.sunk | while | flops 67436544 | bytes 4997209 | solution.py:101
  244.7 5.2 %scatter_fusion = f32[1280,512]{1,0:T(8,128)S(1)} fusion(f32[1280,512]{1,0:T(8,128)S(1)} %get-tuple-element.340, s32[512]{0:T(512)S(1)} %bitcast.147, f32[512,512]{1,0:T(8,128)} %bitcast.140), kind=kCustom, calls=%fused_computation.4.clone.clone.1 | custom fusion | flops 262144 | bytes 3147776 | tf_op jit(solution)/shard_map/while/body/eval_jaxpr/scatter-add | solution.py:95
  253.6 5.2 %scatter_fusion = f32[1280,512]{1,0:T(8,128)S(1)} fusion(f32[1280,512]{1,0:T(8,128)S(1)} %get-tuple-element.340, s32[512]{0:T(512)S(1)} %bitcast.147, f32[512,512]{1,0:T(8,128)} %bitcast.140), kind=kCustom, calls=%fused_computation.4.clone.clone.1 | custom fusion | flops 262144 | bytes 3147776 | tf_op jit(solution)/shard_map/while/body/eval_jaxpr/scatter-add | solution.py:95
  262.5 5.2 %scatter_fusion = f32[1280,512]{1,0:T(8,128)S(1)} fusion(f32[1280,512]{1,0:T(8,128)S(1)} %get-tuple-element.340, s32[512]{0:T(512)S(1)} %bitcast.147, f32[512,512]{1,0:T(8,128)} %bitcast.140), kind=kCustom, calls=%fused_computation.4.clone.clone.1 | custom fusion | flops 262144 | bytes 3147776 | tf_op jit(solution)/shard_map/while/body/eval_jaxpr/scatter-add | solution.py:95
  271.4 5.2 %scatter_fusion = f32[1280,512]{1,0:T(8,128)S(1)} fusion(f32[1280,512]{1,0:T(8,128)S(1)} %get-tuple-element.340, s32[512]{0:T(512)S(1)} %bitcast.147, f32[512,512]{1,0:T(8,128)} %bitcast.140), kind=kCustom, calls=%fused_computation.4.clone.clone.1 | custom fusion | flops 262144 | bytes 3147776 | tf_op jit(solution)/shard_map/while/body/eval_jaxpr/scatter-add | solution.py:95
  280.3 5.2 %scatter_fusion = f32[1280,512]{1,0:T(8,128)S(1)} fusion(f32[1280,512]{1,0:T(8,128)S(1)} %get-tuple-element.340, s32[512]{0:T(512)S(1)} %bitcast.147, f32[512,512]{1,0:T(8,128)} %bitcast.140), kind=kCustom, calls=%fused_computation.4.clone.clone.1 | custom fusion | flops 262144 | bytes 3147776 | tf_op jit(solution)/shard_map/while/body/eval_jaxpr/scatter-add | solution.py:95
  289.2 5.2 %scatter_fusion = f32[1280,512]{1,0:T(8,128)S(1)} fusion(f32[1280,512]{1,0:T(8,128)S(1)} %get-tuple-element.340, s32[512]{0:T(512)S(1)} %bitcast.147, f32[512,512]{1,0:T(8,128)} %bitcast.140), kind=kCustom, calls=%fused_computation.4.clone.clone.1 | custom fusion | flops 262144 | bytes 3147776 | tf_op jit(solution)/shard_map/while/body/eval_jaxpr/scatter-add | solution.py:95
  298.1 5.2 %scatter_fusion = f32[1280,512]{1,0:T(8,128)S(1)} fusion(f32[1280,512]{1,0:T(8,128)S(1)} %get-tuple-element.340, s32[512]{0:T(512)S(1)} %bitcast.147, f32[512,512]{1,0:T(8,128)} %bitcast.140), kind=kCustom, calls=%fused_computation.4.clone.clone.1 | custom fusion | flops 262144 | bytes 3147776 | tf_op jit(solution)/shard_map/while/body/eval_jaxpr/scatter-add | solution.py:95
  307.0 5.2 %scatter_fusion = f32[1280,512]{1,0:T(8,128)S(1)} fusion(f32[1280,512]{1,0:T(8,128)S(1)} %get-tuple-element.340, s32[512]{0:T(512)S(1)} %bitcast.147, f32[512,512]{1,0:T(8,128)} %bitcast.140), kind=kCustom, calls=%fused_computation.4.clone.clone.1 | custom fusion | flops 262144 | bytes 3147776 | tf_op jit(solution)/shard_map/while/body/eval_jaxpr/scatter-add | solution.py:95
  313.4 6.0 %all-to-all-start.4 = ((bf16[128,8,512]{2,1,0:T(8,128)(2,1)}), bf16[128,8,512]{2,1,0:T(8,128)(2,1)}, u32[]{:S(2)}, u32[]{:S(2)}) async-start(bf16[128,8,512]{2,1,0:T(8,128)(2,1)} %fusion.39), calls=%async_computation.4 | async-start | bytes 2097152 | tf_op jit(solution)/shard_map/all_to_all | solution.py:159
  322.8 4.3 copy.53
  327.1 4.7 dot_general.41
  335.0 4.3 copy.57
  339.3 4.7 dot_general.45
  345.9 6.0 %convolution_convert_fusion.1 = bf16[64,2,36,349]{3,0,2,1:T(8,128)(2,1)} fusion(bf16[64,2,36,256]{3,2,1,0:T(8,128)(2,1)} %dot_general.45, f32[256,349]{0,1:T(8,128)} %copy-done.5, f32[]{:T(128)} %bitcast.13, f32[256]{0:T(256)S(1)} %get-tuple-element.185, f32[256]{0:T(256)S(1)} %get-tuple-element.184, s32[256]{0:T(256)S(1)} %copy-done.10), kind=kOutput, calls=%fused_computation.50 | convolution fusion | flops 825627904 | bytes 5936132 | tf_op jit(solution)/shard_map/dot_general | solution.py:170
  351.8 9.1 %scatter_custom_fusion.1 = f32[256,512]{1,0:T(8,128)} fusion(f32[256,512]{1,0:T(8,128)} %convolution_add_fusion, s32[1024]{0:T(1024)S(1)} %reshape.276, bf16[128,8,512]{2,1,0:T(8,128)(2,1)} %all-to-all-done.4, f32[]{:T(128)} %constant.45.clone.1, pred[128,8]{1,0:T(8,128)(4,1)S(1)} %iota_compare_fusion.7), kind=kCustom, calls=%fused_computation.56 | custom fusion | flops 1572864 | bytes 1589760 | tf_op jit(solution)/shard_map/scatter-add | solution.py:161
  361.0 4.6 convolution_convert_fusion
  365.6 8.0 %maximum_bitcast_fusion = bf16[2,64,36,861]{3,1,2,0:T(8,128)(2,1)} fusion(bf16[64,2,36,349]{3,0,2,1:T(8,128)(2,1)} %convolution_convert_fusion.1, bf16[64,2,36,512]{3,0,2,1:T(8,128)(2,1)} %convolution_convert_fusion), kind=kLoop, calls=%fused_computation.40 | loop fusion | flops 15869952 | bytes 15869952 | tf_op jit(solution)/shard_map/transpose | solution.py:41
  373.6 18.3 %all_to_all.39 = bf16[2,64,36,861]{3,1,2,0:T(8,128)(2,1)} all-to-all(bf16[2,64,36,861]{3,1,2,0:T(8,128)(2,1)} %maximum_bitcast_fusion), channel_id=1, replica_groups=mesh['dom_0'=4,'dom_1'=4,'dom_2'=4,'dom_3'=2] {'dom_3'}, dimensions={0} | all-to-all | bytes 15869952 | tf_op jit(solution)/shard_map/all_to_all | solution.py:46
  391.8 8.2 %reduce_sum.99 = bf16[64,36,861]{2,0,1:T(8,128)(2,1)} reduce(bf16[2,64,36,861]{3,1,2,0:T(8,128)(2,1)} %all_to_all.39, bf16[]{:T(256)} %constant.44.clone.1), dimensions={0}, to_apply=%region_17.18 | reduce | flops 1983744 | bytes 11902466 | tf_op jit(solution)/shard_map/reduce_sum | solution.py:47
  400.1 6.6 %copy.59 = bf16[64,36,861]{2,1,0:T(8,128)(2,1)} copy(bf16[64,36,861]{2,0,1:T(8,128)(2,1)} %reduce_sum.99) | data formatting | bytes 7934976 | tf_op jit(solution)/shard_map/reduce_sum | solution.py:47
  406.6 10.1 %all-to-all-start.6 = ((bf16[64,36,861]{2,1,0:T(8,128)(2,1)}), bf16[64,36,861]{2,1,0:T(8,128)(2,1)}, u32[]{:S(2)}, u32[]{:S(2)}) async-start(bf16[64,36,861]{2,1,0:T(8,128)(2,1)} %copy.59), calls=%async_computation.6 | async-start | bytes 9175040 | tf_op jit(solution)/shard_map/all_to_all | solution.py:54
  418.3 58.6 %all-to-all-done.6 = bf16[64,36,861]{2,1,0:T(8,128)(2,1)} async-done(((bf16[64,36,861]{2,1,0:T(8,128)(2,1)}), bf16[64,36,861]{2,1,0:T(8,128)(2,1)}, u32[]{:S(2)}, u32[]{:S(2)}) %all-to-all-start.6) | async-done | bytes 3967520 | tf_op jit(solution)/shard_map/all_to_all | solution.py:54
  (236 shorter events, 135.7 us)
Async XLA Ops:
  0.6 209.7 %copy-start = (bf16[8,512,349]{1,0,2:T(8,128)(2,1)S(1)}, bf16[8,512,349]{1,0,2:T(8,128)(2,1)}, u32[]{:S(2)}) copy-start(bf16[8,512,349]{1,0,2:T(8,128)(2,1)} %param.17) | copy-start | bytes 8577028
  8.5 32.9 %copy-start.2 = (bf16[256,512]{1,0:T(8,128)(2,1)S(1)}, bf16[256,512]{1,0:T(8,128)(2,1)}, u32[]{:S(2)}) copy-start(bf16[256,512]{1,0:T(8,128)(2,1)} %param.15) | copy-start | bytes 786436
  11.0 30.4 %all-to-all-start = ((bf16[128,8,512]{2,1,0:T(8,128)(2,1)}), bf16[128,8,512]{2,1,0:T(8,128)(2,1)}, u32[]{:S(2)}, u32[]{:S(2)}) async-start(bf16[128,8,512]{2,1,0:T(8,128)(2,1)} %bitcast_select_fusion.1), calls=%async_computation | async-start | bytes 2097152 | tf_op jit(solution)/shard_map/all_to_all | solution.py:119
  120.3 24.5 %all-to-all-start.1 = ((bf16[128,8,512]{2,1,0:T(8,128)(2,1)}), bf16[128,8,512]{2,1,0:T(8,128)(2,1)}, u32[]{:S(2)}, u32[]{:S(2)}) async-start(bf16[128,8,512]{2,1,0:T(8,128)(2,1)} %bitcast_select_fusion), calls=%async_computation.1 | async-start | bytes 2097152 | tf_op jit(solution)/shard_map/all_to_all | solution.py:131
  210.3 3.4 copy-start.7
  210.3 4.5 copy-start.10
  214.0 0.7 copy-start.5
  312.2 7.1 %copy-start.9 = (s32[1,128,8]{1,2,0:T(8,128)S(1)}, s32[1,128,8]{1,2,0:T(8,128)}, u32[]{:S(2)}) copy-start(s32[1,128,8]{1,2,0:T(8,128)} %param.21) | copy-start | bytes 12292
  313.4 38.5 %all-to-all-start.4 = ((bf16[128,8,512]{2,1,0:T(8,128)(2,1)}), bf16[128,8,512]{2,1,0:T(8,128)(2,1)}, u32[]{:S(2)}, u32[]{:S(2)}) async-start(bf16[128,8,512]{2,1,0:T(8,128)(2,1)} %fusion.39), calls=%async_computation.4 | async-start | bytes 2097152 | tf_op jit(solution)/shard_map/all_to_all | solution.py:159
  339.3 4.8 copy-start.6
  339.3 4.8 copy-start.8
  345.9 15.1 %copy-start.3 = (bf16[64,2,36,256]{3,2,1,0:T(8,128)(2,1)S(1)}, bf16[64,2,36,256]{3,2,1,0:T(8,128)(2,1)}, u32[]{:S(2)}) copy-start(bf16[64,2,36,256]{3,2,1,0:T(8,128)(2,1)} %dot_general.41) | copy-start | bytes 7077892
  345.9 15.1 %copy-start.4 = (f32[256,512]{1,0:T(8,128)S(1)}, f32[256,512]{1,0:T(8,128)}, u32[]{:S(2)}) copy-start(f32[256,512]{1,0:T(8,128)} %get-tuple-element.189) | copy-start | bytes 1572868
  406.6 70.3 %all-to-all-start.6 = ((bf16[64,36,861]{2,1,0:T(8,128)(2,1)}), bf16[64,36,861]{2,1,0:T(8,128)(2,1)}, u32[]{:S(2)}, u32[]{:S(2)}) async-start(bf16[64,36,861]{2,1,0:T(8,128)(2,1)} %copy.59), calls=%async_computation.6 | async-start | bytes 9175040 | tf_op jit(solution)/shard_map/all_to_all | solution.py:54
  416.7 64.6 %copy-start.1 = (bf16[8,512,349]{1,0,2:T(8,128)(2,1)S(1)}, bf16[8,512,349]{1,0,2:T(8,128)(2,1)}, u32[]{:S(2)}) copy-start(bf16[8,512,349]{1,0,2:T(8,128)(2,1)} %param.17) | copy-start | bytes 8577028
where the time goes:
time: 489 us; the launch traced here: 482 us
  local copies, waits for them, and re-layouts  151 us (31%)
  other arithmetic  103 us (21%)
  waiting for transfers between devices  96.1 us (20%)
  matrix products  58.3 us (12%)
  blocking collectives  36.3 us (7%)
  starting transfers between devices  33.5 us (7%)
    gather x16, local copies, waits for them, and re-layouts, one_relation(): picked = node_table[src_rel]  66.2 us
    all_to_all x1, waiting for transfers between devices, summed_rows(): lax.all_to_all(own.astype(jnp.bfloat16), far, 0, 0, tiled=True)  58.6 us
    scatter-add x8, other arithmetic, add_relation(): jax.ops.segment_sum(per_edge.reshape(-1, per_edge.shape[-1]), src_rel.res...  41.6 us
    dot_general x16, matrix products, one_relation(): jnp.einsum('bve,bed->bvd', one_hot.astype(jnp.bfloat16), picked, preferre...  20.5 us
    all_to_all x1, waiting for transfers between devices, on_device(): lax.all_to_all(pack_rows(features, picks, live_slot), DOM, split_axis=0,...  18.7 us
    all_to_all x1, waiting for transfers between devices, on_device(): lax.all_to_all(pack_rows(hidden, picks, live_slot), DOM, split_axis=0, co...  18.7 us
    all_to_all x1, blocking collectives, summed_on_arrival(): lax.all_to_all(parts, axis, split_axis=0, concat_axis=0, tiled=True)  18.3 us
    all_to_all x2, blocking collectives, copy_for_each(): lax.all_to_all(jnp.broadcast_to(value[None], (count, *value.shape)), axis...  18 us
  transfers between devices with their start and end apart: 4, of which 3 were waited for; matrix products, arithmetic and copies ran while one was open for 7% of the time, Pallas kernels for 0%

commit v1 on v0

v1 whole, which is shorter than its diff:
```python
import functools

import jax
import jax.numpy as jnp
from jax import lax
from jax.experimental import pallas as pl
from jax.experimental.pallas import tpu as pltpu
from jax.sharding import Mesh
from jax.sharding import PartitionSpec as P

DOM = ("dom_0", "dom_1", "dom_2", "dom_3")
BF = jnp.bfloat16
F32 = jnp.float32
I32 = jnp.int32
loss_scale = 256.0
MB = 1 << 20


def copy_for_each(value, axis):
    count = lax.axis_size(axis)
    return lax.all_to_all(
        jnp.broadcast_to(value[None], (count, *value.shape)), axis, 0, 0, tiled=True
    )


def taken_together(value, axis):
    return jnp.sum(copy_for_each(value, axis), axis=0)


def one_axis_at_a_time(value, axes):
    far, near = axes
    return taken_together(taken_together(value, near), far)


def in_blocks(value, dim, count):
    shape = value.shape
    parts = value.reshape(*shape[:dim], count, shape[dim] // count, *shape[dim + 1 :])
    return jnp.moveaxis(parts, dim, 0)


def summed_on_arrival(value, axis, dim):
    parts = in_blocks(value, dim, lax.axis_size(axis))
    arrived = lax.all_to_all(parts, axis, split_axis=0, concat_axis=0, tiled=True)
    return arrived.astype(F32).sum(axis=0)


def summed_rows(value, axes, dim):
    far, near = axes
    own = summed_on_arrival(in_blocks(value, dim, lax.axis_size(far)), near, dim + 1)
    return jnp.sum(
        lax.all_to_all(own.astype(BF), far, 0, 0, tiled=True).astype(F32), axis=0
    )


def dot(a, b):
    return jnp.dot(a, b, preferred_element_type=F32)


def dot_nt(a, b):
    return lax.dot_general(a, b, (((1,), (1,)), ((), ())), preferred_element_type=F32)


def dot_tn(a, b):
    return lax.dot_general(a, b, (((0,), (0,)), ((), ())), preferred_element_type=F32)


def iota(shape, dim):
    return lax.broadcasted_iota(I32, shape, dim)


def one_hot_cols(col, count):
    return jnp.where(col == iota((col.shape[0], count), 1), 1.0, 0.0).astype(BF)


def one_hot_rows(row, count):
    return jnp.where(row == iota((count, row.shape[1]), 0), 1.0, 0.0).astype(BF)


def pack_body(values, picks, packed):
    hot = one_hot_cols(picks[...], values.shape[0])
    packed[...] = dot(hot, values[...]).astype(BF)


def adjacency_body(src_row, dst_row, src_col, dst_col, adj, adj_t, norm):
    table_rows = adj.shape[2]
    for b in range(2):
        dst_hot = one_hot_rows(dst_row[0, b : b + 1, :], 128)
        src_hot = one_hot_cols(src_col[0, :, b : b + 1], table_rows)
        adj[0, b * 128 : (b + 1) * 128, :] = dot(dst_hot, src_hot).astype(BF)
        counts = jnp.sum(dst_hot.astype(F32), axis=1, keepdims=True)
        norm[0, b * 128 : (b + 1) * 128, :] = jnp.broadcast_to(
            1.0 / jnp.maximum(counts, 1.0), (128, 128)
        )
        src_hot_t = one_hot_rows(src_row[0, b : b + 1, :], table_rows)
        dst_hot_t = one_hot_cols(dst_col[0, :, b : b + 1], 128)
        adj_t[0, :, b * 128 : (b + 1) * 128] = dot(src_hot_t, dst_hot_t).astype(BF)


def averaged_rows(adj, norm, own, arrived):
    rows = own.shape[0]
    sums = dot(adj[0, :, :rows], own[...]) + dot(adj[0, :, rows:], arrived[...])
    return (sums * norm[0, :, :1]).astype(BF)


def first_body(own, arrived, adj, norm, w, w_self, picks, avg, pre, hidden, packed, acc):
    r = pl.program_id(0)

    @pl.when(r == 0)
    def _():
        acc[...] = dot(own[...], w_self[0])

    a = averaged_rows(adj, norm, own, arrived)
    avg[0] = a
    acc[...] += dot(a, w[0])

    @pl.when(r == pl.num_programs(0) - 1)
    def _():
        total = acc[...]
        pre[...] = total
        h = jnp.maximum(total, 0.0).astype(BF)
        hidden[...] = h
        packed[...] = dot(one_hot_cols(picks[...], h.shape[0]), h).astype(BF)


def second_body(count, own, arrived, adj, norm, w, w_self, labels, avg, logits, grad, part, acc):
    r = pl.program_id(0)

    @pl.when(r == 0)
    def _():
        acc[...] = dot(own[...], w_self[...])

    a = averaged_rows(adj, norm, own, arrived)
    avg[0] = a
    acc[...] += dot(a, w[0])

    @pl.when(r == pl.num_programs(0) - 1)
    def _():
        out = acc[...]
        logits[...] = out
        lab = labels[...]
        labelled = lab >= 0
        top = jnp.max(out, axis=1, keepdims=True)
        log_total = jnp.log(jnp.sum(jnp.exp(out - top), axis=1, keepdims=True)) + top
        hot = jnp.where(lab == iota(out.shape, 1), 1.0, 0.0)
        picked = jnp.sum(out * hot, axis=1, keepdims=True)
        part[...] = jnp.sum(
            jnp.where(labelled, log_total - picked, 0.0), axis=0, keepdims=True
        )
        soft = jnp.exp(out - log_total)
        mask = jnp.where(labelled, 1.0, 0.0)
        grad[...] = (loss_scale * (soft - hot) * mask / count[0, 0]).astype(BF)


def spread_body(grad, w, w_self, adj_t, norm, back, local, acc):
    r = pl.program_id(0)
    rows = local.shape[0]

    @pl.when(r == 0)
    def _():
        acc[...] = jnp.zeros_like(acc)

    spread = (dot_nt(grad[...], w[0]) * norm[0, :, :1]).astype(BF)
    acc[...] += dot(adj_t[0], spread)

    @pl.when(r == pl.num_programs(0) - 1)
    def _():
        back[...] = acc[rows:, :].astype(BF)
        local[...] = acc[:rows, :] + dot_nt(grad[...], w_self[...])


def two_body(avg, own, grad, out):
    r = pl.program_id(0)
    last = pl.num_programs(0) - 1

    @pl.when(r < last)
    def _():
        out[...] = dot_tn(avg[0], grad[...]).astype(BF)

    @pl.when(r == last)
    def _():
        out[...] = dot_tn(own[...], grad[...]).astype(BF)


def one_body(avg, own, local, returned, picks, pre, out, grad_pre):
    r = pl.program_id(0)
    last = pl.num_programs(0) - 1

    @pl.when(r == 0)
    def _():
        hot = one_hot_rows(picks[...], local.shape[0])
        grad = local[...] + dot(hot, returned[...])
        grad_pre[...] = jnp.where(pre[...] > 0.0, grad, 0.0).astype(BF)

    @pl.when(r < last)
    def _():
        out[...] = dot_tn(avg[0], grad_pre[...]).astype(BF)

    @pl.when(r == last)
    def _():
        out[...] = dot_tn(own[...], grad_pre[...]).astype(BF)


def whole(shape, space=None):
    n = len(shape)
    return pl.BlockSpec(shape, lambda *_: (0,) * n)


def per_r(shape, top=None):
    n = len(shape)
    if top is None:
        return pl.BlockSpec((1, *shape), lambda r: (r,) + (0,) * n)
    return pl.BlockSpec((1, *shape), lambda r: (jnp.minimum(r, top),) + (0,) * n)


def sds(shape, dtype):
    return jax.ShapeDtypeStruct(shape, dtype)


def call(body, name, grid, ins, outs, shapes, scratch, flops, args, vmem=32 * MB):
    return pl.pallas_call(
        body,
        name=name,
        grid=grid,
        in_specs=ins,
        out_specs=outs,
        out_shape=shapes,
        scratch_shapes=scratch,
        compiler_params=pltpu.CompilerParams(
            vmem_limit_bytes=vmem, dimension_semantics=("arbitrary",) * len(grid)
        ),
        cost_estimate=pl.CostEstimate(flops=flops, bytes_accessed=0, transcendentals=0),
    )(*args)


def on_device(features, w_one, w_two, self_two, edge_src, edge_dst, send_rows, send_count, labels):
    peers = lax.axis_size(DOM)
    n, d = features.shape
    rel = w_two.shape[0]
    classes = w_two.shape[2]
    slots = send_rows.shape[2]
    far = peers * slots
    table = n + far
    live_slot = jnp.arange(slots, dtype=I32)[None, :] < send_count[0][:, None]
    picks = jnp.where(live_slot, send_rows[0], -1)
    picks_col = picks.reshape(far, 1)
    picks_row = picks.reshape(1, far)

    local_count = jnp.sum((labels >= 0).astype(F32))
    label_count = one_axis_at_a_time(
        local_count.reshape(1), (("dom_0", "dom_1", "dom_2"), "dom_3")
    )[0]

    packed = call(
        pack_body, "pack", (1,), [whole((n, d)), whole((far, 1))], whole((far, d)),
        sds((far, d), BF), [], 2 * far * n * d, (features, picks_col),
    )

    def exchange(v):
        return lax.all_to_all(
            v.reshape(peers, slots, d), DOM, split_axis=0, concat_axis=0, tiled=True
        ).reshape(far, d)

    arrived = exchange(packed)
    adj, adj_t, norm = call(
        adjacency_body, "adjacency", (rel,),
        [per_r((2, 256)), per_r((2, 256)), per_r((256, 2)), per_r((256, 2))],
        [per_r((n, table)), per_r((table, n)), per_r((n, 128))],
        [sds((rel, n, table), BF), sds((rel, table, n), BF), sds((rel, n, 128), F32)],
        [], 4 * rel * 2 * 128 * 256 * table,
        (edge_src, edge_dst, jnp.swapaxes(edge_src, 1, 2), jnp.swapaxes(edge_dst, 1, 2)),
    )
    w_last = pl.BlockSpec((1, d, d), lambda r: (rel, 0, 0))
    avg_one, pre, hidden, packed_hidden = call(
        first_body, "first", (rel,),
        [whole((n, d)), whole((far, d)), per_r((n, table)), per_r((n, 128)), per_r((d, d)), w_last,
         whole((far, 1))],
        [per_r((n, d)), whole((n, d)), whole((n, d)), whole((far, d))],
        [sds((rel, n, d), BF), sds((n, d), F32), sds((n, d), BF), sds((far, d), BF)],
        [pltpu.VMEM((n, d), F32)], 2 * rel * n * d * (table + d),
        (features, arrived, adj, norm, w_one, w_one, picks_col),
    )
    arrived_hidden = exchange(packed_hidden)
    avg_two, logits, grad_logits, part = call(
        second_body, "second", (rel,),
        [pl.BlockSpec(memory_space=pltpu.SMEM), whole((n, d)), whole((far, d)), per_r((n, table)),
         per_r((n, 128)), per_r((d, classes)), whole((d, classes)), whole((n, 1))],
        [per_r((n, d)), whole((n, classes)), whole((n, classes)), whole((1, 1))],
        [sds((rel, n, d), BF), sds((n, classes), F32), sds((n, classes), BF), sds((1, 1), F32)],
        [pltpu.VMEM((n, classes), F32)], 2 * rel * n * d * (table + classes),
        (label_count.reshape(1, 1), hidden, arrived_hidden, adj, norm, w_two, self_two,
         labels.reshape(n, 1)),
    )
    back, local = call(
        spread_body, "spread", (rel,),
        [whole((n, classes)), per_r((d, classes)), whole((d, classes)), per_r((table, n)),
         per_r((n, 128))],
        [whole((far, d)), whole((n, d))],
        [sds((far, d), BF), sds((n, d), F32)],
        [pltpu.VMEM((table, d), F32)], 2 * rel * n * d * (table + classes),
        (grad_logits, w_two, self_two, adj_t, norm),
    )
    returned = exchange(back)
    total = one_axis_at_a_time(part.reshape(1), (("dom_0", "dom_1", "dom_2"), "dom_3"))[0]
    loss = total / label_count
    g_two = call(
        two_body, "two", (rel + 1,),
        [per_r((n, d), rel - 1), whole((n, d)), whole((n, classes))],
        pl.BlockSpec((d, classes), lambda r: (r, 0)),
        sds(((rel + 1) * d, classes), BF), [], 2 * (rel + 1) * n * d * classes,
        (avg_two, hidden, grad_logits),
    )
    g_one = call(
        one_body, "one", (rel + 1,),
        [per_r((n, d), rel - 1), whole((n, d)), whole((n, d)), whole((far, d)), whole((1, far)),
         whole((n, d))],
        pl.BlockSpec((d, d), lambda r: (r, 0)),
        sds(((rel + 1) * d, d), BF), [pltpu.VMEM((n, d), BF)], 2 * (rel + 1) * n * d * d,
        (avg_one, features, local, returned, picks_row, pre),
    )
    joined = summed_rows(
        jnp.concatenate([g_one, g_two], axis=1), (("dom_0", "dom_1", "dom_2"), "dom_3"), 0
    )
    return (logits, loss, joined[:, :d], joined[:, d:])


def solution(mesh):
    split = Mesh(mesh.devices.reshape(4, 4, 4, 2), DOM)
    return jax.shard_map(
        on_device,
        mesh=split,
        in_specs=(
            P(DOM, None),
            P(),
            P(),
            P(),
            P(None, DOM, None),
            P(None, DOM, None),
            P(DOM, None, None),
            P(DOM, None),
            P(DOM),
        ),
        out_specs=(P(DOM, None), P(), P(DOM, None), P(DOM, None)),
        check_vma=False,
    )
```

time: 489 us -> 318 us (0.65)
  the two profiles are of different devices: /device:TPU:0 before, /device:TPU:103 now
where the time goes in v1:
time: 318 us; the launch traced here: 316 us
  local copies, waits for them, and re-layouts  87 us (27%)
  waiting for transfers between devices  78.8 us (25%)
  starting transfers between devices  66.1 us (21%)
  Pallas kernels  38.3 us (12%)
  other arithmetic  23.6 us (7%)
  blocking collectives  18.4 us (6%)
  between operations  3.41 us (1%)
    all_to_all x1, waiting for transfers between devices, summed_rows(): lax.all_to_all(own.astype(BF), far, 0, 0, tiled=True).astype(F32)  64.4 us
    unnamed x86, local copies, waits for them, and re-layouts  50.5 us
    pallas_call x7, Pallas kernels, call(): pl.pallas_call(body, name=name, grid=grid, in_specs=ins, out_specs=outs,...  38.3 us
    all_to_all x3, starting transfers between devices, exchange(): lax.all_to_all(v.reshape(peers, slots, d), DOM, split_axis=0, concat_axis...  29.7 us
    all_to_all x4, starting transfers between devices, copy_for_each(): lax.all_to_all(jnp.broadcast_to(value[None], (count, *value.shape)), axis...  26.4 us
    all_to_all x1, blocking collectives, summed_on_arrival(): lax.all_to_all(parts, axis, split_axis=0, concat_axis=0, tiled=True)  18.4 us
    all_to_all x3, waiting for transfers between devices, exchange(): lax.all_to_all(v.reshape(peers, slots, d), DOM, split_axis=0, concat_axis...  14.3 us
    another operation x1, local copies, waits for them, and re-layouts, in_blocks(): value.reshape(*shape[:dim], count, shape[dim] // count, *shape[dim + 1:])  12.5 us
  transfers between devices with their start and end apart: 8, of which 3 were waited for; matrix products, arithmetic and copies ran while one was open for 10% of the time, Pallas kernels for 8%

profile of v1, /device:TPU:103, one launch (start us, length us, event | category | flops | bytes accessed | tf_op | source)
XLA Modules:
  0.0 315.5 jit_solution(8014440208492849467)
XLA Ops:
  0.7 1.3 fusion
  3.2 3.9 %all-to-all-start = ((f32[2,1,1]{2,1,0:T(1,128)}), f32[2,1,1]{2,1,0:T(1,128)S(1)}, u32[]{:S(2)}, u32[]{:S(2)}) async-start(f32[2,1,1]{2,1,0:T(1,128)} %broadcast_in_dim.16), calls=%async_computation | async-start | bytes 2048 | tf_op jit(solution)/shard_map/all_to_all | solution.py:21
  10.4 1.4 pack.1
  11.8 9.5 %all-to-all-start.2 = ((bf16[128,8,512]{2,1,0:T(8,128)(2,1)}), bf16[128,8,512]{2,1,0:T(8,128)(2,1)S(1)}, u32[]{:S(2)}, u32[]{:S(2)}) async-start(bf16[128,8,512]{2,1,0:T(8,128)(2,1)} %bitcast.2), calls=%async_computation.2 | async-start | bytes 2097152 | tf_op jit(solution)/shard_map/all_to_all | solution.py:259
  21.4 1.4 copy.93
  22.8 1.4 copy.94
  24.7 1.2 copy-done.17
  25.9 1.2 copy-done.18
  27.2 6.4 %adjacency.1 = (bf16[8,256,1280]{2,1,0:T(8,128)(2,1)S(1)}, bf16[8,1280,256]{2,1,0:T(8,128)(2,1)S(1)}, f32[8,256,128]{2,1,0:T(8,128)S(1)}) custom-call(s32[8,2,256]{2,1,0:T(2,128)S(1)} %copy-done.32, s32[8,2,256]{2,1,0:T(2,128)S(1)} %copy-done.33, s32[8,256,2]{2,1,0:T(8,128)S(1)} %bitcast.16, s32[8,256,2]{2,1,0:T(8,128)S(1)} %bitcast.17), custom_call_target="tpu_custom_call" | custom-call | flops 2684354560 | tf_op jit(solution)/shard_map/adjacency/pallas_call | solution.py:220
  33.6 2.4 copy-done.2
  36.0 2.3 copy-done.34
  38.3 1.3 broadcast_in_dim.32
  39.6 9.7 %all-to-all-start.1 = ((f32[64,1,1]{2,1,0:T(1,128)}), f32[64,1,1]{2,1,0:T(1,128)S(1)}, u32[]{:S(2)}, u32[]{:S(2)}) async-start(f32[64,1,1]{2,1,0:T(1,128)} %broadcast_in_dim.32), calls=%async_computation.1 | async-start | bytes 65536 | tf_op jit(solution)/shard_map/all_to_all | solution.py:21
  49.4 2.3 copy-done.1
  51.7 2.5 copy-done.3
  54.2 6.6 %first.1 = (bf16[8,256,512]{2,1,0:T(8,128)(2,1)S(1)}, f32[256,512]{1,0:T(8,128)S(1)}, bf16[256,512]{1,0:T(8,128)(2,1)S(1)}, bf16[1024,512]{1,0:T(8,128)(2,1)S(1)}) custom-call(bf16[256,512]{1,0:T(8,128)(2,1)S(1)} %copy-done.6, bf16[1024,512]{1,0:T(8,128)(2,1)S(1)} %bitcast.13, bf16[8,256,1280]{2,1,0:T(8,128)(2,1)S(1)} %copy-done.3, ...), custom_call_target="tpu_custom_call" | custom-call | flops 3758096384 | tf_op jit(solution)/shard_map/first/pallas_call | solution.py:220
  60.8 1.4 copy-done.10
  64.7 10.8 %all-to-all-start.3 = ((bf16[128,8,512]{2,1,0:T(8,128)(2,1)}), bf16[128,8,512]{2,1,0:T(8,128)(2,1)}, u32[]{:S(2)}, u32[]{:S(2)}) async-start(bf16[128,8,512]{2,1,0:T(8,128)(2,1)} %bitcast.15), calls=%async_computation.3 | async-start | bytes 2097152 | tf_op jit(solution)/shard_map/all_to_all | solution.py:259
  76.5 3.8 %copy.95.w = bf16[8,512,349]{2,1,0:T(8,128)(2,1)S(1)} copy(bf16[8,512,349]{1,0,2:T(8,128)(2,1)} %param.11) | data formatting | bytes 5718016 | tf_op args[2]
  80.3 1.4 reduce_sum.68
  81.7 8.5 %all-to-all-done.3 = bf16[128,8,512]{2,1,0:T(8,128)(2,1)} async-done(((bf16[128,8,512]{2,1,0:T(8,128)(2,1)}), bf16[128,8,512]{2,1,0:T(8,128)(2,1)}, u32[]{:S(2)}, u32[]{:S(2)}) %all-to-all-start.3) | async-done | bytes 1048608 | tf_op jit(solution)/shard_map/all_to_all | solution.py:259
  90.2 2.5 copy-done.4
  92.7 1.2 copy-done.13
  95.8 9.0 %second.1 = (bf16[8,256,512]{2,1,0:T(8,128)(2,1)S(1)}, f32[256,349]{1,0:T(8,128)S(1)}, bf16[256,349]{1,0:T(8,128)(2,1)S(1)}, f32[1,1]{1,0:T(1,128)}) custom-call(f32[1,1]{1,0:T(1,128)} %bitcast.count, bf16[256,512]{1,0:T(8,128)(2,1)S(1)} %copy-done.26, bf16[1024,512]{1,0:T(8,128)(2,1)} %bitcast.7.arrived, bf16[8,256,1280]{2,1,0:T(8,128)(2,1)S(1)} %copy-done.4, ...), custom_call_target="tpu_custom_call" | custom-call | flops 3416260608 | tf_op jit(solution)/shard_map/second/pallas_call | solution.py:220
  104.8 1.3 copy-done.8
  108.7 4.2 %all-to-all-start.4 = ((f32[2,1,1]{2,1,0:T(1,128)}), f32[2,1,1]{2,1,0:T(1,128)}, u32[]{:S(2)}, u32[]{:S(2)}) async-start(f32[2,1,1]{2,1,0:T(1,128)} %broadcast_in_dim.35), calls=%async_computation.4 | async-start | bytes 2048 | tf_op jit(solution)/shard_map/all_to_all | solution.py:21
  112.9 1.2 copy-done.14
  115.0 2.5 copy-done.35
  117.5 7.1 %spread.1 = (bf16[1024,512]{1,0:T(8,128)(2,1)S(1)}, f32[256,512]{1,0:T(8,128)S(1)}) custom-call(bf16[256,349]{1,0:T(8,128)(2,1)S(1)} %copy-done.29, bf16[8,512,349]{2,1,0:T(8,128)(2,1)S(1)} %copy.95.w, bf16[512,349]{1,0:T(8,128)(2,1)S(1)} %copy.96.w_self, bf16[8,1280,256]{2,1,0:T(8,128)(2,1)S(1)} %copy-done.35, f32[8,256,128]{2,1,0:T(8,128)S(1)} %copy-done.14), custom_call_target="tpu_custom_call" | custom-call | flops 3416260608 | tf_op jit(solution)/shard_map/spread/pallas_call | solution.py:220
  126.4 9.3 %all-to-all-start.6 = ((bf16[128,8,512]{2,1,0:T(8,128)(2,1)}), bf16[128,8,512]{2,1,0:T(8,128)(2,1)}, u32[]{:S(2)}, u32[]{:S(2)}) async-start(bf16[128,8,512]{2,1,0:T(8,128)(2,1)} %bitcast.14), calls=%async_computation.6 | async-start | bytes 2097152 | tf_op jit(solution)/shard_map/all_to_all | solution.py:259
  136.7 1.2 reduce_sum.69
  138.0 1.6 copy-done.9
  141.5 3.0 two.1
  144.5 5.9 %all-to-all-done.6 = bf16[128,8,512]{2,1,0:T(8,128)(2,1)} async-done(((bf16[128,8,512]{2,1,0:T(8,128)(2,1)}), bf16[128,8,512]{2,1,0:T(8,128)(2,1)}, u32[]{:S(2)}, u32[]{:S(2)}) %all-to-all-start.6) | async-done | bytes 1048608 | tf_op jit(solution)/shard_map/all_to_all | solution.py:259
  151.3 1.6 copy-done.11
  155.0 4.7 %one.1 = bf16[4608,512]{1,0:T(8,128)(2,1)S(1)} custom-call(bf16[8,256,512]{2,1,0:T(8,128)(2,1)S(1)} %copy-done.11, bf16[256,512]{1,0:T(8,128)(2,1)S(1)} %copy-done.7, f32[256,512]{1,0:T(8,128)S(1)} %copy-done.22, bf16[1024,512]{1,0:T(8,128)(2,1)} %bitcast.11.returned, s32[1,1024]{1,0:T(1,128)S(1)} %broadcast_select_fusion.1.picks, f32[256,512]{1,0:T(8,128)S(1)} %copy-done.20), custom_call_target="tpu_custom_call" | custom-call | flops 1207959552 | tf_op jit(solution)/shard_map/one/pallas_call | solution.py:220
  159.7 2.1 copy-done
  161.9 6.3 %pad_maximum_fusion = bf16[4608,861]{1,0:T(8,128)(2,1)} fusion(bf16[4608,349]{1,0:T(8,128)(2,1)S(1)} %two.1, bf16[4608,512]{1,0:T(8,128)(2,1)} %copy-done), kind=kLoop, calls=%fused_computation.1 | loop fusion | flops 15869952 | bytes 15869952 | tf_op jit(solution)/shard_map/concatenate | solution.py:321
  168.1 12.5 %reshape_reshape.3 = bf16[64,2,36,861]{3,2,1,0:T(8,128)(2,1)} reshape(bf16[4608,861]{1,0:T(8,128)(2,1)} %pad_maximum_fusion) | data formatting | bytes 15869952 | tf_op jit(solution)/shard_map/reshape;reshape | solution.py:37
  180.7 8.9 %copy.103 = bf16[2,64,36,861]{3,1,2,0:T(8,128)(2,1)} copy(bf16[2,64,36,861]{3,2,0,1:T(8,128)(2,1)} %bitcast.18) | data formatting | bytes 15869952 | tf_op jit(solution)/shard_map/transpose | solution.py:38
  189.6 18.4 %all_to_all.49 = bf16[2,64,36,861]{3,1,2,0:T(8,128)(2,1)} all-to-all(bf16[2,64,36,861]{3,1,2,0:T(8,128)(2,1)} %copy.103), channel_id=1, replica_groups=mesh['dom_0'=4,'dom_1'=4,'dom_2'=4,'dom_3'=2] {'dom_3'}, dimensions={0} | all-to-all | bytes 15869952 | tf_op jit(solution)/shard_map/all_to_all | solution.py:43
  207.9 1.3 broadcast_in_dim.36
  209.2 8.5 %all-to-all-start.5 = ((f32[64,1,1]{2,1,0:T(1,128)}), f32[64,1,1]{2,1,0:T(1,128)S(1)}, u32[]{:S(2)}, u32[]{:S(2)}) async-start(f32[64,1,1]{2,1,0:T(1,128)} %broadcast_in_dim.36), calls=%async_computation.5 | async-start | bytes 65536 | tf_op jit(solution)/shard_map/all_to_all | solution.py:21
  217.8 8.2 %reduce_sum.71 = bf16[64,36,861]{2,0,1:T(8,128)(2,1)} reduce(bf16[2,64,36,861]{3,1,2,0:T(8,128)(2,1)} %all_to_all.49, bf16[]{:T(256)} %constant.7.clone.1), dimensions={0}, to_apply=%region_5.6 | reduce | flops 1983744 | bytes 11902466 | tf_op jit(solution)/shard_map/reduce_sum | solution.py:44
  226.0 6.6 %copy.104 = bf16[64,36,861]{2,1,0:T(8,128)(2,1)} copy(bf16[64,36,861]{2,0,1:T(8,128)(2,1)} %reduce_sum.71) | data formatting | bytes 7934976 | tf_op jit(solution)/shard_map/reduce_sum | solution.py:44
  232.6 10.1 %all-to-all-start.8 = ((bf16[64,36,861]{2,1,0:T(8,128)(2,1)}), bf16[64,36,861]{2,1,0:T(8,128)(2,1)}, u32[]{:S(2)}, u32[]{:S(2)}) async-start(bf16[64,36,861]{2,1,0:T(8,128)(2,1)} %copy.104), calls=%async_computation.8 | async-start | bytes 9175040 | tf_op jit(solution)/shard_map/all_to_all | solution.py:51
  245.6 64.4 %all-to-all-done.8 = bf16[64,36,861]{2,1,0:T(8,128)(2,1)} async-done(((bf16[64,36,861]{2,1,0:T(8,128)(2,1)}), bf16[64,36,861]{2,1,0:T(8,128)(2,1)}, u32[]{:S(2)}, u32[]{:S(2)}) %all-to-all-start.8) | async-done | bytes 3967520 | tf_op jit(solution)/shard_map/all_to_all | solution.py:51
  310.1 3.1 convert_reduce_fusion
  (87 shorter events, 24.6 us)
Async XLA Ops:
  0.6 20.8 %copy-start.32 = (s32[8,2,256]{2,1,0:T(2,128)S(1)}, s32[8,2,256]{2,1,0:T(2,128)}, u32[]{:S(2)}) copy-start(s32[8,2,256]{2,1,0:T(2,128)} %src_row.1) | copy-start | bytes 49156
  0.6 22.1 %copy-start.33 = (s32[8,2,256]{2,1,0:T(2,128)S(1)}, s32[8,2,256]{2,1,0:T(2,128)}, u32[]{:S(2)}) copy-start(s32[8,2,256]{2,1,0:T(2,128)} %dst_row.1) | copy-start | bytes 49156
  3.2 8.7 %all-to-all-start = ((f32[2,1,1]{2,1,0:T(1,128)}), f32[2,1,1]{2,1,0:T(1,128)S(1)}, u32[]{:S(2)}, u32[]{:S(2)}) async-start(f32[2,1,1]{2,1,0:T(1,128)} %broadcast_in_dim.16), calls=%async_computation | async-start | bytes 2048 | tf_op jit(solution)/shard_map/all_to_all | solution.py:21
  8.5 0.6 copy-start.36
  9.4 1.0 copy-start.5
  11.8 26.5 %all-to-all-start.2 = ((bf16[128,8,512]{2,1,0:T(8,128)(2,1)}), bf16[128,8,512]{2,1,0:T(8,128)(2,1)S(1)}, u32[]{:S(2)}, u32[]{:S(2)}) async-start(bf16[128,8,512]{2,1,0:T(8,128)(2,1)} %bitcast.2), calls=%async_computation.2 | async-start | bytes 2097152 | tf_op jit(solution)/shard_map/all_to_all | solution.py:259
  24.1 25.3 %copy-start.6 = (bf16[256,512]{1,0:T(8,128)(2,1)S(1)}, bf16[256,512]{1,0:T(8,128)(2,1)}, u32[]{:S(2)}) copy-start(bf16[256,512]{1,0:T(8,128)(2,1)} %own.3) | copy-start | bytes 786436
  24.7 1.2 copy-start.17
  25.9 1.2 copy-start.18
  33.6 2.4 copy-start.2
  36.0 2.3 copy-start.34
  38.3 22.5 %copy-start.12 = (f32[8,256,128]{2,1,0:T(8,128)}, f32[8,256,128]{2,1,0:T(8,128)S(1)}, u32[]{:S(2)}) copy-start(f32[8,256,128]{2,1,0:T(8,128)S(1)} %get-tuple-element.18.norm) | copy-start | bytes 3145732
  39.6 25.1 %all-to-all-start.1 = ((f32[64,1,1]{2,1,0:T(1,128)}), f32[64,1,1]{2,1,0:T(1,128)S(1)}, u32[]{:S(2)}, u32[]{:S(2)}) async-start(f32[64,1,1]{2,1,0:T(1,128)} %broadcast_in_dim.32), calls=%async_computation.1 | async-start | bytes 65536 | tf_op jit(solution)/shard_map/all_to_all | solution.py:21
  49.4 2.3 copy-start.1
  51.7 2.5 copy-start.3
  54.2 21.3 %copy-start.39 = (s32[256]{0:T(256)S(1)}, s32[256]{0:T(256)}, u32[]{:S(2)}) copy-start(s32[256]{0:T(256)} %param.17) | copy-start | bytes 3076
  54.2 22.1 %copy-start.37 = (bf16[512,349]{0,1:T(8,128)(2,1)S(1)}, bf16[512,349]{0,1:T(8,128)(2,1)}, u32[]{:S(2)}) copy-start(bf16[512,349]{0,1:T(8,128)(2,1)} %param.12) | copy-start | bytes 1072132
  60.8 1.4 copy-start.10
  62.2 1.0 copy-start.16
  63.2 0.8 copy-start.19
  64.0 0.7 copy-start.25
  64.7 10.8 %copy-start.38 = (f32[64,1,1]{2,1,0:T(1,128)}, f32[64,1,1]{2,1,0:T(1,128)S(1)}, u32[]{:S(2)}) copy-start(f32[64,1,1]{2,1,0:T(1,128)S(1)} %all-to-all-done.1) | copy-start | bytes 772
  64.7 25.5 %all-to-all-start.3 = ((bf16[128,8,512]{2,1,0:T(8,128)(2,1)}), bf16[128,8,512]{2,1,0:T(8,128)(2,1)}, u32[]{:S(2)}, u32[]{:S(2)}) async-start(bf16[128,8,512]{2,1,0:T(8,128)(2,1)} %bitcast.15), calls=%async_computation.3 | async-start | bytes 2097152 | tf_op jit(solution)/shard_map/all_to_all | solution.py:259
  90.2 2.5 copy-start.4
  92.7 1.2 copy-start.13
  93.9 0.9 copy-start.26
  94.9 0.9 copy-start.31
  104.8 1.3 copy-start.8
  106.1 0.8 copy-start.23
  106.8 0.7 copy-start.28
  108.7 17.7 %all-to-all-start.4 = ((f32[2,1,1]{2,1,0:T(1,128)}), f32[2,1,1]{2,1,0:T(1,128)}, u32[]{:S(2)}, u32[]{:S(2)}) async-start(f32[2,1,1]{2,1,0:T(1,128)} %broadcast_in_dim.35), calls=%async_computation.4 | async-start | bytes 2048 | tf_op jit(solution)/shard_map/all_to_all | solution.py:21
  112.9 1.2 copy-start.14
  114.1 0.9 copy-start.29
  115.0 2.5 copy-start.35
  124.6 1.0 copy-start.15
  125.6 0.8 copy-start.21
  126.4 24.0 %all-to-all-start.6 = ((bf16[128,8,512]{2,1,0:T(8,128)(2,1)}), bf16[128,8,512]{2,1,0:T(8,128)(2,1)}, u32[]{:S(2)}, u32[]{:S(2)}) async-start(bf16[128,8,512]{2,1,0:T(8,128)(2,1)} %bitcast.14), calls=%async_computation.6 | async-start | bytes 2097152 | tf_op jit(solution)/shard_map/all_to_all | solution.py:259
  138.0 1.6 copy-start.9
  139.6 0.9 copy-start.27
  140.5 0.9 copy-start.30
  150.4 1.0 copy-start.7
  151.3 1.6 copy-start.11
  152.9 1.0 copy-start.20
  154.0 1.0 copy-start.22
  159.7 2.1 copy-start
  209.2 23.4 %all-to-all-start.5 = ((f32[64,1,1]{2,1,0:T(1,128)}), f32[64,1,1]{2,1,0:T(1,128)S(1)}, u32[]{:S(2)}, u32[]{:S(2)}) async-start(f32[64,1,1]{2,1,0:T(1,128)} %broadcast_in_dim.36), calls=%async_computation.5 | async-start | bytes 65536 | tf_op jit(solution)/shard_map/all_to_all | solution.py:21
  232.6 10.1 %copy-start.24 = (f32[256,349]{1,0:T(8,128)S(1)}, f32[256,349]{1,0:T(8,128)}, u32[]{:S(2)}) copy-start(f32[256,349]{1,0:T(8,128)} %copy-done.23) | copy-start | bytes 1072132
  232.6 77.4 %all-to-all-start.8 = ((bf16[64,36,861]{2,1,0:T(8,128)(2,1)}), bf16[64,36,861]{2,1,0:T(8,128)(2,1)}, u32[]{:S(2)}, u32[]{:S(2)}) async-start(bf16[64,36,861]{2,1,0:T(8,128)(2,1)} %copy.104), calls=%async_computation.8 | async-start | bytes 9175040 | tf_op jit(solution)/shard_map/all_to_all | solution.py:51

commit v2 on v1

--- a/solution.py
+++ b/solution.py
@@ -200,6 +200,32 @@
         out[...] = dot_tn(own[...], grad_pre[...]).astype(BF)
 
 
+def a2a_body(x, y, send_sem, recv_sem):
+    sizes = [lax.axis_size(a) for a in DOM]
+    me = [lax.axis_index(a) for a in DOM]
+    mine = ((me[0] * sizes[1] + me[1]) * sizes[2] + me[2]) * sizes[3] + me[3]
+    count = x.shape[0]
+
+    def send(k, carry):
+        d0 = k % 4
+        d1 = (k // 4 + d0) % 4
+        d2 = (k // 16 + d1) % 4
+        step = (d0, d1, d2, k // 64)
+        to = [lax.rem(m + s, n) for m, s, n in zip(me, step, sizes)]
+        peer = ((to[0] * sizes[1] + to[1]) * sizes[2] + to[2]) * sizes[3] + to[3]
+        pltpu.make_async_remote_copy(
+            src_ref=x.at[peer], dst_ref=y.at[mine], send_sem=send_sem, recv_sem=recv_sem,
+            device_id=tuple(to), device_id_type=pl.DeviceIdType.MESH,
+        ).start()
+        return carry
+
+    lax.fori_loop(1, count, send, 0)
+    y[mine] = x[mine]
+    rest = pl.ds(0, count - 1)
+    pltpu.make_async_copy(x.at[rest], y.at[rest], send_sem).wait()
+    pltpu.make_async_copy(x.at[rest], y.at[rest], recv_sem).wait()
+
+
 def whole(shape, space=None):
     n = len(shape)
     return pl.BlockSpec(shape, lambda *_: (0,) * n)
@@ -256,9 +282,15 @@
     )
 
     def exchange(v):
-        return lax.all_to_all(
-            v.reshape(peers, slots, d), DOM, split_axis=0, concat_axis=0, tiled=True
-        ).reshape(far, d)
+        return pl.pallas_call(
+            a2a_body,
+            name="boundary",
+            in_specs=[pl.BlockSpec(memory_space=pltpu.VMEM)],
+            out_specs=pl.BlockSpec(memory_space=pltpu.VMEM),
+            out_shape=sds((peers, slots, d), BF),
+            scratch_shapes=[pltpu.SemaphoreType.DMA, pltpu.SemaphoreType.DMA],
+            compiler_params=pltpu.CompilerParams(has_side_effects=True, vmem_limit_bytes=4 * MB),
+        )(v.reshape(peers, slots, d)).reshape(far, d)
 
     arrived = exchange(packed)
     adj, adj_t, norm = call(

time: 318 us -> 326 us (1.025)
  Pallas kernels: 38.3 us -> 105 us
  starting transfers between devices: 66.1 us -> 38.8 us
  blocking collectives: 18.4 us -> 4.03 us
  local copies, waits for them, and re-layouts: 87 us -> 78.8 us
  waiting for transfers between devices: 78.8 us -> 70.9 us
    pallas_call x0 -> x3, Pallas kernels: none -> 70.3 us  [exchange(): pl.pallas_call(a2a_body, name='boundary', in_specs=[pl.BlockSpec(memory_s...]
    all_to_all x3 -> x1, starting transfers between devices: 29.7 us -> 7.13 us  [summed_on_arrival(): lax.all_to_all(parts, axis, split_axis=0, concat_axis=0, tiled=True)]
    all_to_all x1, blocking collectives: 18.4 us -> 4.03 us  [copy_for_each(): lax.all_to_all(jnp.broadcast_to(value[None], (count, *value.shape)), axis...]
    all_to_all x3 -> x1, waiting for transfers between devices: 14.3 us -> 6.42 us  [summed_on_arrival(): lax.all_to_all(parts, axis, split_axis=0, concat_axis=0, tiled=True)]
    unnamed x86 -> x80, local copies, waits for them, and re-layouts: 50.5 us -> 43 us
    all_to_all x4 -> x3, starting transfers between devices: 26.4 us -> 21.6 us  [copy_for_each(): lax.all_to_all(jnp.broadcast_to(value[None], (count, *value.shape)), axis...]
    pallas_call x7, Pallas kernels: 38.3 us -> 34.9 us  [call(): pl.pallas_call(body, name=name, grid=grid, in_specs=ins, out_specs=outs,...]
  transfers between devices with their start and end apart: 8 -> 5, of which waited for: 3 -> 2; matrix products, arithmetic and copies ran while one was open for 10% -> 17% of each run, Pallas kernels for 8% -> 21%
where the time goes in v2:
time: 326 us; the launch traced here: 324 us
  Pallas kernels  105 us (32%)
  local copies, waits for them, and re-layouts  78.8 us (24%)
  waiting for transfers between devices  70.9 us (22%)
  starting transfers between devices  38.8 us (12%)
  other arithmetic  22.9 us (7%)
  blocking collectives  4.03 us (1%)
  between operations  3.5 us (1%)
    pallas_call x3, Pallas kernels, exchange(): pl.pallas_call(a2a_body, name='boundary', in_specs=[pl.BlockSpec(memory_s...  70.3 us
    all_to_all x1, waiting for transfers between devices, summed_rows(): lax.all_to_all(own.astype(BF), far, 0, 0, tiled=True).astype(F32)  64.4 us
    unnamed x80, local copies, waits for them, and re-layouts  43 us
    pallas_call x7, Pallas kernels, call(): pl.pallas_call(body, name=name, grid=grid, in_specs=ins, out_specs=outs,...  34.9 us
    all_to_all x3, starting transfers between devices, copy_for_each(): lax.all_to_all(jnp.broadcast_to(value[None], (count, *value.shape)), axis...  21.6 us
    another operation x1, local copies, waits for them, and re-layouts, in_blocks(): value.reshape(*shape[:dim], count, shape[dim] // count, *shape[dim + 1:])  12.5 us
    all_to_all x1, starting transfers between devices, summed_rows(): lax.all_to_all(own.astype(BF), far, 0, 0, tiled=True).astype(F32)  10.1 us
    transpose x1, local copies, waits for them, and re-layouts, in_blocks(): return jnp.moveaxis(parts, dim, 0)  8.85 us
  transfers between devices with their start and end apart: 5, of which 2 were waited for; matrix products, arithmetic and copies ran while one was open for 17% of the time, Pallas kernels for 21%

profile of v2, /device:TPU:103, one launch (start us, length us, event | category | flops | bytes accessed | tf_op | source)
XLA Modules:
  0.0 324.2 jit_solution(2292043864337504739)
XLA Ops:
  0.7 1.3 fusion
  2.6 4.0 %all_to_all.34 = f32[2,1,1]{2,1,0:T(1,128)S(1)} all-to-all(f32[2,1,1]{2,1,0:T(1,128)S(1)} %broadcast_in_dim.16), channel_id=1, replica_groups=mesh['dom_0'=4,'dom_1'=4,'dom_2'=4,'dom_3'=2] {'dom_3'}, dimensions={0} | all-to-all | bytes 16 | tf_op jit(solution)/shard_map/all_to_all | solution.py:21
  7.2 1.3 broadcast_in_dim.32
  8.5 10.0 %all-to-all-start.1 = ((f32[64,1,1]{2,1,0:T(1,128)}), f32[64,1,1]{2,1,0:T(1,128)}, u32[]{:S(2)}, u32[]{:S(2)}) async-start(f32[64,1,1]{2,1,0:T(1,128)} %broadcast_in_dim.32), calls=%async_computation.1 | async-start | bytes 65536 | tf_op jit(solution)/shard_map/all_to_all | solution.py:21
  20.7 1.5 copy.97.labels
  22.1 1.2 copy.96.w_self
  24.8 24.9 %boundary.3 = bf16[128,8,512]{2,1,0:T(8,128)(2,1)S(1)} custom-call(bf16[128,8,512]{2,1,0:T(8,128)(2,1)S(1)} %bitcast.16), custom_call_target="tpu_custom_call" | custom-call | tf_op jit(solution)/shard_map/boundary/pallas_call | solution.py:285
  50.1 1.4 copy.94
  51.5 1.4 copy-done.16
  52.9 6.4 %adjacency.1 = (bf16[8,256,1280]{2,1,0:T(8,128)(2,1)S(1)}, bf16[8,1280,256]{2,1,0:T(8,128)(2,1)S(1)}, f32[8,256,128]{2,1,0:T(8,128)S(1)}) custom-call(s32[8,2,256]{2,1,0:T(2,128)S(1)} %copy-done.31, s32[8,2,256]{2,1,0:T(2,128)S(1)} %copy-done.32, s32[8,256,2]{2,1,0:T(8,128)S(1)} %bitcast.19, s32[8,256,2]{2,1,0:T(8,128)S(1)} %bitcast.20), custom_call_target="tpu_custom_call" | custom-call | flops 2684354560 | tf_op jit(solution)/shard_map/adjacency/pallas_call | solution.py:246
  59.3 2.3 copy-done.33
  61.7 6.6 %first.1 = (bf16[8,256,512]{2,1,0:T(8,128)(2,1)S(1)}, f32[256,512]{1,0:T(8,128)S(1)}, bf16[256,512]{1,0:T(8,128)(2,1)S(1)}, bf16[1024,512]{1,0:T(8,128)(2,1)S(1)}) custom-call(bf16[256,512]{1,0:T(8,128)(2,1)S(1)} %copy-done.6, bf16[1024,512]{1,0:T(8,128)(2,1)S(1)} %bitcast.15, bf16[8,256,1280]{2,1,0:T(8,128)(2,1)S(1)} %get-tuple-element.17.adj, ...), custom_call_target="tpu_custom_call" | custom-call | flops 3758096384 | tf_op jit(solution)/shard_map/first/pallas_call | solution.py:246
  68.3 2.4 copy-done.1
  70.7 1.4 copy-done.10
  72.0 1.0 copy-done.12
  73.0 1.0 copy-done.17
  75.6 3.7 %copy.95.w = bf16[8,512,349]{2,1,0:T(8,128)(2,1)S(1)} copy(bf16[8,512,349]{1,0,2:T(8,128)(2,1)} %param.11) | data formatting | bytes 5718016 | tf_op args[2]
  79.3 1.2 copy-done.18
  80.5 22.7 %boundary.4 = bf16[128,8,512]{2,1,0:T(8,128)(2,1)S(1)} custom-call(bf16[128,8,512]{2,1,0:T(8,128)(2,1)S(1)} %bitcast.21), custom_call_target="tpu_custom_call" | custom-call | tf_op jit(solution)/shard_map/boundary/pallas_call | solution.py:285
  104.2 1.4 reduce_sum.68
  105.7 2.5 copy-done.2
  108.2 1.2 copy-done.13
  109.4 1.2 copy-done.15
  112.5 7.8 %second.1 = (bf16[8,256,512]{2,1,0:T(8,128)(2,1)S(1)}, f32[256,349]{1,0:T(8,128)S(1)}, bf16[256,349]{1,0:T(8,128)(2,1)S(1)}, f32[1,1]{1,0:T(1,128)}) custom-call(f32[1,1]{1,0:T(1,128)} %bitcast.count, bf16[256,512]{1,0:T(8,128)(2,1)S(1)} %copy-done.26, bf16[1024,512]{1,0:T(8,128)(2,1)S(1)} %bitcast.18, bf16[8,256,1280]{2,1,0:T(8,128)(2,1)S(1)} %copy-done.2, ...), custom_call_target="tpu_custom_call" | custom-call | flops 3416260608 | tf_op jit(solution)/shard_map/second/pallas_call | solution.py:246
  120.2 3.5 %copy-done.34 = bf16[8,1280,256]{2,1,0:T(8,128)(2,1)S(1)} copy-done((bf16[8,1280,256]{2,1,0:T(8,128)(2,1)S(1)}, bf16[8,1280,256]{2,1,0:T(8,128)(2,1)}, u32[]{:S(2)}) %copy-start.34) | copy-done | bytes 5242904
  123.7 7.1 %spread.1 = (bf16[1024,512]{1,0:T(8,128)(2,1)S(1)}, f32[256,512]{1,0:T(8,128)S(1)}) custom-call(bf16[256,349]{1,0:T(8,128)(2,1)S(1)} %get-tuple-element.24.grad, bf16[8,512,349]{2,1,0:T(8,128)(2,1)S(1)} %copy.95.w, bf16[512,349]{1,0:T(8,128)(2,1)S(1)} %copy.96.w_self, bf16[8,1280,256]{2,1,0:T(8,128)(2,1)S(1)} %copy-done.34, f32[8,256,128]{2,1,0:T(8,128)S(1)} %copy-done.13), custom_call_target="tpu_custom_call" | custom-call | flops 3416260608 | tf_op jit(solution)/shard_map/spread/pallas_call | solution.py:246
  130.8 22.8 %boundary.5 = bf16[128,8,512]{2,1,0:T(8,128)(2,1)S(1)} custom-call(bf16[128,8,512]{2,1,0:T(8,128)(2,1)S(1)} %bitcast.22), custom_call_target="tpu_custom_call" | custom-call | tf_op jit(solution)/shard_map/boundary/pallas_call | solution.py:285
  153.6 1.1 copy-done.3
  154.7 1.2 broadcast_in_dim.35
  155.9 3.2 all-to-all-start.2
  159.1 1.7 copy-done.9
  162.6 3.0 two.1
  166.7 1.6 copy-done.11
  168.2 1.0 copy-done.20
  169.3 3.5 %one.1 = bf16[4608,512]{1,0:T(8,128)(2,1)S(1)} custom-call(bf16[8,256,512]{2,1,0:T(8,128)(2,1)S(1)} %copy-done.11, bf16[256,512]{1,0:T(8,128)(2,1)S(1)} %copy-done.7, f32[256,512]{1,0:T(8,128)S(1)} %copy-done.22, bf16[1024,512]{1,0:T(8,128)(2,1)S(1)} %bitcast.17, s32[1,1024]{1,0:T(1,128)S(1)} %broadcast_select_fusion.1.picks, f32[256,512]{1,0:T(8,128)S(1)} %copy-done.20), custom_call_target="tpu_custom_call" | custom-call | flops 1207959552 | tf_op jit(solution)/shard_map/one/pallas_call | solution.py:246
  172.8 2.1 copy-done
  174.9 6.3 %pad_maximum_fusion = bf16[4608,861]{1,0:T(8,128)(2,1)} fusion(bf16[4608,349]{1,0:T(8,128)(2,1)S(1)} %two.1, bf16[4608,512]{1,0:T(8,128)(2,1)} %copy-done), kind=kLoop, calls=%fused_computation.1 | loop fusion | flops 15869952 | bytes 15869952 | tf_op jit(solution)/shard_map/concatenate | solution.py:353
  181.2 12.5 %reshape_reshape.3 = bf16[64,2,36,861]{3,2,1,0:T(8,128)(2,1)} reshape(bf16[4608,861]{1,0:T(8,128)(2,1)} %pad_maximum_fusion) | data formatting | bytes 15869952 | tf_op jit(solution)/shard_map/reshape;reshape | solution.py:37
  193.7 8.8 %copy.103 = bf16[2,64,36,861]{3,1,2,0:T(8,128)(2,1)} copy(bf16[2,64,36,861]{3,2,0,1:T(8,128)(2,1)} %bitcast.23) | data formatting | bytes 15869952 | tf_op jit(solution)/shard_map/transpose | solution.py:38
  202.6 7.1 %all-to-all-start.4 = ((bf16[2,64,36,861]{3,1,2,0:T(8,128)(2,1)}), bf16[2,64,36,861]{3,1,2,0:T(8,128)(2,1)}, u32[]{:S(2)}, u32[]{:S(2)}) async-start(bf16[2,64,36,861]{3,1,2,0:T(8,128)(2,1)} %copy.103), calls=%async_computation.4 | async-start | bytes 16515072 | tf_op jit(solution)/shard_map/all_to_all | solution.py:43
  210.3 6.4 %all-to-all-done.4 = bf16[2,64,36,861]{3,1,2,0:T(8,128)(2,1)} async-done(((bf16[2,64,36,861]{3,1,2,0:T(8,128)(2,1)}), bf16[2,64,36,861]{3,1,2,0:T(8,128)(2,1)}, u32[]{:S(2)}, u32[]{:S(2)}) %all-to-all-start.4) | async-done | bytes 7935008 | tf_op jit(solution)/shard_map/all_to_all | solution.py:43
  216.7 1.3 broadcast_in_dim.36
  218.0 8.4 %all-to-all-start.3 = ((f32[64,1,1]{2,1,0:T(1,128)}), f32[64,1,1]{2,1,0:T(1,128)S(1)}, u32[]{:S(2)}, u32[]{:S(2)}) async-start(f32[64,1,1]{2,1,0:T(1,128)} %broadcast_in_dim.36), calls=%async_computation.3 | async-start | bytes 65536 | tf_op jit(solution)/shard_map/all_to_all | solution.py:21
  226.4 8.2 %reduce_sum.71 = bf16[64,36,861]{2,0,1:T(8,128)(2,1)} reduce(bf16[2,64,36,861]{3,1,2,0:T(8,128)(2,1)} %all-to-all-done.4, bf16[]{:T(256)} %constant.7.clone.1), dimensions={0}, to_apply=%region_5.6 | reduce | flops 1983744 | bytes 11902466 | tf_op jit(solution)/shard_map/reduce_sum | solution.py:44
  234.7 6.6 %copy.104 = bf16[64,36,861]{2,1,0:T(8,128)(2,1)} copy(bf16[64,36,861]{2,0,1:T(8,128)(2,1)} %reduce_sum.71) | data formatting | bytes 7934976 | tf_op jit(solution)/shard_map/reduce_sum | solution.py:44
  241.3 10.1 %all-to-all-start.5 = ((bf16[64,36,861]{2,1,0:T(8,128)(2,1)}), bf16[64,36,861]{2,1,0:T(8,128)(2,1)}, u32[]{:S(2)}, u32[]{:S(2)}) async-start(bf16[64,36,861]{2,1,0:T(8,128)(2,1)} %copy.104), calls=%async_computation.5 | async-start | bytes 9175040 | tf_op jit(solution)/shard_map/all_to_all | solution.py:51
  254.3 64.4 %all-to-all-done.5 = bf16[64,36,861]{2,1,0:T(8,128)(2,1)} async-done(((bf16[64,36,861]{2,1,0:T(8,128)(2,1)}), bf16[64,36,861]{2,1,0:T(8,128)(2,1)}, u32[]{:S(2)}, u32[]{:S(2)}) %all-to-all-start.5) | async-done | bytes 3967520 | tf_op jit(solution)/shard_map/all_to_all | solution.py:51
  318.7 3.1 convert_reduce_fusion
  (79 shorter events, 15.9 us)
Async XLA Ops:
  0.6 49.1 %copy-start.31 = (s32[8,2,256]{2,1,0:T(2,128)S(1)}, s32[8,2,256]{2,1,0:T(2,128)}, u32[]{:S(2)}) copy-start(s32[8,2,256]{2,1,0:T(2,128)} %src_row.1) | copy-start | bytes 49156
  0.6 49.5 %copy-start.32 = (s32[8,2,256]{2,1,0:T(2,128)S(1)}, s32[8,2,256]{2,1,0:T(2,128)}, u32[]{:S(2)}) copy-start(s32[8,2,256]{2,1,0:T(2,128)} %dst_row.1) | copy-start | bytes 49156
  8.5 95.7 %all-to-all-start.1 = ((f32[64,1,1]{2,1,0:T(1,128)}), f32[64,1,1]{2,1,0:T(1,128)}, u32[]{:S(2)}, u32[]{:S(2)}) async-start(f32[64,1,1]{2,1,0:T(1,128)} %broadcast_in_dim.32), calls=%async_computation.1 | async-start | bytes 65536 | tf_op jit(solution)/shard_map/all_to_all | solution.py:21
  23.4 1.0 copy-start.5
  51.5 10.2 %slice-start = ((s8[4718592]{0:T(1024)(128)(4,1)}), s8[4194304]{0:T(1024)(128)(4,1)S(1)}, s32[]{:S(2)}) async-start(s8[4718592]{0:T(1024)(128)(4,1)} %bitcast.13), calls=%async_computation.6 | async-start | bytes 8388608
  51.5 10.2 %copy-start.6 = (bf16[256,512]{1,0:T(8,128)(2,1)S(1)}, bf16[256,512]{1,0:T(8,128)(2,1)}, u32[]{:S(2)}) copy-start(bf16[256,512]{1,0:T(8,128)(2,1)} %own.3) | copy-start | bytes 786436
  51.5 1.4 copy-start.16
  52.9 8.8 %slice-start.1 = ((s8[4718592]{0:T(1024)(128)(4,1)}), s8[524288]{0:T(1024)(128)(4,1)S(1)}, s32[]{:S(2)}) async-start(s8[4718592]{0:T(1024)(128)(4,1)} %bitcast.13), calls=%async_computation.7 | async-start | bytes 1048576
  59.3 2.3 copy-start.33
  68.3 2.4 copy-start.1
  70.7 1.4 copy-start.10
  72.0 1.0 copy-start.12
  73.0 1.0 copy-start.17
  74.0 0.8 copy-start.19
  74.9 0.7 copy-start.25
  79.3 1.2 copy-start.18
  103.2 1.0 copy-start.14
  105.7 2.5 copy-start.2
  108.2 1.2 copy-start.13
  109.4 1.2 copy-start.15
  110.6 0.9 copy-start.26
  111.6 0.9 copy-start.30
  120.2 10.6 %copy-start.8 = (bf16[8,256,512]{2,1,0:T(8,128)(2,1)}, bf16[8,256,512]{2,1,0:T(8,128)(2,1)S(1)}, u32[]{:S(2)}) copy-start(bf16[8,256,512]{2,1,0:T(8,128)(2,1)S(1)} %get-tuple-element.29.avg) | copy-start | bytes 6291460
  120.2 10.6 %copy-start.23 = (f32[256,349]{1,0:T(8,128)}, f32[256,349]{1,0:T(8,128)S(1)}, u32[]{:S(2)}) copy-start(f32[256,349]{1,0:T(8,128)S(1)} %get-tuple-element.54) | copy-start | bytes 1072132
  120.2 10.6 %copy-start.28 = (bf16[256,349]{1,0:T(8,128)(2,1)}, bf16[256,349]{1,0:T(8,128)(2,1)S(1)}, u32[]{:S(2)}) copy-start(bf16[256,349]{1,0:T(8,128)(2,1)S(1)} %get-tuple-element.24.grad) | copy-start | bytes 536068
  120.2 3.5 %copy-start.34 = (bf16[8,1280,256]{2,1,0:T(8,128)(2,1)S(1)}, bf16[8,1280,256]{2,1,0:T(8,128)(2,1)}, u32[]{:S(2)}) copy-start(bf16[8,1280,256]{2,1,0:T(8,128)(2,1)} %copy-done.33) | copy-start | bytes 15728644
  130.8 22.8 %copy-start.21 = (f32[256,512]{1,0:T(8,128)}, f32[256,512]{1,0:T(8,128)S(1)}, u32[]{:S(2)}) copy-start(f32[256,512]{1,0:T(8,128)S(1)} %get-tuple-element.26.local) | copy-start | bytes 1572868
  153.6 1.1 copy-start.3
  155.9 46.7 %all-to-all-start.2 = ((f32[2,1,1]{2,1,0:T(1,128)}), f32[2,1,1]{2,1,0:T(1,128)S(1)}, u32[]{:S(2)}, u32[]{:S(2)}) async-start(f32[2,1,1]{2,1,0:T(1,128)} %broadcast_in_dim.35), calls=%async_computation.2 | async-start | bytes 2048 | tf_op jit(solution)/shard_map/all_to_all | solution.py:21
  159.1 6.6 %copy-start.4 = (bf16[128,8,512]{2,1,0:T(8,128)(2,1)S(1)}, bf16[128,8,512]{2,1,0:T(8,128)(2,1)}, u32[]{:S(2)}) copy-start(bf16[128,8,512]{2,1,0:T(8,128)(2,1)} %copy-done.3) | copy-start | bytes 3145732
  159.1 1.7 copy-start.9
  160.8 0.9 copy-start.27
  161.7 0.9 copy-start.29
  162.6 3.1 copy-start.22
  165.7 1.0 copy-start.7
  166.7 1.6 copy-start.11
  168.2 1.0 copy-start.20
  172.8 2.2 copy-start
  202.6 14.2 %all-to-all-start.4 = ((bf16[2,64,36,861]{3,1,2,0:T(8,128)(2,1)}), bf16[2,64,36,861]{3,1,2,0:T(8,128)(2,1)}, u32[]{:S(2)}, u32[]{:S(2)}) async-start(bf16[2,64,36,861]{3,1,2,0:T(8,128)(2,1)} %copy.103), calls=%async_computation.4 | async-start | bytes 16515072 | tf_op jit(solution)/shard_map/all_to_all | solution.py:43
  218.0 23.3 %all-to-all-start.3 = ((f32[64,1,1]{2,1,0:T(1,128)}), f32[64,1,1]{2,1,0:T(1,128)S(1)}, u32[]{:S(2)}, u32[]{:S(2)}) async-start(f32[64,1,1]{2,1,0:T(1,128)} %broadcast_in_dim.36), calls=%async_computation.3 | async-start | bytes 65536 | tf_op jit(solution)/shard_map/all_to_all | solution.py:21
  241.3 10.1 %copy-start.24 = (f32[256,349]{1,0:T(8,128)S(1)}, f32[256,349]{1,0:T(8,128)}, u32[]{:S(2)}) copy-start(f32[256,349]{1,0:T(8,128)} %copy-done.23) | copy-start | bytes 1072132
  241.3 77.4 %all-to-all-start.5 = ((bf16[64,36,861]{2,1,0:T(8,128)(2,1)}), bf16[64,36,861]{2,1,0:T(8,128)(2,1)}, u32[]{:S(2)}, u32[]{:S(2)}) async-start(bf16[64,36,861]{2,1,0:T(8,128)(2,1)} %copy.104), calls=%async_computation.5 | async-start | bytes 9175040 | tf_op jit(solution)/shard_map/all_to_all | solution.py:51

commit v3 on v0

v3 whole, which is shorter than its diff:
```python
import jax
import jax.numpy as jnp
from jax import lax
from jax.experimental import pallas as pl
from jax.experimental.pallas import tpu as pltpu
from jax.sharding import Mesh
from jax.sharding import PartitionSpec as P

DOM = ("dom_0", "dom_1", "dom_2", "dom_3")
SIZES = (4, 4, 4, 2)
BF = jnp.bfloat16
F32 = jnp.float32
I32 = jnp.int32
MESH = pl.DeviceIdType.MESH
loss_scale = 256.0
MB = 1 << 20

PEERS = 128
CHIPS = 64
SLOTS = 8
REL = 8
N = 256
D = 512
C = 349
CP = 384
FAR = PEERS * SLOTS
TABLE = N + FAR
ROWS = 36
WIDE = D + CP
BLOCK = 16 * ROWS

STREAMS = ((0, 256, (0, 1, 2)), (256, 256, (1, 2, 0)), (512, 384, (2, 0, 1)))


def dot(a, b):
    return jnp.dot(a, b, preferred_element_type=F32)


def dot_nt(a, b):
    return lax.dot_general(a, b, (((1,), (1,)), ((), ())), preferred_element_type=F32)


def iota(shape, dim):
    return lax.broadcasted_iota(I32, shape, dim)


def hot(mask):
    return jnp.where(mask, 1.0, 0.0).astype(BF)


def step_body(
    own, w_one_hbm, w_two_hbm, w_self_hbm, src, dst, rows, count, labels,
    logits_t, loss, grad_one, grad_two,
    w_one, w_two, w_self, adj, adj_t, norm, picks, picks_t,
    send, got_one, got_two, got_three, avg, avg_one_t, avg_two_t,
    pre, hidden, acc, table_acc, grad, grad_pre, keep,
    small_out, counts, totals,
    parts, near, half, r1a, r1b, r1c, q_a, q_b, q_c, r2a, r2b, r2c, t_a, t_b, t_c, r3a, r3b, r3c,
    w_sems, a_send, a_recv, s_send, s_recv, p_send, p_recv, x_send, x_recv,
):
    me = [lax.axis_index(a) for a in DOM]
    mine = ((me[0] * 4 + me[1]) * 4 + me[2]) * 2 + me[3]
    core = me[3]

    loads = [
        pltpu.make_async_copy(w_one_hbm, w_one, w_sems.at[0]),
        pltpu.make_async_copy(w_two_hbm, w_two, w_sems.at[1]),
        pltpu.make_async_copy(w_self_hbm, w_self, w_sems.at[2]),
    ]
    for load in loads:
        load.start()

    def relative(k):
        d0 = k % 4
        d1 = (k // 4 + d0) % 4
        d2 = (k // 16 + d1) % 4
        to = [lax.rem(m + s, n) for m, s, n in zip(me, (d0, d1, d2, k // 64), SIZES)]
        return to, ((to[0] * 4 + to[1]) * 4 + to[2]) * 2 + to[3]

    barrier = pltpu.get_barrier_semaphore()

    def greet(k, carry):
        to, _ = relative(k)
        pl.semaphore_signal(barrier, inc=1, device_id=tuple(to), device_id_type=MESH)
        return carry

    lax.fori_loop(1, PEERS, greet, 0)

    spot = iota((FAR, PEERS), 0)
    peer_hot = spot // SLOTS == iota((FAR, PEERS), 1)
    by_peer = dot(hot(peer_hot), rows[...].astype(F32).astype(BF))
    slot = iota((FAR, SLOTS), 0) % SLOTS
    chosen = jnp.sum(jnp.where(slot == iota((FAR, SLOTS), 1), by_peer, 0.0), axis=1, keepdims=True)
    live = jnp.sum(
        jnp.where(peer_hot, jnp.broadcast_to(count[...], (FAR, PEERS)), 0).astype(F32),
        axis=1, keepdims=True,
    )
    row_of = jnp.where(
        (iota((FAR, 1), 0) % SLOTS).astype(F32) < live, chosen, -1.0
    ).astype(I32)
    picks[...] = hot(row_of == iota((FAR, N), 1))

    def pack(values):
        send[...] = dot(picks[...], values).astype(BF).reshape(PEERS, SLOTS, D)

    pack(own[...])
    small_out[0] = jnp.broadcast_to(
        jnp.sum(jnp.where(labels[...] >= 0, 1.0, 0.0), axis=1, keepdims=True), (1, 128)
    )
    pl.semaphore_wait(barrier, PEERS - 1)

    def exchange(got, which, small, small_got):
        def one(k, carry):
            to, peer = relative(k)
            pltpu.make_async_remote_copy(
                src_ref=send.at[peer], dst_ref=got.at[mine], send_sem=a_send.at[which],
                recv_sem=a_recv.at[which], device_id=tuple(to), device_id_type=MESH,
            ).start()
            if small is not None:
                pltpu.make_async_remote_copy(
                    src_ref=small_out.at[small], dst_ref=small_got.at[mine],
                    send_sem=s_send.at[small], recv_sem=s_recv.at[small],
                    device_id=tuple(to), device_id_type=MESH,
                ).start()
            return carry

        lax.fori_loop(1, PEERS, one, 0)
        got[mine] = send[mine]
        if small is not None:
            small_got[mine] = small_out[small]

    rest = pl.ds(0, PEERS - 1)

    def exchange_wait(got, which):
        pltpu.make_async_copy(send.at[rest], got.at[rest], a_send.at[which]).wait()
        pltpu.make_async_copy(send.at[rest], got.at[rest], a_recv.at[which]).wait()

    def small_wait(which):
        pltpu.make_async_copy(counts.at[rest], totals.at[rest], s_send.at[which]).wait()
        pltpu.make_async_copy(counts.at[rest], totals.at[rest], s_recv.at[which]).wait()

    exchange(got_one, 0, 0, counts)

    def relation(r, carry):
        for b in range(2):
            at = slice(b * 128, (b + 1) * 128)
            dst_hot = hot(dst[r, b : b + 1, :] == iota((128, 256), 0))
            src_hot = hot(src[r, b : b + 1, :] == iota((TABLE, 256), 0))
            adj[r, at, :] = dot_nt(dst_hot, src_hot).astype(BF)
            adj_t[r, :, at] = dot_nt(src_hot, dst_hot).astype(BF)
            live_edges = jnp.sum(dst_hot.astype(F32), axis=1, keepdims=True)
            norm[r, at, :] = jnp.broadcast_to(1.0 / jnp.maximum(live_edges, 1.0), (128, 128))
        return carry

    lax.fori_loop(0, REL, relation, 0)
    picks_t[...] = picks[...].T
    avg_one_t[REL * D :, :] = own[...].T
    for load in loads:
        load.wait()
    pre[...] = dot(own[...], w_one[REL])
    small_wait(0)
    labelled_count = jnp.sum(counts[:, :, 0:1])
    exchange_wait(got_one, 0)

    def averaged(r, values, got):
        far = got[...].reshape(FAR, D)
        sums = dot(adj[r, :, :N], values[...]) + dot(adj[r, :, N:], far)
        return (sums * norm[r, :, :1]).astype(BF)

    def first(r, carry):
        a = averaged(r, own, got_one)
        avg[r] = a
        pre[...] += dot(a, w_one[r])
        return carry

    lax.fori_loop(0, REL, first, 0)
    hidden[...] = jnp.maximum(pre[...], 0.0).astype(BF)
    pack(hidden[...])
    exchange(got_two, 1, None, None)

    def turn(r, out):
        out[pl.ds(pl.multiple_of(r * D, D), D), :] = avg[r].T
        return out

    def turn_one(r, carry):
        turn(r, avg_one_t)
        return carry

    lax.fori_loop(0, REL, turn_one, 0)
    avg_two_t[REL * D :, :] = hidden[...].T
    acc[...] = dot_nt(hidden[...], w_self[...])
    label_row = jnp.broadcast_to(labels[...], (128, N))
    lab = label_row.T[:, :1]
    exchange_wait(got_two, 1)

    def second(r, carry):
        a = averaged(r, hidden, got_two)
        avg[r] = a
        acc[...] += dot_nt(a, w_two[r])
        return carry

    lax.fori_loop(0, REL, second, 0)
    out = acc[...]
    labelled = lab >= 0
    top = jnp.max(out, axis=1, keepdims=True)
    log_total = jnp.log(jnp.sum(jnp.exp(out - top), axis=1, keepdims=True)) + top
    label_hot = jnp.where(lab == iota((N, C), 1), 1.0, 0.0)
    picked = jnp.sum(out * label_hot, axis=1, keepdims=True)
    soft = jnp.exp(out - log_total)
    mask = jnp.where(labelled, 1.0, 0.0)
    grad[...] = jnp.zeros_like(grad)
    grad[:, :C] = (loss_scale * (soft - label_hot) * mask / labelled_count).astype(BF)
    small_out[1] = jnp.broadcast_to(
        jnp.sum(jnp.where(labelled, log_total - picked, 0.0), axis=0, keepdims=True), (1, 128)
    )
    table_acc[...] = jnp.zeros_like(table_acc)

    def spread(r, carry):
        s = (dot(grad[:, :C], w_two[r]) * norm[r, :, :1]).astype(BF)
        table_acc[...] += dot(adj_t[r], s)
        return carry

    lax.fori_loop(0, REL, spread, 0)
    send[...] = table_acc[N:, :].astype(BF).reshape(PEERS, SLOTS, D)
    exchange(got_three, 2, 1, totals)

    partner = (me[0], me[1], me[2], 1 - core)

    def chunks(x, h, left, right, lanes):
        start = pl.multiple_of((x * 2 + h) * BLOCK, BLOCK)
        value = dot(left[pl.ds(start, BLOCK), :], right[...]).astype(BF)
        for j in range(16):
            to = (x, h * 2 + j // 8, (j // 2) % 4, j % 2)
            parts[(*to, slice(None), lanes)] = value[ROWS * j : ROWS * (j + 1), :]

    def to_partner(x, lanes, sem):
        return pltpu.make_async_remote_copy(
            src_ref=parts.at[x, :, :, 1 - core, :, lanes], dst_ref=near.at[x, :, :, :, lanes],
            send_sem=p_send.at[sem], recv_sem=p_recv.at[sem], device_id=partner,
            device_id_type=MESH,
        )

    def add_near(x, z, lanes):
        half[x, z, :, :, lanes] = (
            parts[x, z, :, core, :, lanes].astype(F32) + near[x, z, :, :, lanes].astype(F32)
        ).astype(BF)

    two_lanes = pl.ds(D, CP)
    one_lanes = pl.ds(0, D)

    def turn_two(r, carry):
        turn(r, avg_two_t)
        return carry

    lax.fori_loop(0, REL, turn_two, 0)

    def two_chunks(i, carry):
        chunks(i // 2, i % 2, avg_two_t, grad, two_lanes)
        return carry

    lax.fori_loop(0, 8, two_chunks, 0)
    two_copy = to_partner(slice(None), two_lanes, 4)
    two_copy.start()
    keep[:, :C] = out
    logits_t[...] = keep[...].T[:C, :]
    table_acc[:N, :] += dot(grad[:, :C], w_self[...])
    two_copy.wait()

    def add_two(i, carry):
        add_near(i // 4, i % 4, two_lanes)
        return carry

    lax.fori_loop(0, 16, add_two, 0)

    first_got = (r1a, r1b, r1c)
    first_sum = (q_a, q_b, q_c)
    second_got = (r2a, r2b, r2c)
    second_sum = (t_a, t_b, t_c)
    third_got = (r3a, r3b, r3c)

    def hop(s, phase, j):
        lane, width, order = STREAMS[s]
        axis = order[phase]
        k = lax.rem(me[axis] + j, 4)
        to = list(me)
        to[axis] = k
        if phase == 0:
            at = tuple(k if a == axis else slice(None) for a in range(3))
            ref = half.at[(*at, slice(None), pl.ds(lane, width))]
            got = first_got[s]
        elif phase == 1:
            left = sorted(order[1:])
            at = tuple(k if a == axis else slice(None) for a in left)
            ref = first_sum[s].at[at]
            got = second_got[s]
        else:
            ref = second_sum[s].at[k]
            got = third_got[s]
        sem = (s * 3 + phase) * 3 + j - 1
        return pltpu.make_async_remote_copy(
            src_ref=ref, dst_ref=got.at[j - 1], send_sem=x_send.at[sem], recv_sem=x_recv.at[sem],
            device_id=tuple(to), device_id_type=MESH,
        )

    exchange_wait(got_three, 2)
    for j in (2, 1, 3):
        hop(2, 0, j).start()

    grad_hidden = table_acc[:N, :] + dot(picks_t[...], got_three[...].reshape(FAR, D))
    grad_pre[...] = jnp.where(pre[...] > 0.0, grad_hidden, 0.0).astype(BF)

    for j in (1, 2, 3, 4):
        k = lax.rem(me[0] + j, 4)

        def one_chunks(i, carry):
            chunks(k, i, avg_one_t, grad_pre, one_lanes)
            return carry

        lax.fori_loop(0, 2, one_chunks, 0)
        to_partner(k, one_lanes, j - 1).start()
    for j in (1, 2, 3, 4):
        k = lax.rem(me[0] + j, 4)
        to_partner(k, one_lanes, j - 1).wait()

        def add_one(i, carry):
            add_near(k, i, one_lanes)
            return carry

        lax.fori_loop(0, 4, add_one, 0)
        if j < 4:
            hop(0, 0, j).start()
    for j in (2, 1, 3):
        hop(1, 0, j).start()

    def wide(ref, at):
        return ref[at].astype(F32)

    def sum_first(s):
        lane, width, order = STREAMS[s]
        for j in (1, 2, 3):
            hop(s, 0, j).wait()

        def body(i, carry):
            at = [None, None, None]
            left = sorted(order[1:])
            at[order[0]] = me[order[0]]
            at[left[0]] = i
            at[left[1]] = slice(None)
            total = half[(*at, slice(None), pl.ds(lane, width))].astype(F32)
            for j in range(3):
                total += first_got[s][j, i].astype(F32)
            first_sum[s][i] = total.astype(BF)
            return carry

        lax.fori_loop(0, 4, body, 0)
        for j in (2, 1, 3):
            hop(s, 1, j).start()

    def sum_second(s):
        order = STREAMS[s][2]
        for j in (1, 2, 3):
            hop(s, 1, j).wait()
        m = me[order[1]]
        if order[1] < order[2]:
            total = first_sum[s][m].astype(F32)
        else:
            total = first_sum[s][:, m].astype(F32)
        for j in range(3):
            total += second_got[s][j].astype(F32)
        second_sum[s][...] = total.astype(BF)
        for j in (2, 1, 3):
            hop(s, 2, j).start()

    def sum_third(s):
        order = STREAMS[s][2]
        for j in (1, 2, 3):
            hop(s, 2, j).wait()
        total = second_sum[s][me[order[2]]].astype(F32)
        for j in range(3):
            total += third_got[s][j].astype(F32)
        return total

    for s in (0, 1, 2):
        sum_first(s)
    for s in (0, 1, 2):
        sum_second(s)
    small_wait(1)
    loss[...] = jnp.broadcast_to(jnp.sum(totals[:, :, 0:1]) / labelled_count, (1, 1))
    grad_one[:, :256] = sum_third(0)
    grad_one[:, 256:] = sum_third(1)
    grad_two[...] = sum_third(2)[:, :C]


def sds(shape, dtype):
    return jax.ShapeDtypeStruct(shape, dtype)


def on_device(features, w_one, w_two, self_two, edge_src, edge_dst, send_rows, send_count, labels):
    vm = pl.BlockSpec(memory_space=pltpu.VMEM)
    hbm = pl.BlockSpec(memory_space=pl.ANY)
    V = pltpu.VMEM
    widths = [s[1] for s in STREAMS]
    scratch = [
        V((REL + 1, D, D), BF), V((REL, C, D), BF), V((C, D), BF),
        V((REL, N, TABLE), BF), V((REL, TABLE, N), BF), V((REL, N, 128), F32),
        V((FAR, N), BF), V((N, FAR), BF),
        V((PEERS, SLOTS, D), BF), V((PEERS, SLOTS, D), BF), V((PEERS, SLOTS, D), BF),
        V((PEERS, SLOTS, D), BF),
        V((REL, N, D), BF), V(((REL + 1) * D, N), BF), V(((REL + 1) * D, N), BF),
        V((N, D), F32), V((N, D), BF), V((N, C), F32), V((TABLE, D), F32),
        V((N, CP), BF), V((N, D), BF), V((N, CP), F32),
        V((2, 1, 128), F32), V((PEERS, 1, 128), F32), V((PEERS, 1, 128), F32),
        V((4, 4, 4, 2, ROWS, WIDE), BF), V((4, 4, 4, ROWS, WIDE), BF), V((4, 4, 4, ROWS, WIDE), BF),
        *[V((3, 4, 4, ROWS, w), BF) for w in widths],
        *[V((4, 4, ROWS, w), BF) for w in widths],
        *[V((3, 4, ROWS, w), BF) for w in widths],
        *[V((4, ROWS, w), BF) for w in widths],
        *[V((3, ROWS, w), BF) for w in widths],
        pltpu.SemaphoreType.DMA((3,)),
        pltpu.SemaphoreType.DMA((3,)), pltpu.SemaphoreType.DMA((3,)),
        pltpu.SemaphoreType.DMA((2,)), pltpu.SemaphoreType.DMA((2,)),
        pltpu.SemaphoreType.DMA((5,)), pltpu.SemaphoreType.DMA((5,)),
        pltpu.SemaphoreType.DMA((27,)), pltpu.SemaphoreType.DMA((27,)),
    ]
    logits_t, loss, grad_one, grad_two = pl.pallas_call(
        step_body,
        name="step",
        in_specs=[vm, hbm, hbm, hbm, vm, vm, vm, vm, vm],
        out_specs=[vm, vm, vm, vm],
        out_shape=[sds((C, N), F32), sds((1, 1), F32), sds((ROWS, D), F32), sds((ROWS, C), F32)],
        scratch_shapes=scratch,
        compiler_params=pltpu.CompilerParams(
            collective_id=0, has_side_effects=True, vmem_limit_bytes=62 * MB
        ),
    )(
        features, w_one, jnp.swapaxes(w_two, 1, 2), self_two.T, edge_src, edge_dst, send_rows[0],
        send_count, labels.reshape(1, N),
    )
    return (logits_t.T, loss[0, 0], grad_one, grad_two)


def solution(mesh):
    split = Mesh(mesh.devices.reshape(SIZES), DOM)
    return jax.shard_map(
        on_device,
        mesh=split,
        in_specs=(
            P(DOM, None),
            P(),
            P(),
            P(),
            P(None, DOM, None),
            P(None, DOM, None),
            P(DOM, None, None),
            P(DOM, None),
            P(DOM),
        ),
        out_specs=(P(DOM, None), P(), P(DOM, None), P(DOM, None)),
        check_vma=False,
    )
```

time: 489 us -> 131 us (0.27); the launches traced: 482 us -> 130 us
  local copies, waits for them, and re-layouts: 151 us -> 10.5 us
  Pallas kernels: 0 us -> 117 us
  other arithmetic: 103 us -> 0 us
  waiting for transfers between devices: 96.1 us -> 0 us
  matrix products: 58.3 us -> 0 us
  blocking collectives: 36.3 us -> 0 us
  starting transfers between devices: 33.5 us -> 0 us
    pallas_call x0 -> x1, Pallas kernels: none -> 117 us  [on_device(): pl.pallas_call(step_body, name='step', in_specs=[vm, hbm, hbm, hbm, vm, v...]
    all_to_all x4 -> x0, waiting for transfers between devices: 96.1 us -> none  [the longest x1 58.6 us: summed_rows(): lax.all_to_all(own.astype(jnp.bfloat16), far, 0, 0, tiled=True)]
    gather x18 -> x0, local copies, waits for them, and re-layouts: 77.3 us -> none  [the longest x16 66.2 us: one_relation(): picked = node_table[src_rel]]
    dot_general x32 -> x0, matrix products: 58.3 us -> none  [the longest x16 20.5 us: one_relation(): jnp.einsum('bve,bed->bvd', one_hot.astype(jnp.bfloat16), picked, preferre...]
    scatter-add x9 -> x0, other arithmetic: 50.8 us -> none  [the longest x8 41.6 us: add_relation(): jax.ops.segment_sum(per_edge.reshape(-1, per_edge.shape[-1]), src_rel.res...]
    all_to_all x3 -> x0, blocking collectives: 36.3 us -> none  [the longest x1 18.3 us: summed_on_arrival(): lax.all_to_all(parts, axis, split_axis=0, concat_axis=0, tiled=True)]
    all_to_all x4 -> x0, starting transfers between devices: 33.5 us -> none  [the longest x1 11.7 us: on_device(): lax.all_to_all(pack_rows(features, picks, live_slot), DOM, split_axis=0,...]
    eq x24 -> x0, local copies, waits for them, and re-layouts: 16.4 us -> none  [the longest x16 10.9 us: one_relation(): one_hot = dst_rel[:, None, :] == block_rows[None, :, None]]
  transfers between devices with their start and end apart: 4 -> 0, of which waited for: 3 -> 0; matrix products, arithmetic and copies ran while one was open for 7% -> 0% of each run, Pallas kernels for 0% -> 0%
where the time goes in v3:
time: 131 us; the launch traced here: 130 us
  Pallas kernels  117 us (89%)
  local copies, waits for them, and re-layouts  10.5 us (8%)
  between operations  2.33 us (2%)
    pallas_call x1, Pallas kernels, on_device(): pl.pallas_call(step_body, name='step', in_specs=[vm, hbm, hbm, hbm, vm, v...  117 us
    unnamed x5, local copies, waits for them, and re-layouts  10.5 us

profile of v3, /device:TPU:0, one launch (start us, length us, event | category | flops | bytes accessed | tf_op | source)
XLA Modules:
  0.0 130.3 jit_solution(2351295721853494893)
XLA Ops:
  0.6 1.4 %copy.14 = s32[1,128,8]{2,1,0:T(8,128)} copy(s32[1,128,8]{1,2,0:T(8,128)} %param.15) | data formatting | bytes 8192 | tf_op args[6]
  2.0 4.3 %copy.16 = bf16[8,512,349]{1,2,0:T(8,128)(2,1)} copy(bf16[8,512,349]{1,0,2:T(8,128)(2,1)} %param.11) | data formatting | bytes 5718016 | tf_op args[2]
  6.4 117.5 %step.1 = (f32[349,256]{1,0:T(8,128)}, f32[1,1]{1,0:T(1,128)}, f32[36,512]{1,0:T(8,128)}, f32[36,349]{1,0:T(8,128)}) custom-call(bf16[256,512]{1,0:T(8,128)(2,1)} %own.1, bf16[9,512,512]{2,1,0:T(8,128)(2,1)} %w_one_hbm.1, bf16[8,349,512]{2,1,0:T(8,128)(2,1)} %bitcast.8, bf16[349,512]{1,0:T(8,128)(2,1)} %bitcast.9, s32[8,2,256]{2,1,0:T(2,128)} %src.1, ...), custom_call_target="tpu_custom_call" | custom-call | tf_op jit(solution)/shard_map/step/pallas_call | solution.py:425
  123.9 1.7 %copy.21 = f32[256,349]{0,1:T(8,128)} copy(f32[256,349]{0,1:T(8,128)} %bitcast.10) | data formatting | bytes 714752
  126.2 1.5 %copy.23 = f32[36,512]{1,0:T(8,128)} copy(f32[36,512]{1,0:T(8,128)} %get-tuple-element.18) | data formatting | bytes 147456
  127.7 1.5 %copy.24 = f32[36,349]{1,0:T(8,128)} copy(f32[36,349]{1,0:T(8,128)} %get-tuple-element.19) | data formatting | bytes 100512

commit v4 on v3

--- a/solution.py
+++ b/solution.py
@@ -48,56 +48,106 @@
     return jnp.where(mask, 1.0, 0.0).astype(BF)
 
 
+def phases():
+    now = []
+
+    def begin(name):
+        if now:
+            now.pop().__exit__(None, None, None)
+        if name:
+            now.append(jax.named_scope(name))
+            now[0].__enter__()
+
+    return begin
+
+
 def step_body(
     own, w_one_hbm, w_two_hbm, w_self_hbm, src, dst, rows, count, labels,
     logits_t, loss, grad_one, grad_two,
-    w_one, w_two, w_self, adj, adj_t, norm, picks, picks_t,
-    send, got_one, got_two, got_three, avg, avg_one_t, avg_two_t,
-    pre, hidden, acc, table_acc, grad, grad_pre, keep,
+    w_one, w_two, w_two_raw, turned, w_self, where_src, adj, adj_t, norm, picks, picks_t,
+    send, got_one, got_two, sums, avg, avg_one_t, avg_two_t,
+    pre, hidden, acc, own_grad, spreads, grad, grad_pre,
     small_out, counts, totals,
-    parts, near, half, r1a, r1b, r1c, q_a, q_b, q_c, r2a, r2b, r2c, t_a, t_b, t_c, r3a, r3b, r3c,
+    parts, half, r1a, r1b, r1c, q_a, q_b, q_c, r2a, r2b, r2c, t_a, t_b, t_c, r3a, r3b, r3c,
     w_sems, a_send, a_recv, s_send, s_recv, p_send, p_recv, x_send, x_recv,
 ):
+    begin = phases()
     me = [lax.axis_index(a) for a in DOM]
     mine = ((me[0] * 4 + me[1]) * 4 + me[2]) * 2 + me[3]
     core = me[3]
 
+    begin("a_greet")
     loads = [
         pltpu.make_async_copy(w_one_hbm, w_one, w_sems.at[0]),
-        pltpu.make_async_copy(w_two_hbm, w_two, w_sems.at[1]),
-        pltpu.make_async_copy(w_self_hbm, w_self, w_sems.at[2]),
+        pltpu.make_async_copy(w_self_hbm, w_self, w_sems.at[1]),
     ]
-    for load in loads:
+
+    def two_load(i):
+        count = min(32, C - 32 * i)
+        return pltpu.make_async_copy(
+            w_two_hbm.at[pl.ds(32 * i, count)], w_two_raw.at[i % 4, pl.ds(0, count)],
+            w_sems.at[2 + i % 4],
+        )
+
+    for load in loads + [two_load(i) for i in range(4)]:
         load.start()
 
-    def relative(k):
-        d0 = k % 4
-        d1 = (k // 4 + d0) % 4
-        d2 = (k // 16 + d1) % 4
-        to = [lax.rem(m + s, n) for m, s, n in zip(me, (d0, d1, d2, k // 64), SIZES)]
-        return to, ((to[0] * 4 + to[1]) * 4 + to[2]) * 2 + to[3]
+    ahead = [[lax.rem(m + d, n) for d in range(n)] for m, n in zip(me, SIZES)]
+    behind = [[lax.rem(m + n - d, n) for d in range(n)] for m, n in zip(me, SIZES)]
+
+    def sixteen(hi, sign, body):
+        q = lax.rem(hi, 4)
+        d3 = lax.div(hi, 4)
+        c = lax.rem(core + d3, 2)
+        if sign > 0:
+            ys = [lax.rem(me[2] + q + j, 4) for j in range(4)]
+        else:
+            ys = [lax.rem(me[2] + 8 - q - j, 4) for j in range(4)]
+        near_axes = ahead if sign > 0 else behind
+        for i in range(16):
+            d0 = i % 4
+            d1 = (i // 4 + d0) % 4
+            if isinstance(hi, int) and hi == 0 and i == 0:
+                continue
+            body(hi * 16 + i, (near_axes[0][d0], near_axes[1][d1], ys[d1], c))
+
+    def everyone(sign, body, start=0, stop=8):
+        if start == 0:
+            sixteen(0, sign, body)
+            start = 1
+
+        def loop(hi, carry):
+            sixteen(hi, sign, body)
+            return carry
+
+        lax.fori_loop(start, stop, loop, 0)
 
     barrier = pltpu.get_barrier_semaphore()
 
-    def greet(k, carry):
-        to, _ = relative(k)
-        pl.semaphore_signal(barrier, inc=1, device_id=tuple(to), device_id_type=MESH)
-        return carry
-
-    lax.fori_loop(1, PEERS, greet, 0)
-
-    spot = iota((FAR, PEERS), 0)
-    peer_hot = spot // SLOTS == iota((FAR, PEERS), 1)
-    by_peer = dot(hot(peer_hot), rows[...].astype(F32).astype(BF))
-    slot = iota((FAR, SLOTS), 0) % SLOTS
+    def greet(k, to):
+        pl.semaphore_signal(barrier, inc=1, device_id=to, device_id_type=MESH)
+
+    everyone(1, greet)
+
+    begin("b_pack")
+    spot = iota((FAR, 1), 0)
+    block = spot >> 3
+    e0 = block & 3
+    e1 = ((block >> 2) + e0) & 3
+    e2 = ((block >> 4) + e1) & 3
+    peer = (
+        (((me[0] + e0) & 3) << 5) + (((me[1] + e1) & 3) << 3) + (((me[2] + e2) & 3) << 1)
+        + ((core + (block >> 6)) & 1)
+    )
+    peer_hot = peer == iota((FAR, PEERS), 1)
+    by_peer = dot_nt(hot(peer_hot), rows[...].astype(F32).astype(BF))
+    slot = spot & 7
     chosen = jnp.sum(jnp.where(slot == iota((FAR, SLOTS), 1), by_peer, 0.0), axis=1, keepdims=True)
     live = jnp.sum(
         jnp.where(peer_hot, jnp.broadcast_to(count[...], (FAR, PEERS)), 0).astype(F32),
         axis=1, keepdims=True,
     )
-    row_of = jnp.where(
-        (iota((FAR, 1), 0) % SLOTS).astype(F32) < live, chosen, -1.0
-    ).astype(I32)
+    row_of = jnp.where(slot.astype(F32) < live, chosen, -1.0).astype(I32)
     picks[...] = hot(row_of == iota((FAR, N), 1))
 
     def pack(values):
@@ -107,100 +157,168 @@
     small_out[0] = jnp.broadcast_to(
         jnp.sum(jnp.where(labels[...] >= 0, 1.0, 0.0), axis=1, keepdims=True), (1, 128)
     )
+    begin("c_barrier")
     pl.semaphore_wait(barrier, PEERS - 1)
 
-    def exchange(got, which, small, small_got):
-        def one(k, carry):
-            to, peer = relative(k)
+    def sender(got, which, small, small_got):
+        def one(k, to):
             pltpu.make_async_remote_copy(
-                src_ref=send.at[peer], dst_ref=got.at[mine], send_sem=a_send.at[which],
-                recv_sem=a_recv.at[which], device_id=tuple(to), device_id_type=MESH,
+                src_ref=send.at[k], dst_ref=got.at[k], send_sem=a_send.at[which],
+                recv_sem=a_recv.at[which * 4 + k // 32], device_id=to, device_id_type=MESH,
             ).start()
             if small is not None:
                 pltpu.make_async_remote_copy(
-                    src_ref=small_out.at[small], dst_ref=small_got.at[mine],
+                    src_ref=small_out.at[small], dst_ref=small_got.at[k],
                     send_sem=s_send.at[small], recv_sem=s_recv.at[small],
-                    device_id=tuple(to), device_id_type=MESH,
+                    device_id=to, device_id_type=MESH,
                 ).start()
-            return carry
-
-        lax.fori_loop(1, PEERS, one, 0)
-        got[mine] = send[mine]
-        if small is not None:
-            small_got[mine] = small_out[small]
+
+        return one
+
+    def group_wait(got, which, g):
+        part = pl.ds(0, 31 if g == 0 else 32)
+        pltpu.make_async_copy(send.at[part], got.at[part], a_recv.at[which * 4 + g]).wait()
 
     rest = pl.ds(0, PEERS - 1)
 
-    def exchange_wait(got, which):
+    def sent_wait(got, which):
         pltpu.make_async_copy(send.at[rest], got.at[rest], a_send.at[which]).wait()
-        pltpu.make_async_copy(send.at[rest], got.at[rest], a_recv.at[which]).wait()
 
     def small_wait(which):
         pltpu.make_async_copy(counts.at[rest], totals.at[rest], s_send.at[which]).wait()
         pltpu.make_async_copy(counts.at[rest], totals.at[rest], s_recv.at[which]).wait()
 
-    exchange(got_one, 0, 0, counts)
+    begin("d_send")
+    everyone(1, sender(got_one, 0, 0, counts))
+    got_one[0] = send[0]
+    counts[0] = small_out[0]
+
+    begin("e_adjacency")
+    far_src = src[...] - N
+    p = far_src >> 3
+    o0 = (me[0] + 4 - (p >> 5)) & 3
+    o1 = (me[1] + 4 - ((p >> 3) & 3)) & 3
+    o2 = (me[2] + 4 - ((p >> 1) & 3)) & 3
+    o3 = (core + 2 - (p & 1)) & 1
+    block_of = o0 + (((o1 - o0) & 3) << 2) + (((o2 - o1) & 3) << 4) + (o3 << 6)
+    where_src[...] = jnp.where(far_src >= 0, N + (block_of << 3) + (far_src & 7), src[...])
 
     def relation(r, carry):
         for b in range(2):
             at = slice(b * 128, (b + 1) * 128)
             dst_hot = hot(dst[r, b : b + 1, :] == iota((128, 256), 0))
-            src_hot = hot(src[r, b : b + 1, :] == iota((TABLE, 256), 0))
+            src_hot = hot(where_src[r, b : b + 1, :] == iota((TABLE, 256), 0))
             adj[r, at, :] = dot_nt(dst_hot, src_hot).astype(BF)
-            adj_t[r, :, at] = dot_nt(src_hot, dst_hot).astype(BF)
             live_edges = jnp.sum(dst_hot.astype(F32), axis=1, keepdims=True)
             norm[r, at, :] = jnp.broadcast_to(1.0 / jnp.maximum(live_edges, 1.0), (128, 128))
         return carry
 
     lax.fori_loop(0, REL, relation, 0)
-    picks_t[...] = picks[...].T
+    begin("f_local")
+
+    def rows_of(got, g, count):
+        return got[32 * g : 32 * (g + count)].reshape(256 * count, D)
+
+    def columns(r, g, count):
+        return adj[r, :, N + 256 * g : N + 256 * (g + count)]
+
+    def gather_most(values, got, which):
+        group_wait(got, which, 0)
+
+        def near_rows(r, carry):
+            sums[r] = dot(adj[r, :, :N], values[...]) + dot(columns(r, 0, 1), rows_of(got, 0, 1))
+            return carry
+
+        lax.fori_loop(0, REL, near_rows, 0)
+        group_wait(got, which, 1)
+        group_wait(got, which, 2)
+
+        def middle_rows(r, carry):
+            sums[r] += dot(columns(r, 1, 2), rows_of(got, 1, 2))
+            return carry
+
+        lax.fori_loop(0, REL, middle_rows, 0)
+
+    def averaged(r, got):
+        total = sums[r] + dot(columns(r, 3, 1), rows_of(got, 3, 1))
+        return (total * norm[r, :, :1]).astype(BF)
+
     avg_one_t[REL * D :, :] = own[...].T
     for load in loads:
         load.wait()
     pre[...] = dot(own[...], w_one[REL])
+    gather_most(own, got_one, 0)
+    begin("g_wait")
     small_wait(0)
     labelled_count = jnp.sum(counts[:, :, 0:1])
-    exchange_wait(got_one, 0)
-
-    def averaged(r, values, got):
-        far = got[...].reshape(FAR, D)
-        sums = dot(adj[r, :, :N], values[...]) + dot(adj[r, :, N:], far)
-        return (sums * norm[r, :, :1]).astype(BF)
+    sent_wait(got_one, 0)
+    group_wait(got_one, 0, 3)
+
+    begin("h_first")
 
     def first(r, carry):
-        a = averaged(r, own, got_one)
+        a = averaged(r, got_one)
         avg[r] = a
         pre[...] += dot(a, w_one[r])
         return carry
 
     lax.fori_loop(0, REL, first, 0)
     hidden[...] = jnp.maximum(pre[...], 0.0).astype(BF)
+    begin("i_pack")
     pack(hidden[...])
-    exchange(got_two, 1, None, None)
+    everyone(1, sender(got_two, 1, None, None))
+    got_two[0] = send[0]
+
+    begin("j_turns")
 
     def turn(r, out):
         out[pl.ds(pl.multiple_of(r * D, D), D), :] = avg[r].T
-        return out
-
-    def turn_one(r, carry):
+
+    def relation_t(r, carry):
+        for b in range(2):
+            dst_hot = hot(dst[r, b : b + 1, :] == iota((128, 256), 0))
+            src_hot = hot(where_src[r, b : b + 1, :] == iota((TABLE, 256), 0))
+            lanes = pl.ds(pl.multiple_of(r * N + b * 128, 128), 128)
+            adj_t[:, lanes] = dot_nt(src_hot, dst_hot).astype(BF)
         turn(r, avg_one_t)
         return carry
 
-    lax.fori_loop(0, REL, turn_one, 0)
+    lax.fori_loop(0, REL, relation_t, 0)
+    begin("ja_weights")
+
+    for i in range(11):
+        two_load(i).wait()
+        at = pl.ds(i * 32, 32)
+        for j in range(4):
+            lanes = slice(128 * j, 128 * (j + 1))
+            turned[j % 2] = w_two_raw[i % 4, :, :, lanes].astype(F32).reshape(32 * REL, 128)
+            for r in range(REL):
+                w_two[r, at, lanes] = turned[j % 2, pl.ds(r, 32, stride=REL), :].astype(BF)
+        if i + 4 < 11:
+            two_load(i + 4).start()
+
+    begin("jb_picks")
+    picks_t[...] = picks[...].T
     avg_two_t[REL * D :, :] = hidden[...].T
-    acc[...] = dot_nt(hidden[...], w_self[...])
-    label_row = jnp.broadcast_to(labels[...], (128, N))
-    lab = label_row.T[:, :1]
-    exchange_wait(got_two, 1)
+    acc[:, :C] = dot_nt(hidden[...], w_self[...])
+    lab = jnp.broadcast_to(labels[...], (128, N)).T[:, :1]
+    begin("jc_gather")
+    gather_most(hidden, got_two, 1)
+    begin("k_wait")
+    sent_wait(got_two, 1)
+    group_wait(got_two, 1, 3)
+
+    begin("l_second")
 
     def second(r, carry):
-        a = averaged(r, hidden, got_two)
+        a = averaged(r, got_two)
         avg[r] = a
-        acc[...] += dot_nt(a, w_two[r])
+        acc[:, :C] += dot_nt(a, w_two[r, :C, :])
         return carry
 
     lax.fori_loop(0, REL, second, 0)
-    out = acc[...]
+    begin("m_soft")
+    out = acc[:, :C]
     labelled = lab >= 0
     top = jnp.max(out, axis=1, keepdims=True)
     log_total = jnp.log(jnp.sum(jnp.exp(out - top), axis=1, keepdims=True)) + top
@@ -213,17 +331,26 @@
     small_out[1] = jnp.broadcast_to(
         jnp.sum(jnp.where(labelled, log_total - picked, 0.0), axis=0, keepdims=True), (1, 128)
     )
-    table_acc[...] = jnp.zeros_like(table_acc)
+
+    begin("n_spread")
 
     def spread(r, carry):
-        s = (dot(grad[:, :C], w_two[r]) * norm[r, :, :1]).astype(BF)
-        table_acc[...] += dot(adj_t[r], s)
+        at = pl.ds(pl.multiple_of(r * N, N), N)
+        spreads[at, :] = (dot(grad[:, :C], w_two[r, :C, :]) * norm[r, :, :1]).astype(BF)
         return carry
 
     lax.fori_loop(0, REL, spread, 0)
-    send[...] = table_acc[N:, :].astype(BF).reshape(PEERS, SLOTS, D)
-    exchange(got_three, 2, 1, totals)
-
+    begin("o_send")
+    got_three = got_one
+    back = sender(got_three, 2, 1, totals)
+    for g in range(4):
+        group = dot(adj_t[N + 256 * g : N + 256 * (g + 1), :], spreads[...])
+        send[32 * g : 32 * (g + 1)] = group.astype(BF).reshape(32, SLOTS, D)
+        everyone(-1, back, 2 * g, 2 * g + 2)
+    got_three[0] = send[0]
+    totals[0] = small_out[1]
+
+    begin("p_two")
     partner = (me[0], me[1], me[2], 1 - core)
 
     def chunks(x, h, left, right, lanes):
@@ -235,14 +362,14 @@
 
     def to_partner(x, lanes, sem):
         return pltpu.make_async_remote_copy(
-            src_ref=parts.at[x, :, :, 1 - core, :, lanes], dst_ref=near.at[x, :, :, :, lanes],
+            src_ref=parts.at[x, :, :, 1 - core, :, lanes], dst_ref=half.at[x, :, :, :, lanes],
             send_sem=p_send.at[sem], recv_sem=p_recv.at[sem], device_id=partner,
             device_id_type=MESH,
         )
 
     def add_near(x, z, lanes):
         half[x, z, :, :, lanes] = (
-            parts[x, z, :, core, :, lanes].astype(F32) + near[x, z, :, :, lanes].astype(F32)
+            parts[x, z, :, core, :, lanes].astype(F32) + half[x, z, :, :, lanes].astype(F32)
         ).astype(BF)
 
     two_lanes = pl.ds(D, CP)
@@ -261,9 +388,8 @@
     lax.fori_loop(0, 8, two_chunks, 0)
     two_copy = to_partner(slice(None), two_lanes, 4)
     two_copy.start()
-    keep[:, :C] = out
-    logits_t[...] = keep[...].T[:C, :]
-    table_acc[:N, :] += dot(grad[:, :C], w_self[...])
+    logits_t[...] = acc[...].T[:C, :]
+    own_grad[...] = dot(adj_t[:N, :], spreads[...]) + dot(grad[:, :C], w_self[...])
     two_copy.wait()
 
     def add_two(i, carry):
@@ -302,13 +428,18 @@
             device_id=tuple(to), device_id_type=MESH,
         )
 
-    exchange_wait(got_three, 2)
+    begin("q_wait")
+    sent_wait(got_three, 2)
+    for g in range(4):
+        group_wait(got_three, 2, g)
     for j in (2, 1, 3):
         hop(2, 0, j).start()
 
-    grad_hidden = table_acc[:N, :] + dot(picks_t[...], got_three[...].reshape(FAR, D))
+    begin("r_gradpre")
+    grad_hidden = own_grad[...] + dot(picks_t[...], got_three[...].reshape(FAR, D))
     grad_pre[...] = jnp.where(pre[...] > 0.0, grad_hidden, 0.0).astype(BF)
 
+    begin("s_one")
     for j in (1, 2, 3, 4):
         k = lax.rem(me[0] + j, 4)
 
@@ -318,6 +449,7 @@
 
         lax.fori_loop(0, 2, one_chunks, 0)
         to_partner(k, one_lanes, j - 1).start()
+    begin("t_near")
     for j in (1, 2, 3, 4):
         k = lax.rem(me[0] + j, 4)
         to_partner(k, one_lanes, j - 1).wait()
@@ -380,15 +512,26 @@
             total += third_got[s][j].astype(F32)
         return total
 
+    begin("u_first")
     for s in (0, 1, 2):
         sum_first(s)
+    begin("v_second")
     for s in (0, 1, 2):
         sum_second(s)
+    begin("w_third")
     small_wait(1)
     loss[...] = jnp.broadcast_to(jnp.sum(totals[:, :, 0:1]) / labelled_count, (1, 1))
     grad_one[:, :256] = sum_third(0)
     grad_one[:, 256:] = sum_third(1)
     grad_two[...] = sum_third(2)[:, :C]
+    begin(None)
+
+
+def finish_body(a, b, c, d, a_out, b_out, c_out, d_out):
+    a_out[...] = a[...]
+    b_out[...] = b[...]
+    c_out[...] = c[...]
+    d_out[...] = d[...]
 
 
 def sds(shape, dtype):
@@ -401,23 +544,24 @@
     V = pltpu.VMEM
     widths = [s[1] for s in STREAMS]
     scratch = [
-        V((REL + 1, D, D), BF), V((REL, C, D), BF), V((C, D), BF),
-        V((REL, N, TABLE), BF), V((REL, TABLE, N), BF), V((REL, N, 128), F32),
+        V((REL + 1, D, D), BF), V((REL, 352, D), BF), V((4, 32, REL, D), BF), V((2, 256, 128), F32),
+        V((C, D), BF), V((REL, 2, N), I32),
+        V((REL, N, TABLE), BF), V((TABLE, REL * N), BF), V((REL, N, 128), F32),
         V((FAR, N), BF), V((N, FAR), BF),
         V((PEERS, SLOTS, D), BF), V((PEERS, SLOTS, D), BF), V((PEERS, SLOTS, D), BF),
-        V((PEERS, SLOTS, D), BF),
-        V((REL, N, D), BF), V(((REL + 1) * D, N), BF), V(((REL + 1) * D, N), BF),
-        V((N, D), F32), V((N, D), BF), V((N, C), F32), V((TABLE, D), F32),
-        V((N, CP), BF), V((N, D), BF), V((N, CP), F32),
+        V((REL, N, D), F32), V((REL, N, D), BF), V(((REL + 1) * D, N), BF), V(((REL + 1) * D, N), BF),
+        V((N, D), F32), V((N, D), BF), V((N, CP), F32), V((N, D), F32),
+        V((REL * N, D), BF),
+        V((N, CP), BF), V((N, D), BF),
         V((2, 1, 128), F32), V((PEERS, 1, 128), F32), V((PEERS, 1, 128), F32),
-        V((4, 4, 4, 2, ROWS, WIDE), BF), V((4, 4, 4, ROWS, WIDE), BF), V((4, 4, 4, ROWS, WIDE), BF),
+        V((4, 4, 4, 2, ROWS, WIDE), BF), V((4, 4, 4, ROWS, WIDE), BF),
         *[V((3, 4, 4, ROWS, w), BF) for w in widths],
         *[V((4, 4, ROWS, w), BF) for w in widths],
         *[V((3, 4, ROWS, w), BF) for w in widths],
         *[V((4, ROWS, w), BF) for w in widths],
         *[V((3, ROWS, w), BF) for w in widths],
-        pltpu.SemaphoreType.DMA((3,)),
-        pltpu.SemaphoreType.DMA((3,)), pltpu.SemaphoreType.DMA((3,)),
+        pltpu.SemaphoreType.DMA((6,)),
+        pltpu.SemaphoreType.DMA((3,)), pltpu.SemaphoreType.DMA((12,)),
         pltpu.SemaphoreType.DMA((2,)), pltpu.SemaphoreType.DMA((2,)),
         pltpu.SemaphoreType.DMA((5,)), pltpu.SemaphoreType.DMA((5,)),
         pltpu.SemaphoreType.DMA((27,)), pltpu.SemaphoreType.DMA((27,)),
@@ -430,12 +574,20 @@
         out_shape=[sds((C, N), F32), sds((1, 1), F32), sds((ROWS, D), F32), sds((ROWS, C), F32)],
         scratch_shapes=scratch,
         compiler_params=pltpu.CompilerParams(
-            collective_id=0, has_side_effects=True, vmem_limit_bytes=62 * MB
+            collective_id=0, has_side_effects=True, vmem_limit_bytes=63 * MB
         ),
     )(
-        features, w_one, jnp.swapaxes(w_two, 1, 2), self_two.T, edge_src, edge_dst, send_rows[0],
-        send_count, labels.reshape(1, N),
+        features, w_one, jnp.transpose(w_two, (2, 0, 1)), self_two.T, edge_src, edge_dst,
+        send_rows[0].T, send_count, labels.reshape(1, N),
     )
+    logits_t, loss, grad_one, grad_two = pl.pallas_call(
+        finish_body,
+        name="finish",
+        in_specs=[vm] * 4,
+        out_specs=[vm] * 4,
+        out_shape=[sds((C, N), F32), sds((1, 1), F32), sds((ROWS, D), F32), sds((ROWS, C), F32)],
+        compiler_params=pltpu.CompilerParams(vmem_limit_bytes=4 * MB),
+    )(logits_t, loss, grad_one, grad_two)
     return (logits_t.T, loss[0, 0], grad_one, grad_two)
 
 

time: 131 us -> 112 us (0.85)
  Pallas kernels: 117 us -> 108 us
  local copies, waits for them, and re-layouts: 10.5 us -> 2.69 us
  between operations: 2.33 us -> 0.65 us
    pallas_call x1, Pallas kernels: 117 us -> 107 us  [on_device(): pl.pallas_call(step_body, name='step', in_specs=[vm, hbm, hbm, hbm, vm, v...]
    unnamed x5 -> x6, local copies, waits for them, and re-layouts: 10.5 us -> 2.69 us
    pallas_call x0 -> x1, Pallas kernels: none -> 1.36 us  [on_device(): pl.pallas_call(finish_body, name='finish', in_specs=[vm] * 4, out_specs=[...]
where the time goes in v4:
time: 112 us
  Pallas kernels  108 us (96%)
  local copies, waits for them, and re-layouts  2.69 us (2%)
    pallas_call x1, Pallas kernels, on_device(): pl.pallas_call(step_body, name='step', in_specs=[vm, hbm, hbm, hbm, vm, v...  107 us
    unnamed x6, local copies, waits for them, and re-layouts  2.69 us

profile of v4, /device:TPU:0, one launch (start us, length us, event | category | flops | bytes accessed | tf_op | source)
XLA Modules:
  0.0 111.7 jit_solution(3342694845171469287)
XLA Ops:
  0.6 107.0 %step.1 = (f32[349,256]{1,0:T(8,128)}, f32[1,1]{1,0:T(1,128)}, f32[36,512]{1,0:T(8,128)}, f32[36,349]{1,0:T(8,128)}) custom-call(bf16[256,512]{1,0:T(8,128)(2,1)} %own.1, bf16[9,512,512]{2,1,0:T(8,128)(2,1)} %w_one_hbm.1, bf16[349,8,512]{2,1,0:T(8,128)(2,1)} %bitcast.8, bf16[349,512]{1,0:T(8,128)(2,1)} %bitcast.9, s32[8,2,256]{2,1,0:T(2,128)} %src.1, ...), custom_call_target="tpu_custom_call" | custom-call | tf_op jit(solution)/shard_map/step/pallas_call | solution.py:569
  107.7 0.0 copy-start
  107.7 1.0 copy-done
  108.6 0.0 copy-start.1
  108.6 0.9 copy-done.1
  109.5 0.0 copy-start.2
  109.5 0.8 copy-done.2
  110.4 1.4 %finish.1 = (f32[349,256]{1,0:T(8,128)}, f32[1,1]{1,0:T(1,128)}, f32[36,512]{1,0:T(8,128)}, f32[36,349]{1,0:T(8,128)}) custom-call(f32[349,256]{1,0:T(8,128)S(1)} %copy-done, f32[1,1]{1,0:T(1,128)} %get-tuple-element.13.b, f32[36,512]{1,0:T(8,128)S(1)} %copy-done.1, f32[36,349]{1,0:T(8,128)S(1)} %copy-done.2), custom_call_target="tpu_custom_call" | custom-call | tf_op jit(solution)/shard_map/finish/pallas_call | solution.py:583
Async XLA Ops:
  107.7 1.0 copy-start
  108.6 0.9 copy-start.1
  109.5 0.8 copy-start.2

commit v5 on v4

--- a/solution.py
+++ b/solution.py
@@ -1,5 +1,6 @@
 import jax
 import jax.numpy as jnp
+import numpy as np
 from jax import lax
 from jax.experimental import pallas as pl
 from jax.experimental.pallas import tpu as pltpu
@@ -32,6 +33,27 @@
 STREAMS = ((0, 256, (0, 1, 2)), (256, 256, (1, 2, 0)), (512, 384, (2, 0, 1)))
 
 
+def hops(code):
+    return sum(min(d, 4 - d) for d in digits(code)[:3])
+
+
+def digits(code):
+    return (code % 4, code // 4 % 4, code // 16 % 4, code // 64)
+
+
+def block_order():
+    spread = []
+    for k in range(1, PEERS):
+        d0 = k % 4
+        d1 = (k // 4 + d0) % 4
+        d2 = (k // 16 + d1) % 4
+        spread.append(d0 + 4 * d1 + 16 * d2 + 64 * (k // 64))
+    return [0] + sorted(spread, key=lambda code: -hops(code))
+
+
+ORDER = block_order()
+
+
 def dot(a, b):
     return jnp.dot(a, b, preferred_element_type=F32)
 
@@ -62,9 +84,9 @@
 
 
 def step_body(
-    own, w_one_hbm, w_two_hbm, w_self_hbm, src, dst, rows, count, labels,
+    own, w_one_hbm, w_two_hbm, w_self_hbm, src, dst, rows, count, labels, codes,
     logits_t, loss, grad_one, grad_two,
-    w_one, w_two, w_two_raw, turned, w_self, where_src, adj, adj_t, norm, picks, picks_t,
+    w_one, w_two, w_two_raw, turned, w_self, where_src, row_code, adj, adj_t, norm, picks, picks_t,
     send, got_one, got_two, sums, avg, avg_one_t, avg_two_t,
     pre, hidden, acc, own_grad, spreads, grad, grad_pre,
     small_out, counts, totals,
@@ -95,49 +117,24 @@
     ahead = [[lax.rem(m + d, n) for d in range(n)] for m, n in zip(me, SIZES)]
     behind = [[lax.rem(m + n - d, n) for d in range(n)] for m, n in zip(me, SIZES)]
 
-    def sixteen(hi, sign, body):
-        q = lax.rem(hi, 4)
-        d3 = lax.div(hi, 4)
-        c = lax.rem(core + d3, 2)
-        if sign > 0:
-            ys = [lax.rem(me[2] + q + j, 4) for j in range(4)]
-        else:
-            ys = [lax.rem(me[2] + 8 - q - j, 4) for j in range(4)]
-        near_axes = ahead if sign > 0 else behind
-        for i in range(16):
-            d0 = i % 4
-            d1 = (i // 4 + d0) % 4
-            if isinstance(hi, int) and hi == 0 and i == 0:
-                continue
-            body(hi * 16 + i, (near_axes[0][d0], near_axes[1][d1], ys[d1], c))
-
-    def everyone(sign, body, start=0, stop=8):
-        if start == 0:
-            sixteen(0, sign, body)
-            start = 1
-
-        def loop(hi, carry):
-            sixteen(hi, sign, body)
-            return carry
-
-        lax.fori_loop(start, stop, loop, 0)
+    def everyone(where, body, start=1, stop=PEERS):
+        for k in range(start, stop):
+            body(k, tuple(where[i][d] for i, d in enumerate(digits(ORDER[k]))))
 
     barrier = pltpu.get_barrier_semaphore()
 
     def greet(k, to):
         pl.semaphore_signal(barrier, inc=1, device_id=to, device_id_type=MESH)
 
-    everyone(1, greet)
+    everyone(ahead, greet)
 
     begin("b_pack")
-    spot = iota((FAR, 1), 0)
-    block = spot >> 3
-    e0 = block & 3
-    e1 = ((block >> 2) + e0) & 3
-    e2 = ((block >> 4) + e1) & 3
+    row_code[...] = jnp.broadcast_to(codes[...], (TABLE, 128))
+    spot = codes[N:, :] - N
+    code = spot >> 3
     peer = (
-        (((me[0] + e0) & 3) << 5) + (((me[1] + e1) & 3) << 3) + (((me[2] + e2) & 3) << 1)
-        + ((core + (block >> 6)) & 1)
+        (((me[0] + code) & 3) << 5) + (((me[1] + (code >> 2)) & 3) << 3)
+        + (((me[2] + (code >> 4)) & 3) << 1) + ((core + (code >> 6)) & 1)
     )
     peer_hot = peer == iota((FAR, PEERS), 1)
     by_peer = dot_nt(hot(peer_hot), rows[...].astype(F32).astype(BF))
@@ -189,7 +186,7 @@
         pltpu.make_async_copy(counts.at[rest], totals.at[rest], s_recv.at[which]).wait()
 
     begin("d_send")
-    everyone(1, sender(got_one, 0, 0, counts))
+    everyone(ahead, sender(got_one, 0, 0, counts))
     got_one[0] = send[0]
     counts[0] = small_out[0]
 
@@ -200,14 +197,20 @@
     o1 = (me[1] + 4 - ((p >> 3) & 3)) & 3
     o2 = (me[2] + 4 - ((p >> 1) & 3)) & 3
     o3 = (core + 2 - (p & 1)) & 1
-    block_of = o0 + (((o1 - o0) & 3) << 2) + (((o2 - o1) & 3) << 4) + (o3 << 6)
-    where_src[...] = jnp.where(far_src >= 0, N + (block_of << 3) + (far_src & 7), src[...])
+    code_of = o0 + (o1 << 2) + (o2 << 4) + (o3 << 6)
+    where_src[...] = jnp.where(far_src >= 0, N + (code_of << 3) + (far_src & 7), src[...])
+
+    def source_hot(r, b):
+        halves = [
+            hot(where_src[r, b : b + 1, 128 * i : 128 * (i + 1)] == row_code[...]) for i in range(2)
+        ]
+        return jnp.concatenate(halves, axis=1)
 
     def relation(r, carry):
         for b in range(2):
             at = slice(b * 128, (b + 1) * 128)
             dst_hot = hot(dst[r, b : b + 1, :] == iota((128, 256), 0))
-            src_hot = hot(where_src[r, b : b + 1, :] == iota((TABLE, 256), 0))
+            src_hot = source_hot(r, b)
             adj[r, at, :] = dot_nt(dst_hot, src_hot).astype(BF)
             live_edges = jnp.sum(dst_hot.astype(F32), axis=1, keepdims=True)
             norm[r, at, :] = jnp.broadcast_to(1.0 / jnp.maximum(live_edges, 1.0), (128, 128))
@@ -231,16 +234,15 @@
 
         lax.fori_loop(0, REL, near_rows, 0)
         group_wait(got, which, 1)
-        group_wait(got, which, 2)
 
         def middle_rows(r, carry):
-            sums[r] += dot(columns(r, 1, 2), rows_of(got, 1, 2))
+            sums[r] += dot(columns(r, 1, 1), rows_of(got, 1, 1))
             return carry
 
         lax.fori_loop(0, REL, middle_rows, 0)
 
     def averaged(r, got):
-        total = sums[r] + dot(columns(r, 3, 1), rows_of(got, 3, 1))
+        total = sums[r] + dot(columns(r, 2, 2), rows_of(got, 2, 2))
         return (total * norm[r, :, :1]).astype(BF)
 
     avg_one_t[REL * D :, :] = own[...].T
@@ -252,6 +254,7 @@
     small_wait(0)
     labelled_count = jnp.sum(counts[:, :, 0:1])
     sent_wait(got_one, 0)
+    group_wait(got_one, 0, 2)
     group_wait(got_one, 0, 3)
 
     begin("h_first")
@@ -266,7 +269,7 @@
     hidden[...] = jnp.maximum(pre[...], 0.0).astype(BF)
     begin("i_pack")
     pack(hidden[...])
-    everyone(1, sender(got_two, 1, None, None))
+    everyone(ahead, sender(got_two, 1, None, None))
     got_two[0] = send[0]
 
     begin("j_turns")
@@ -277,7 +280,7 @@
     def relation_t(r, carry):
         for b in range(2):
             dst_hot = hot(dst[r, b : b + 1, :] == iota((128, 256), 0))
-            src_hot = hot(where_src[r, b : b + 1, :] == iota((TABLE, 256), 0))
+            src_hot = source_hot(r, b)
             lanes = pl.ds(pl.multiple_of(r * N + b * 128, 128), 128)
             adj_t[:, lanes] = dot_nt(src_hot, dst_hot).astype(BF)
         turn(r, avg_one_t)
@@ -306,6 +309,7 @@
     gather_most(hidden, got_two, 1)
     begin("k_wait")
     sent_wait(got_two, 1)
+    group_wait(got_two, 1, 2)
     group_wait(got_two, 1, 3)
 
     begin("l_second")
@@ -346,7 +350,7 @@
     for g in range(4):
         group = dot(adj_t[N + 256 * g : N + 256 * (g + 1), :], spreads[...])
         send[32 * g : 32 * (g + 1)] = group.astype(BF).reshape(32, SLOTS, D)
-        everyone(-1, back, 2 * g, 2 * g + 2)
+        everyone(behind, back, max(1, 32 * g), 32 * (g + 1))
     got_three[0] = send[0]
     totals[0] = small_out[1]
 
@@ -404,43 +408,83 @@
     second_sum = (t_a, t_b, t_c)
     third_got = (r3a, r3b, r3c)
 
+    def to_axis(axis, step):
+        to = list(me)
+        to[axis] = lax.rem(me[axis] + step, 4)
+        return tuple(to), to[axis]
+
+    def cut(s, upper):
+        lane, width, _ = STREAMS[s]
+        low = 128 * (width // 256)
+        return (lane + low, low, width - low) if upper else (lane, 0, low)
+
+    def first_at(s, k, lane, size):
+        at = tuple(k if a == STREAMS[s][2][0] else slice(None) for a in range(3))
+        return (*at, slice(None), pl.ds(lane, size))
+
+    def first_hop(s, kind, forward):
+        axis = STREAMS[s][2][0]
+        to, k = to_axis(axis, 1 if forward else 3)
+        lane, inner, size = cut(s, forward if kind == "own" else not forward)
+        if kind == "far":
+            k = lax.rem(me[axis] + 2, 4)
+            slot = 2
+        else:
+            slot = 0 if forward else 1
+        sem = s * 12 + {"far": 0, "own": 2, "both": 4}[kind] + (0 if forward else 1)
+        return pltpu.make_async_remote_copy(
+            src_ref=half.at[first_at(s, k, lane, size)],
+            dst_ref=first_got[s].at[slot, :, :, :, pl.ds(inner, size)],
+            send_sem=x_send.at[sem], recv_sem=x_recv.at[sem], device_id=to, device_id_type=MESH,
+        )
+
+    def relay(s):
+        axis = STREAMS[s][2][0]
+        for forward in (True, False):
+            first_hop(s, "far", forward).wait()
+            _, k = to_axis(axis, 1 if forward else 3)
+            lane, inner, size = cut(s, not forward)
+            at = first_at(s, k, lane, size)
+            half[at] = (
+                half[at].astype(F32) + first_got[s][2, :, :, :, inner : inner + size].astype(F32)
+            ).astype(BF)
+            first_hop(s, "both", forward).start()
+
     def hop(s, phase, j):
-        lane, width, order = STREAMS[s]
+        order = STREAMS[s][2]
         axis = order[phase]
-        k = lax.rem(me[axis] + j, 4)
-        to = list(me)
-        to[axis] = k
-        if phase == 0:
-            at = tuple(k if a == axis else slice(None) for a in range(3))
-            ref = half.at[(*at, slice(None), pl.ds(lane, width))]
-            got = first_got[s]
-        elif phase == 1:
-            left = sorted(order[1:])
-            at = tuple(k if a == axis else slice(None) for a in left)
+        to, k = to_axis(axis, j)
+        if phase == 1:
+            at = tuple(k if a == axis else slice(None) for a in sorted(order[1:]))
             ref = first_sum[s].at[at]
             got = second_got[s]
         else:
             ref = second_sum[s].at[k]
             got = third_got[s]
-        sem = (s * 3 + phase) * 3 + j - 1
+        sem = s * 12 + 3 + phase * 3 + j - 1
         return pltpu.make_async_remote_copy(
             src_ref=ref, dst_ref=got.at[j - 1], send_sem=x_send.at[sem], recv_sem=x_recv.at[sem],
-            device_id=tuple(to), device_id_type=MESH,
+            device_id=to, device_id_type=MESH,
         )
 
+    def first_start(s):
+        for kind in ("far", "own"):
+            for forward in (True, False):
+                first_hop(s, kind, forward).start()
+
+    first_start(2)
     begin("q_wait")
     sent_wait(got_three, 2)
     for g in range(4):
         group_wait(got_three, 2, g)
-    for j in (2, 1, 3):
-        hop(2, 0, j).start()
 
     begin("r_gradpre")
     grad_hidden = own_grad[...] + dot(picks_t[...], got_three[...].reshape(FAR, D))
     grad_pre[...] = jnp.where(pre[...] > 0.0, grad_hidden, 0.0).astype(BF)
 
     begin("s_one")
-    for j in (1, 2, 3, 4):
+
+    def one_block(j):
         k = lax.rem(me[0] + j, 4)
 
         def one_chunks(i, carry):
@@ -448,29 +492,42 @@
             return carry
 
         lax.fori_loop(0, 2, one_chunks, 0)
-        to_partner(k, one_lanes, j - 1).start()
-    begin("t_near")
-    for j in (1, 2, 3, 4):
+        to_partner(k, one_lanes, j).start()
+
+    def one_near(j):
         k = lax.rem(me[0] + j, 4)
-        to_partner(k, one_lanes, j - 1).wait()
+        to_partner(k, one_lanes, j).wait()
 
         def add_one(i, carry):
             add_near(k, i, one_lanes)
             return carry
 
         lax.fori_loop(0, 4, add_one, 0)
-        if j < 4:
-            hop(0, 0, j).start()
-    for j in (2, 1, 3):
-        hop(1, 0, j).start()
-
-    def wide(ref, at):
-        return ref[at].astype(F32)
+        if j == 2:
+            first_hop(0, "far", True).start()
+            first_hop(0, "far", False).start()
+        elif j:
+            first_hop(0, "own", j == 1).start()
+
+    one_block(2)
+    one_block(1)
+    one_near(2)
+    one_block(3)
+    one_near(1)
+    one_block(0)
+    begin("t_near")
+    relay(2)
+    one_near(3)
+    one_near(0)
+    first_start(1)
+    relay(0)
+    relay(1)
 
     def sum_first(s):
         lane, width, order = STREAMS[s]
-        for j in (1, 2, 3):
-            hop(s, 0, j).wait()
+        for kind in ("own", "both"):
+            for forward in (True, False):
+                first_hop(s, kind, forward).wait()
 
         def body(i, carry):
             at = [None, None, None]
@@ -479,7 +536,7 @@
             at[left[0]] = i
             at[left[1]] = slice(None)
             total = half[(*at, slice(None), pl.ds(lane, width))].astype(F32)
-            for j in range(3):
+            for j in range(2):
                 total += first_got[s][j, i].astype(F32)
             first_sum[s][i] = total.astype(BF)
             return carry
@@ -513,10 +570,10 @@
         return total
 
     begin("u_first")
-    for s in (0, 1, 2):
+    for s in (2, 0, 1):
         sum_first(s)
     begin("v_second")
-    for s in (0, 1, 2):
+    for s in (2, 0, 1):
         sum_second(s)
     begin("w_third")
     small_wait(1)
@@ -545,7 +602,7 @@
     widths = [s[1] for s in STREAMS]
     scratch = [
         V((REL + 1, D, D), BF), V((REL, 352, D), BF), V((4, 32, REL, D), BF), V((2, 256, 128), F32),
-        V((C, D), BF), V((REL, 2, N), I32),
+        V((C, D), BF), V((REL, 2, N), I32), V((TABLE, 128), I32),
         V((REL, N, TABLE), BF), V((TABLE, REL * N), BF), V((REL, N, 128), F32),
         V((FAR, N), BF), V((N, FAR), BF),
         V((PEERS, SLOTS, D), BF), V((PEERS, SLOTS, D), BF), V((PEERS, SLOTS, D), BF),
@@ -564,12 +621,15 @@
         pltpu.SemaphoreType.DMA((3,)), pltpu.SemaphoreType.DMA((12,)),
         pltpu.SemaphoreType.DMA((2,)), pltpu.SemaphoreType.DMA((2,)),
         pltpu.SemaphoreType.DMA((5,)), pltpu.SemaphoreType.DMA((5,)),
-        pltpu.SemaphoreType.DMA((27,)), pltpu.SemaphoreType.DMA((27,)),
+        pltpu.SemaphoreType.DMA((36,)), pltpu.SemaphoreType.DMA((36,)),
     ]
+    codes = np.concatenate(
+        [np.arange(N)] + [N + SLOTS * code + np.arange(SLOTS) for code in ORDER]
+    ).astype(np.int32)
     logits_t, loss, grad_one, grad_two = pl.pallas_call(
         step_body,
         name="step",
-        in_specs=[vm, hbm, hbm, hbm, vm, vm, vm, vm, vm],
+        in_specs=[vm, hbm, hbm, hbm, vm, vm, vm, vm, vm, vm],
         out_specs=[vm, vm, vm, vm],
         out_shape=[sds((C, N), F32), sds((1, 1), F32), sds((ROWS, D), F32), sds((ROWS, C), F32)],
         scratch_shapes=scratch,
@@ -579,6 +639,7 @@
     )(
         features, w_one, jnp.transpose(w_two, (2, 0, 1)), self_two.T, edge_src, edge_dst,
         send_rows[0].T, send_count, labels.reshape(1, N),
+        jnp.asarray(codes).reshape(TABLE, 1),
     )
     logits_t, loss, grad_one, grad_two = pl.pallas_call(
         finish_body,

time: 112 us -> 107 us (0.955)
  Pallas kernels: 108 us -> 104 us
    pallas_call x1, Pallas kernels: 107 us -> 102 us  [on_device(): pl.pallas_call(step_body, name='step', in_specs=[vm, hbm, hbm, hbm, vm, v...]
where the time goes in v5:
time: 107 us
  Pallas kernels  104 us (97%)
  local copies, waits for them, and re-layouts  2.69 us (3%)
    pallas_call x1, Pallas kernels, on_device(): pl.pallas_call(step_body, name='step', in_specs=[vm, hbm, hbm, hbm, vm, v...  102 us
    unnamed x6, local copies, waits for them, and re-layouts  2.69 us

profile of v5, /device:TPU:0, one launch (start us, length us, event | category | flops | bytes accessed | tf_op | source)
XLA Modules:
  0.0 106.9 jit_solution(16193540702668567731)
XLA Ops:
  0.6 102.2 %step.1 = (f32[349,256]{1,0:T(8,128)}, f32[1,1]{1,0:T(1,128)}, f32[36,512]{1,0:T(8,128)}, f32[36,349]{1,0:T(8,128)}) custom-call(bf16[256,512]{1,0:T(8,128)(2,1)} %own.1, bf16[9,512,512]{2,1,0:T(8,128)(2,1)} %w_one_hbm.1, bf16[349,8,512]{2,1,0:T(8,128)(2,1)} %bitcast.8, bf16[349,512]{1,0:T(8,128)(2,1)} %bitcast.9, s32[8,2,256]{2,1,0:T(2,128)} %src.1, ...), custom_call_target="tpu_custom_call" | custom-call | tf_op jit(solution)/shard_map/step/pallas_call | solution.py:629
  102.8 0.0 copy-start
  102.8 1.0 copy-done
  103.8 0.0 copy-start.1
  103.8 0.9 copy-done.1
  104.7 0.0 copy-start.2
  104.7 0.8 copy-done.2
  105.5 1.4 %finish.1 = (f32[349,256]{1,0:T(8,128)}, f32[1,1]{1,0:T(1,128)}, f32[36,512]{1,0:T(8,128)}, f32[36,349]{1,0:T(8,128)}) custom-call(f32[349,256]{1,0:T(8,128)S(1)} %copy-done, f32[1,1]{1,0:T(1,128)} %get-tuple-element.13.b, f32[36,512]{1,0:T(8,128)S(1)} %copy-done.1, f32[36,349]{1,0:T(8,128)S(1)} %copy-done.2), custom_call_target="tpu_custom_call" | custom-call | tf_op jit(solution)/shard_map/finish/pallas_call | solution.py:644
Async XLA Ops:
  102.8 1.0 copy-start
  103.8 0.9 copy-start.1
  104.7 0.8 copy-start.2

commit v6 on v5

--- a/solution.py
+++ b/solution.py
@@ -15,6 +15,8 @@
 MESH = pl.DeviceIdType.MESH
 loss_scale = 256.0
 MB = 1 << 20
+VLIM = 63
+UNROLL = 4
 
 PEERS = 128
 CHIPS = 64
@@ -30,7 +32,17 @@
 WIDE = D + CP
 BLOCK = 16 * ROWS
 
-STREAMS = ((0, 256, (0, 1, 2)), (256, 256, (1, 2, 0)), (512, 384, (2, 0, 1)))
+STREAMS = (
+    (0, 0, 36, (0, 1, 2)),
+    (384, 0, 16, (0, 1, 2)),
+    (128, 0, 36, (1, 2, 0)),
+    (384, 16, 20, (1, 2, 0)),
+    (256, 0, 36, (2, 0, 1)),
+    (512, 0, 36, (0, 1, 2)),
+    (640, 0, 36, (1, 2, 0)),
+    (768, 0, 36, (2, 0, 1)),
+)
+ONE_X, ONE_REST, TWO = (0, 1), (2, 3, 4), (5, 6, 7)
 
 
 def hops(code):
@@ -84,16 +96,21 @@
 
 
 def step_body(
-    own, w_one_hbm, w_two_hbm, w_self_hbm, src, dst, rows, count, labels, codes,
+    own_hbm, w_one_hbm, w_two_hbm, w_self_hbm, src_hbm, dst_hbm, rows_hbm, count_hbm, labels_hbm,
+    codes_hbm,
     logits_t, loss, grad_one, grad_two,
-    w_one, w_two, w_two_raw, turned, w_self, where_src, row_code, adj, adj_t, norm, picks, picks_t,
+    own, src, dst, rows, count, labels, w_one, w_two, w_two_raw, turned, w_self, where_src, row_code, adj, adj_t, norm, picks, picks_t,
     send, got_one, got_two, sums, avg, avg_one_t, avg_two_t,
-    pre, hidden, acc, own_grad, spreads, grad, grad_pre,
+    pre, hidden, acc, logits_v, own_grad, spreads, grad, grad_pre,
     small_out, counts, totals,
-    parts, half, r1a, r1b, r1c, q_a, q_b, q_c, r2a, r2b, r2c, t_a, t_b, t_c, r3a, r3b, r3c,
-    w_sems, a_send, a_recv, s_send, s_recv, p_send, p_recv, x_send, x_recv,
+    parts, half, *rest_refs,
 ):
     begin = phases()
+    count_s = len(STREAMS)
+    first_got, first_sum, second_got, second_sum, third_got = (
+        rest_refs[i * count_s : (i + 1) * count_s] for i in range(5)
+    )
+    w_sems, a_send, a_recv, s_send, s_recv, p_send, p_recv, x_send, x_recv = rest_refs[5 * count_s :]
     me = [lax.axis_index(a) for a in DOM]
     mine = ((me[0] * 4 + me[1]) * 4 + me[2]) * 2 + me[3]
     core = me[3]
@@ -111,7 +128,16 @@
             w_sems.at[2 + i % 4],
         )
 
-    for load in loads + [two_load(i) for i in range(4)]:
+    inputs = [
+        pltpu.make_async_copy(a, b, w_sems.at[6 + i])
+        for i, (a, b) in enumerate(
+            (
+                (codes_hbm, row_code), (rows_hbm, rows), (count_hbm, count), (own_hbm, own),
+                (labels_hbm, labels), (src_hbm, src), (dst_hbm, dst),
+            )
+        )
+    ]
+    for load in inputs + loads + [two_load(i) for i in range(4)]:
         load.start()
 
     ahead = [[lax.rem(m + d, n) for d in range(n)] for m, n in zip(me, SIZES)]
@@ -129,8 +155,9 @@
     everyone(ahead, greet)
 
     begin("b_pack")
-    row_code[...] = jnp.broadcast_to(codes[...], (TABLE, 128))
-    spot = codes[N:, :] - N
+    for load in inputs:
+        load.wait()
+    spot = row_code[N:, :1] - N
     code = spot >> 3
     peer = (
         (((me[0] + code) & 3) << 5) + (((me[1] + (code >> 2)) & 3) << 3)
@@ -157,18 +184,22 @@
     begin("c_barrier")
     pl.semaphore_wait(barrier, PEERS - 1)
 
-    def sender(got, which, small, small_got):
+    def sender(got, which):
         def one(k, to):
             pltpu.make_async_remote_copy(
                 src_ref=send.at[k], dst_ref=got.at[k], send_sem=a_send.at[which],
                 recv_sem=a_recv.at[which * 4 + k // 32], device_id=to, device_id_type=MESH,
             ).start()
-            if small is not None:
-                pltpu.make_async_remote_copy(
-                    src_ref=small_out.at[small], dst_ref=small_got.at[k],
-                    send_sem=s_send.at[small], recv_sem=s_recv.at[small],
-                    device_id=to, device_id_type=MESH,
-                ).start()
+
+        return one
+
+    def small_sender(small, small_got):
+        def one(k, to):
+            pltpu.make_async_remote_copy(
+                src_ref=small_out.at[small], dst_ref=small_got.at[k],
+                send_sem=s_send.at[small], recv_sem=s_recv.at[small],
+                device_id=to, device_id_type=MESH,
+            ).start()
 
         return one
 
@@ -186,9 +217,8 @@
         pltpu.make_async_copy(counts.at[rest], totals.at[rest], s_recv.at[which]).wait()
 
     begin("d_send")
-    everyone(ahead, sender(got_one, 0, 0, counts))
+    everyone(ahead, sender(got_one, 0))
     got_one[0] = send[0]
-    counts[0] = small_out[0]
 
     begin("e_adjacency")
     far_src = src[...] - N
@@ -216,7 +246,9 @@
             norm[r, at, :] = jnp.broadcast_to(1.0 / jnp.maximum(live_edges, 1.0), (128, 128))
         return carry
 
-    lax.fori_loop(0, REL, relation, 0)
+    lax.fori_loop(0, REL, relation, 0, unroll=UNROLL)
+    everyone(ahead, small_sender(0, counts))
+    counts[0] = small_out[0]
     begin("f_local")
 
     def rows_of(got, g, count):
@@ -232,14 +264,14 @@
             sums[r] = dot(adj[r, :, :N], values[...]) + dot(columns(r, 0, 1), rows_of(got, 0, 1))
             return carry
 
-        lax.fori_loop(0, REL, near_rows, 0)
+        lax.fori_loop(0, REL, near_rows, 0, unroll=UNROLL)
         group_wait(got, which, 1)
 
         def middle_rows(r, carry):
             sums[r] += dot(columns(r, 1, 1), rows_of(got, 1, 1))
             return carry
 
-        lax.fori_loop(0, REL, middle_rows, 0)
+        lax.fori_loop(0, REL, middle_rows, 0, unroll=UNROLL)
 
     def averaged(r, got):
         total = sums[r] + dot(columns(r, 2, 2), rows_of(got, 2, 2))
@@ -251,8 +283,6 @@
     pre[...] = dot(own[...], w_one[REL])
     gather_most(own, got_one, 0)
     begin("g_wait")
-    small_wait(0)
-    labelled_count = jnp.sum(counts[:, :, 0:1])
     sent_wait(got_one, 0)
     group_wait(got_one, 0, 2)
     group_wait(got_one, 0, 3)
@@ -265,11 +295,11 @@
         pre[...] += dot(a, w_one[r])
         return carry
 
-    lax.fori_loop(0, REL, first, 0)
+    lax.fori_loop(0, REL, first, 0, unroll=UNROLL)
     hidden[...] = jnp.maximum(pre[...], 0.0).astype(BF)
     begin("i_pack")
     pack(hidden[...])
-    everyone(ahead, sender(got_two, 1, None, None))
+    everyone(ahead, sender(got_two, 1))
     got_two[0] = send[0]
 
     begin("j_turns")
@@ -286,7 +316,7 @@
         turn(r, avg_one_t)
         return carry
 
-    lax.fori_loop(0, REL, relation_t, 0)
+    lax.fori_loop(0, REL, relation_t, 0, unroll=UNROLL)
     begin("ja_weights")
 
     for i in range(11):
@@ -308,6 +338,8 @@
     begin("jc_gather")
     gather_most(hidden, got_two, 1)
     begin("k_wait")
+    small_wait(0)
+    labelled_count = jnp.sum(counts[:, :, 0:1])
     sent_wait(got_two, 1)
     group_wait(got_two, 1, 2)
     group_wait(got_two, 1, 3)
@@ -320,7 +352,7 @@
         acc[:, :C] += dot_nt(a, w_two[r, :C, :])
         return carry
 
-    lax.fori_loop(0, REL, second, 0)
+    lax.fori_loop(0, REL, second, 0, unroll=UNROLL)
     begin("m_soft")
     out = acc[:, :C]
     labelled = lab >= 0
@@ -343,16 +375,15 @@
         spreads[at, :] = (dot(grad[:, :C], w_two[r, :C, :]) * norm[r, :, :1]).astype(BF)
         return carry
 
-    lax.fori_loop(0, REL, spread, 0)
+    lax.fori_loop(0, REL, spread, 0, unroll=UNROLL)
     begin("o_send")
     got_three = got_one
-    back = sender(got_three, 2, 1, totals)
+    back = sender(got_three, 2)
     for g in range(4):
         group = dot(adj_t[N + 256 * g : N + 256 * (g + 1), :], spreads[...])
         send[32 * g : 32 * (g + 1)] = group.astype(BF).reshape(32, SLOTS, D)
         everyone(behind, back, max(1, 32 * g), 32 * (g + 1))
     got_three[0] = send[0]
-    totals[0] = small_out[1]
 
     begin("p_two")
     partner = (me[0], me[1], me[2], 1 - core)
@@ -392,7 +423,9 @@
     lax.fori_loop(0, 8, two_chunks, 0)
     two_copy = to_partner(slice(None), two_lanes, 4)
     two_copy.start()
-    logits_t[...] = acc[...].T[:C, :]
+    logits_v[...] = acc[...].T[:C, :]
+    logits_copy = pltpu.make_async_copy(logits_v, logits_t, w_sems.at[13])
+    logits_copy.start()
     own_grad[...] = dot(adj_t[:N, :], spreads[...]) + dot(grad[:, :C], w_self[...])
     two_copy.wait()
 
@@ -402,11 +435,8 @@
 
     lax.fori_loop(0, 16, add_two, 0)
 
-    first_got = (r1a, r1b, r1c)
-    first_sum = (q_a, q_b, q_c)
-    second_got = (r2a, r2b, r2c)
-    second_sum = (t_a, t_b, t_c)
-    third_got = (r3a, r3b, r3c)
+    everyone(ahead, small_sender(1, totals))
+    totals[0] = small_out[1]
 
     def to_axis(axis, step):
         to = list(me)
@@ -414,18 +444,19 @@
         return tuple(to), to[axis]
 
     def cut(s, upper):
-        lane, width, _ = STREAMS[s]
-        low = 128 * (width // 256)
-        return (lane + low, low, width - low) if upper else (lane, 0, low)
-
-    def first_at(s, k, lane, size):
-        at = tuple(k if a == STREAMS[s][2][0] else slice(None) for a in range(3))
-        return (*at, slice(None), pl.ds(lane, size))
+        _, row, rows_s, _ = STREAMS[s]
+        low = 16 if rows_s > 20 else 8
+        return (row + low, low, rows_s - low) if upper else (row, 0, low)
+
+    def first_at(s, k, row, size):
+        lane, _, _, order = STREAMS[s]
+        at = tuple(k if a == order[0] else slice(None) for a in range(3))
+        return (*at, pl.ds(row, size), pl.ds(lane, 128))
 
     def first_hop(s, kind, forward):
-        axis = STREAMS[s][2][0]
+        axis = STREAMS[s][3][0]
         to, k = to_axis(axis, 1 if forward else 3)
-        lane, inner, size = cut(s, forward if kind == "own" else not forward)
+        row, inner, size = cut(s, forward if kind == "own" else not forward)
         if kind == "far":
             k = lax.rem(me[axis] + 2, 4)
             slot = 2
@@ -433,25 +464,25 @@
             slot = 0 if forward else 1
         sem = s * 12 + {"far": 0, "own": 2, "both": 4}[kind] + (0 if forward else 1)
         return pltpu.make_async_remote_copy(
-            src_ref=half.at[first_at(s, k, lane, size)],
-            dst_ref=first_got[s].at[slot, :, :, :, pl.ds(inner, size)],
+            src_ref=half.at[first_at(s, k, row, size)],
+            dst_ref=first_got[s].at[slot, :, :, pl.ds(inner, size), :],
             send_sem=x_send.at[sem], recv_sem=x_recv.at[sem], device_id=to, device_id_type=MESH,
         )
 
     def relay(s):
-        axis = STREAMS[s][2][0]
+        axis = STREAMS[s][3][0]
         for forward in (True, False):
             first_hop(s, "far", forward).wait()
             _, k = to_axis(axis, 1 if forward else 3)
-            lane, inner, size = cut(s, not forward)
-            at = first_at(s, k, lane, size)
+            row, inner, size = cut(s, not forward)
+            at = first_at(s, k, row, size)
             half[at] = (
-                half[at].astype(F32) + first_got[s][2, :, :, :, inner : inner + size].astype(F32)
+                half[at].astype(F32) + first_got[s][2, :, :, inner : inner + size, :].astype(F32)
             ).astype(BF)
             first_hop(s, "both", forward).start()
 
     def hop(s, phase, j):
-        order = STREAMS[s][2]
+        order = STREAMS[s][3]
         axis = order[phase]
         to, k = to_axis(axis, j)
         if phase == 1:
@@ -472,7 +503,8 @@
             for forward in (True, False):
                 first_hop(s, kind, forward).start()
 
-    first_start(2)
+    for s in TWO:
+        first_start(s)
     begin("q_wait")
     sent_wait(got_three, 2)
     for g in range(4):
@@ -503,28 +535,32 @@
             return carry
 
         lax.fori_loop(0, 4, add_one, 0)
-        if j == 2:
-            first_hop(0, "far", True).start()
-            first_hop(0, "far", False).start()
-        elif j:
-            first_hop(0, "own", j == 1).start()
+        for s in ONE_X:
+            if j == 2:
+                first_hop(s, "far", True).start()
+                first_hop(s, "far", False).start()
+            elif j:
+                first_hop(s, "own", j == 1).start()
 
     one_block(2)
     one_block(1)
+    for s in TWO:
+        relay(s)
     one_near(2)
     one_block(3)
     one_near(1)
     one_block(0)
-    begin("t_near")
-    relay(2)
     one_near(3)
     one_near(0)
-    first_start(1)
-    relay(0)
-    relay(1)
+    begin("t_near")
+    for s in ONE_REST:
+        first_start(s)
+    begin("ta_relay")
+    for s in ONE_X + ONE_REST:
+        relay(s)
 
     def sum_first(s):
-        lane, width, order = STREAMS[s]
+        lane, row, rows_s, order = STREAMS[s]
         for kind in ("own", "both"):
             for forward in (True, False):
                 first_hop(s, kind, forward).wait()
@@ -535,7 +571,7 @@
             at[order[0]] = me[order[0]]
             at[left[0]] = i
             at[left[1]] = slice(None)
-            total = half[(*at, slice(None), pl.ds(lane, width))].astype(F32)
+            total = half[(*at, pl.ds(row, rows_s), pl.ds(lane, 128))].astype(F32)
             for j in range(2):
                 total += first_got[s][j, i].astype(F32)
             first_sum[s][i] = total.astype(BF)
@@ -546,7 +582,7 @@
             hop(s, 1, j).start()
 
     def sum_second(s):
-        order = STREAMS[s][2]
+        order = STREAMS[s][3]
         for j in (1, 2, 3):
             hop(s, 1, j).wait()
         m = me[order[1]]
@@ -561,7 +597,7 @@
             hop(s, 2, j).start()
 
     def sum_third(s):
-        order = STREAMS[s][2]
+        order = STREAMS[s][3]
         for j in (1, 2, 3):
             hop(s, 2, j).wait()
         total = second_sum[s][me[order[2]]].astype(F32)
@@ -570,25 +606,40 @@
         return total
 
     begin("u_first")
-    for s in (2, 0, 1):
+    for s in TWO:
+        sum_first(s)
+    begin("ua_first")
+    for s in ONE_X + ONE_REST:
         sum_first(s)
     begin("v_second")
-    for s in (2, 0, 1):
+    for s in TWO + ONE_X + ONE_REST:
         sum_second(s)
     begin("w_third")
     small_wait(1)
-    loss[...] = jnp.broadcast_to(jnp.sum(totals[:, :, 0:1]) / labelled_count, (1, 1))
-    grad_one[:, :256] = sum_third(0)
-    grad_one[:, 256:] = sum_third(1)
-    grad_two[...] = sum_third(2)[:, :C]
+    loss[...] = jnp.broadcast_to(jnp.sum(totals[:, :, 0:1]) / labelled_count, (1, 128))
+    logits_copy.wait()
+    for s in TWO + ONE_X + ONE_REST:
+        lane, row, rows_s, _ = STREAMS[s]
+        total = sum_third(s)
+        if lane < D:
+            grad_one[row : row + rows_s, lane : lane + 128] = total
+        else:
+            lane -= D
+            size = min(128, C - lane)
+            grad_two[:, lane : lane + size] = total[:, :size]
     begin(None)
 
 
-def finish_body(a, b, c, d, a_out, b_out, c_out, d_out):
-    a_out[...] = a[...]
-    b_out[...] = b[...]
-    c_out[...] = c[...]
-    d_out[...] = d[...]
+def finish_body(a, b, c, d, a_out, b_out, c_out, d_out, b_row, sems):
+    copies = [
+        pltpu.make_async_copy(x, y, sems.at[i])
+        for i, (x, y) in enumerate(((a, a_out), (b, b_row), (c, c_out), (d, d_out)))
+    ]
+    for copy in copies:
+        copy.start()
+    for copy in copies:
+        copy.wait()
+    b_out[...] = b_row[:, :1]
 
 
 def sds(shape, dtype):
@@ -599,29 +650,31 @@
     vm = pl.BlockSpec(memory_space=pltpu.VMEM)
     hbm = pl.BlockSpec(memory_space=pl.ANY)
     V = pltpu.VMEM
-    widths = [s[1] for s in STREAMS]
+    rows = [s[2] for s in STREAMS]
     scratch = [
+        V((N, D), BF), V((REL, 2, N), I32), V((REL, 2, N), I32), V((SLOTS, PEERS), I32),
+        V((1, PEERS), I32), V((1, N), I32),
         V((REL + 1, D, D), BF), V((REL, 352, D), BF), V((4, 32, REL, D), BF), V((2, 256, 128), F32),
         V((C, D), BF), V((REL, 2, N), I32), V((TABLE, 128), I32),
         V((REL, N, TABLE), BF), V((TABLE, REL * N), BF), V((REL, N, 128), F32),
         V((FAR, N), BF), V((N, FAR), BF),
         V((PEERS, SLOTS, D), BF), V((PEERS, SLOTS, D), BF), V((PEERS, SLOTS, D), BF),
         V((REL, N, D), F32), V((REL, N, D), BF), V(((REL + 1) * D, N), BF), V(((REL + 1) * D, N), BF),
-        V((N, D), F32), V((N, D), BF), V((N, CP), F32), V((N, D), F32),
+        V((N, D), F32), V((N, D), BF), V((N, CP), F32), V((C, N), F32), V((N, D), F32),
         V((REL * N, D), BF),
         V((N, CP), BF), V((N, D), BF),
         V((2, 1, 128), F32), V((PEERS, 1, 128), F32), V((PEERS, 1, 128), F32),
         V((4, 4, 4, 2, ROWS, WIDE), BF), V((4, 4, 4, ROWS, WIDE), BF),
-        *[V((3, 4, 4, ROWS, w), BF) for w in widths],
-        *[V((4, 4, ROWS, w), BF) for w in widths],
-        *[V((3, 4, ROWS, w), BF) for w in widths],
-        *[V((4, ROWS, w), BF) for w in widths],
-        *[V((3, ROWS, w), BF) for w in widths],
-        pltpu.SemaphoreType.DMA((6,)),
+        *[V((3, 4, 4, r, 128), BF) for r in rows],
+        *[V((4, 4, r, 128), BF) for r in rows],
+        *[V((3, 4, r, 128), BF) for r in rows],
+        *[V((4, r, 128), BF) for r in rows],
+        *[V((3, r, 128), BF) for r in rows],
+        pltpu.SemaphoreType.DMA((14,)),
         pltpu.SemaphoreType.DMA((3,)), pltpu.SemaphoreType.DMA((12,)),
         pltpu.SemaphoreType.DMA((2,)), pltpu.SemaphoreType.DMA((2,)),
         pltpu.SemaphoreType.DMA((5,)), pltpu.SemaphoreType.DMA((5,)),
-        pltpu.SemaphoreType.DMA((36,)), pltpu.SemaphoreType.DMA((36,)),
+        pltpu.SemaphoreType.DMA((96,)), pltpu.SemaphoreType.DMA((96,)),
     ]
     codes = np.concatenate(
         [np.arange(N)] + [N + SLOTS * code + np.arange(SLOTS) for code in ORDER]
@@ -629,25 +682,26 @@
     logits_t, loss, grad_one, grad_two = pl.pallas_call(
         step_body,
         name="step",
-        in_specs=[vm, hbm, hbm, hbm, vm, vm, vm, vm, vm, vm],
-        out_specs=[vm, vm, vm, vm],
-        out_shape=[sds((C, N), F32), sds((1, 1), F32), sds((ROWS, D), F32), sds((ROWS, C), F32)],
+        in_specs=[hbm] * 10,
+        out_specs=[hbm, vm, vm, vm],
+        out_shape=[sds((C, N), F32), sds((1, 128), F32), sds((ROWS, D), F32), sds((ROWS, C), F32)],
         scratch_shapes=scratch,
         compiler_params=pltpu.CompilerParams(
-            collective_id=0, has_side_effects=True, vmem_limit_bytes=63 * MB
+            collective_id=0, has_side_effects=True, vmem_limit_bytes=int(VLIM * MB)
         ),
     )(
         features, w_one, jnp.transpose(w_two, (2, 0, 1)), self_two.T, edge_src, edge_dst,
         send_rows[0].T, send_count, labels.reshape(1, N),
-        jnp.asarray(codes).reshape(TABLE, 1),
+        jnp.asarray(np.repeat(codes[:, None], 128, axis=1)),
     )
     logits_t, loss, grad_one, grad_two = pl.pallas_call(
         finish_body,
         name="finish",
-        in_specs=[vm] * 4,
+        in_specs=[hbm] * 4,
         out_specs=[vm] * 4,
         out_shape=[sds((C, N), F32), sds((1, 1), F32), sds((ROWS, D), F32), sds((ROWS, C), F32)],
-        compiler_params=pltpu.CompilerParams(vmem_limit_bytes=4 * MB),
+        scratch_shapes=[V((1, 128), F32), pltpu.SemaphoreType.DMA((4,))],
+        compiler_params=pltpu.CompilerParams(vmem_limit_bytes=63 * MB),
     )(logits_t, loss, grad_one, grad_two)
     return (logits_t.T, loss[0, 0], grad_one, grad_two)
 

time: 107 us -> 96 us (0.90)
  Pallas kernels: 104 us -> 95 us
  local copies, waits for them, and re-layouts: 2.69 us -> 0 us
    pallas_call x2, Pallas kernels: 104 us -> 95 us  [the longest x1 93.1 us: on_device(): pl.pallas_call(step_body, name='step', in_specs=[hbm] * 10, out_specs=[hb...]
    unnamed x6 -> x0, local copies, waits for them, and re-layouts: 2.69 us -> none
where the time goes in v6:
time: 96 us; the launch traced here: 95.8 us
  Pallas kernels  95 us (99%)
    pallas_call x1, Pallas kernels, on_device(): pl.pallas_call(step_body, name='step', in_specs=[hbm] * 10, out_specs=[hb...  93.1 us

profile of v6, /device:TPU:0, one launch (start us, length us, event | category | flops | bytes accessed | tf_op | source)
XLA Modules:
  0.0 95.8 jit_solution(15579488079253516146)
XLA Ops:
  0.6 93.1 %step.1 = (f32[349,256]{1,0:T(8,128)}, f32[1,128]{1,0:T(1,128)}, f32[36,512]{1,0:T(8,128)}, f32[36,349]{1,0:T(8,128)}) custom-call(bf16[256,512]{1,0:T(8,128)(2,1)} %own_hbm.1, bf16[9,512,512]{2,1,0:T(8,128)(2,1)} %w_one_hbm.1, bf16[349,8,512]{2,1,0:T(8,128)(2,1)} %bitcast.8, bf16[349,512]{1,0:T(8,128)(2,1)} %bitcast.9, s32[8,2,256]{2,1,0:T(2,128)} %src_hbm.1, ...), custom_call_target="tpu_custom_call" | custom-call | tf_op jit(solution)/shard_map/step/pallas_call | solution.py:682
  93.8 1.8 %finish.1 = (f32[349,256]{1,0:T(8,128)}, f32[1,1]{1,0:T(1,128)}, f32[36,512]{1,0:T(8,128)}, f32[36,349]{1,0:T(8,128)}) custom-call(f32[349,256]{1,0:T(8,128)} %get-tuple-element.12.a, f32[1,128]{1,0:T(1,128)} %get-tuple-element.13.b, f32[36,512]{1,0:T(8,128)} %get-tuple-element.14.c, f32[36,349]{1,0:T(8,128)} %get-tuple-element.15.d), custom_call_target="tpu_custom_call" | custom-call | tf_op jit(solution)/shard_map/finish/pallas_call | solution.py:697

commit v7 on v6

--- a/solution.py
+++ b/solution.py
@@ -34,15 +34,16 @@
 
 STREAMS = (
     (0, 0, 36, (0, 1, 2)),
-    (384, 0, 16, (0, 1, 2)),
+    (384, 0, 24, (0, 1, 2)),
     (128, 0, 36, (1, 2, 0)),
-    (384, 16, 20, (1, 2, 0)),
+    (384, 24, 12, (1, 2, 0)),
     (256, 0, 36, (2, 0, 1)),
     (512, 0, 36, (0, 1, 2)),
     (640, 0, 36, (1, 2, 0)),
     (768, 0, 36, (2, 0, 1)),
 )
 ONE_X, ONE_REST, TWO = (0, 1), (2, 3, 4), (5, 6, 7)
+READY = (5, 6, 7, 0, 1, 4, 2, 3)
 
 
 def hops(code):
@@ -101,7 +102,7 @@
     logits_t, loss, grad_one, grad_two,
     own, src, dst, rows, count, labels, w_one, w_two, w_two_raw, turned, w_self, where_src, row_code, adj, adj_t, norm, picks, picks_t,
     send, got_one, got_two, sums, avg, avg_one_t, avg_two_t,
-    pre, hidden, acc, logits_v, own_grad, spreads, grad, grad_pre,
+    pre, hidden, acc, logits_v, loss_v, one_v, two_v, own_grad, spreads, grad, grad_pre,
     small_out, counts, totals,
     parts, half, *rest_refs,
 ):
@@ -403,9 +404,7 @@
         )
 
     def add_near(x, z, lanes):
-        half[x, z, :, :, lanes] = (
-            parts[x, z, :, core, :, lanes].astype(F32) + half[x, z, :, :, lanes].astype(F32)
-        ).astype(BF)
+        half[x, z, :, :, lanes] += parts[x, z, :, core, :, lanes]
 
     two_lanes = pl.ds(D, CP)
     one_lanes = pl.ds(0, D)
@@ -416,24 +415,26 @@
 
     lax.fori_loop(0, REL, turn_two, 0)
 
-    def two_chunks(i, carry):
-        chunks(i // 2, i % 2, avg_two_t, grad, two_lanes)
-        return carry
-
-    lax.fori_loop(0, 8, two_chunks, 0)
-    two_copy = to_partner(slice(None), two_lanes, 4)
-    two_copy.start()
+    for x in range(4):
+
+        def two_chunks(i, carry):
+            chunks(x, i, avg_two_t, grad, two_lanes)
+            return carry
+
+        lax.fori_loop(0, 2, two_chunks, 0)
+        to_partner(x, two_lanes, 4 + x).start()
     logits_v[...] = acc[...].T[:C, :]
     logits_copy = pltpu.make_async_copy(logits_v, logits_t, w_sems.at[13])
     logits_copy.start()
     own_grad[...] = dot(adj_t[:N, :], spreads[...]) + dot(grad[:, :C], w_self[...])
-    two_copy.wait()
-
-    def add_two(i, carry):
-        add_near(i // 4, i % 4, two_lanes)
-        return carry
-
-    lax.fori_loop(0, 16, add_two, 0)
+    for x in range(4):
+        to_partner(x, two_lanes, 4 + x).wait()
+
+        def add_two(i, carry):
+            add_near(x, i, two_lanes)
+            return carry
+
+        lax.fori_loop(0, 4, add_two, 0, unroll=2)
 
     everyone(ahead, small_sender(1, totals))
     totals[0] = small_out[1]
@@ -445,7 +446,7 @@
 
     def cut(s, upper):
         _, row, rows_s, _ = STREAMS[s]
-        low = 16 if rows_s > 20 else 8
+        low = 16 if rows_s > 12 else 8
         return (row + low, low, rows_s - low) if upper else (row, 0, low)
 
     def first_at(s, k, row, size):
@@ -476,9 +477,7 @@
             _, k = to_axis(axis, 1 if forward else 3)
             row, inner, size = cut(s, not forward)
             at = first_at(s, k, row, size)
-            half[at] = (
-                half[at].astype(F32) + first_got[s][2, :, :, inner : inner + size, :].astype(F32)
-            ).astype(BF)
+            half[at] += first_got[s][2, :, :, inner : inner + size, :]
             first_hop(s, "both", forward).start()
 
     def hop(s, phase, j):
@@ -534,7 +533,7 @@
             add_near(k, i, one_lanes)
             return carry
 
-        lax.fori_loop(0, 4, add_one, 0)
+        lax.fori_loop(0, 4, add_one, 0, unroll=2)
         for s in ONE_X:
             if j == 2:
                 first_hop(s, "far", True).start()
@@ -546,17 +545,17 @@
     one_block(1)
     for s in TWO:
         relay(s)
+    one_block(3)
     one_near(2)
-    one_block(3)
+    one_block(0)
     one_near(1)
-    one_block(0)
     one_near(3)
     one_near(0)
     begin("t_near")
     for s in ONE_REST:
         first_start(s)
     begin("ta_relay")
-    for s in ONE_X + ONE_REST:
+    for s in READY[3:]:
         relay(s)
 
     def sum_first(s):
@@ -606,27 +605,36 @@
         return total
 
     begin("u_first")
-    for s in TWO:
-        sum_first(s)
-    begin("ua_first")
-    for s in ONE_X + ONE_REST:
+    for s in READY:
         sum_first(s)
     begin("v_second")
-    for s in TWO + ONE_X + ONE_REST:
+    for s in READY:
         sum_second(s)
     begin("w_third")
     small_wait(1)
-    loss[...] = jnp.broadcast_to(jnp.sum(totals[:, :, 0:1]) / labelled_count, (1, 128))
-    logits_copy.wait()
-    for s in TWO + ONE_X + ONE_REST:
+    loss_v[...] = jnp.broadcast_to(jnp.sum(totals[:, :, 0:1]) / labelled_count, (1, 128))
+    results = [logits_copy]
+
+    def result(value, out, at):
+        copy = pltpu.make_async_copy(value, out, w_sems.at[at])
+        copy.start()
+        results.append(copy)
+
+    result(loss_v, loss, 14)
+    for i, s in enumerate(READY):
         lane, row, rows_s, _ = STREAMS[s]
         total = sum_third(s)
         if lane < D:
-            grad_one[row : row + rows_s, lane : lane + 128] = total
+            one_v[row : row + rows_s, lane : lane + 128] = total
         else:
             lane -= D
             size = min(128, C - lane)
-            grad_two[:, lane : lane + size] = total[:, :size]
+            two_v[:, lane : lane + size] = total[:, :size]
+        if i == 2:
+            result(two_v, grad_two, 15)
+    result(one_v, grad_one, 16)
+    for copy in results:
+        copy.wait()
     begin(None)
 
 
@@ -660,7 +668,8 @@
         V((FAR, N), BF), V((N, FAR), BF),
         V((PEERS, SLOTS, D), BF), V((PEERS, SLOTS, D), BF), V((PEERS, SLOTS, D), BF),
         V((REL, N, D), F32), V((REL, N, D), BF), V(((REL + 1) * D, N), BF), V(((REL + 1) * D, N), BF),
-        V((N, D), F32), V((N, D), BF), V((N, CP), F32), V((C, N), F32), V((N, D), F32),
+        V((N, D), F32), V((N, D), BF), V((N, CP), F32), V((C, N), F32), V((1, 128), F32), V((ROWS, D), F32), V((ROWS, C), F32),
+        V((N, D), F32),
         V((REL * N, D), BF),
         V((N, CP), BF), V((N, D), BF),
         V((2, 1, 128), F32), V((PEERS, 1, 128), F32), V((PEERS, 1, 128), F32),
@@ -670,10 +679,10 @@
         *[V((3, 4, r, 128), BF) for r in rows],
         *[V((4, r, 128), BF) for r in rows],
         *[V((3, r, 128), BF) for r in rows],
-        pltpu.SemaphoreType.DMA((14,)),
+        pltpu.SemaphoreType.DMA((17,)),
         pltpu.SemaphoreType.DMA((3,)), pltpu.SemaphoreType.DMA((12,)),
         pltpu.SemaphoreType.DMA((2,)), pltpu.SemaphoreType.DMA((2,)),
-        pltpu.SemaphoreType.DMA((5,)), pltpu.SemaphoreType.DMA((5,)),
+        pltpu.SemaphoreType.DMA((8,)), pltpu.SemaphoreType.DMA((8,)),
         pltpu.SemaphoreType.DMA((96,)), pltpu.SemaphoreType.DMA((96,)),
     ]
     codes = np.concatenate(
@@ -683,7 +692,7 @@
         step_body,
         name="step",
         in_specs=[hbm] * 10,
-        out_specs=[hbm, vm, vm, vm],
+        out_specs=[hbm] * 4,
         out_shape=[sds((C, N), F32), sds((1, 128), F32), sds((ROWS, D), F32), sds((ROWS, C), F32)],
         scratch_shapes=scratch,
         compiler_params=pltpu.CompilerParams(

time: 96 us -> 94 us (0.979)
  Pallas kernels: 95 us -> 93 us
    pallas_call x1, Pallas kernels: 93.1 us -> 91.1 us  [on_device(): pl.pallas_call(step_body, name='step', in_specs=[hbm] * 10, out_specs=[hb...]
where the time goes in v7:
time: 94 us; the launch traced here: 93.8 us
  Pallas kernels  93 us (99%)
    pallas_call x1, Pallas kernels, on_device(): pl.pallas_call(step_body, name='step', in_specs=[hbm] * 10, out_specs=[hb...  91.1 us

profile of v7, /device:TPU:0, one launch (start us, length us, event | category | flops | bytes accessed | tf_op | source)
XLA Modules:
  0.0 93.8 jit_solution(25320576282079743)
XLA Ops:
  0.6 91.1 %step.1 = (f32[349,256]{1,0:T(8,128)}, f32[1,128]{1,0:T(1,128)}, f32[36,512]{1,0:T(8,128)}, f32[36,349]{1,0:T(8,128)}) custom-call(bf16[256,512]{1,0:T(8,128)(2,1)} %own_hbm.1, bf16[9,512,512]{2,1,0:T(8,128)(2,1)} %w_one_hbm.1, bf16[349,8,512]{2,1,0:T(8,128)(2,1)} %bitcast.8, bf16[349,512]{1,0:T(8,128)(2,1)} %bitcast.9, s32[8,2,256]{2,1,0:T(2,128)} %src_hbm.1, ...), custom_call_target="tpu_custom_call" | custom-call | tf_op jit(solution)/shard_map/step/pallas_call | solution.py:691
  91.8 1.8 %finish.1 = (f32[349,256]{1,0:T(8,128)}, f32[1,1]{1,0:T(1,128)}, f32[36,512]{1,0:T(8,128)}, f32[36,349]{1,0:T(8,128)}) custom-call(f32[349,256]{1,0:T(8,128)} %get-tuple-element.12.a, f32[1,128]{1,0:T(1,128)} %get-tuple-element.13.b, f32[36,512]{1,0:T(8,128)} %get-tuple-element.14.c, f32[36,349]{1,0:T(8,128)} %get-tuple-element.15.d), custom_call_target="tpu_custom_call" | custom-call | tf_op jit(solution)/shard_map/finish/pallas_call | solution.py:706

commit v8 on v7

--- a/solution.py
+++ b/solution.py
@@ -247,7 +247,7 @@
             norm[r, at, :] = jnp.broadcast_to(1.0 / jnp.maximum(live_edges, 1.0), (128, 128))
         return carry
 
-    lax.fori_loop(0, REL, relation, 0, unroll=UNROLL)
+    lax.fori_loop(0, REL, relation, 0)
     everyone(ahead, small_sender(0, counts))
     counts[0] = small_out[0]
     begin("f_local")
@@ -265,14 +265,14 @@
             sums[r] = dot(adj[r, :, :N], values[...]) + dot(columns(r, 0, 1), rows_of(got, 0, 1))
             return carry
 
-        lax.fori_loop(0, REL, near_rows, 0, unroll=UNROLL)
+        lax.fori_loop(0, REL, near_rows, 0, unroll=2)
         group_wait(got, which, 1)
 
         def middle_rows(r, carry):
             sums[r] += dot(columns(r, 1, 1), rows_of(got, 1, 1))
             return carry
 
-        lax.fori_loop(0, REL, middle_rows, 0, unroll=UNROLL)
+        lax.fori_loop(0, REL, middle_rows, 0, unroll=2)
 
     def averaged(r, got):
         total = sums[r] + dot(columns(r, 2, 2), rows_of(got, 2, 2))
@@ -317,7 +317,7 @@
         turn(r, avg_one_t)
         return carry
 
-    lax.fori_loop(0, REL, relation_t, 0, unroll=UNROLL)
+    lax.fori_loop(0, REL, relation_t, 0)
     begin("ja_weights")
 
     for i in range(11):

time: 94 us -> 93.8 us (level)
  no operation moved by 1% of the time
where the time goes in v8:
time: 93.8 us; the launch traced here: 93.6 us
  Pallas kernels  92.8 us (99%)
    pallas_call x1, Pallas kernels, on_device(): pl.pallas_call(step_body, name='step', in_specs=[hbm] * 10, out_specs=[hb...  91 us

profile of v8, /device:TPU:0, one launch (start us, length us, event | category | flops | bytes accessed | tf_op | source)
XLA Modules:
  0.0 93.6 jit_solution(16146724245503147246)
XLA Ops:
  0.6 91.0 %step.1 = (f32[349,256]{1,0:T(8,128)}, f32[1,128]{1,0:T(1,128)}, f32[36,512]{1,0:T(8,128)}, f32[36,349]{1,0:T(8,128)}) custom-call(bf16[256,512]{1,0:T(8,128)(2,1)} %own_hbm.1, bf16[9,512,512]{2,1,0:T(8,128)(2,1)} %w_one_hbm.1, bf16[349,8,512]{2,1,0:T(8,128)(2,1)} %bitcast.8, bf16[349,512]{1,0:T(8,128)(2,1)} %bitcast.9, s32[8,2,256]{2,1,0:T(2,128)} %src_hbm.1, ...), custom_call_target="tpu_custom_call" | custom-call | tf_op jit(solution)/shard_map/step/pallas_call | solution.py:691
  91.6 1.8 %finish.1 = (f32[349,256]{1,0:T(8,128)}, f32[1,1]{1,0:T(1,128)}, f32[36,512]{1,0:T(8,128)}, f32[36,349]{1,0:T(8,128)}) custom-call(f32[349,256]{1,0:T(8,128)} %get-tuple-element.12.a, f32[1,128]{1,0:T(1,128)} %get-tuple-element.13.b, f32[36,512]{1,0:T(8,128)} %get-tuple-element.14.c, f32[36,349]{1,0:T(8,128)} %get-tuple-element.15.d), custom_call_target="tpu_custom_call" | custom-call | tf_op jit(solution)/shard_map/finish/pallas_call | solution.py:706

commit v9 on v7

--- a/solution.py
+++ b/solution.py
@@ -39,11 +39,12 @@
     (384, 24, 12, (1, 2, 0)),
     (256, 0, 36, (2, 0, 1)),
     (512, 0, 36, (0, 1, 2)),
-    (640, 0, 36, (1, 2, 0)),
+    (640, 0, 24, (1, 2, 0)),
     (768, 0, 36, (2, 0, 1)),
+    (640, 24, 12, (2, 0, 1)),
 )
-ONE_X, ONE_REST, TWO = (0, 1), (2, 3, 4), (5, 6, 7)
-READY = (5, 6, 7, 0, 1, 4, 2, 3)
+ONE_X, ONE_REST, TWO = (0, 1), (2, 3, 4), (5, 6, 7, 8)
+READY = (5, 6, 7, 8, 0, 1, 4, 2, 3)
 
 
 def hops(code):
@@ -555,7 +556,7 @@
     for s in ONE_REST:
         first_start(s)
     begin("ta_relay")
-    for s in READY[3:]:
+    for s in READY[4:]:
         relay(s)
 
     def sum_first(s):
@@ -629,8 +630,8 @@
         else:
             lane -= D
             size = min(128, C - lane)
-            two_v[:, lane : lane + size] = total[:, :size]
-        if i == 2:
+            two_v[row : row + rows_s, lane : lane + size] = total[:, :size]
+        if i == 3:
             result(two_v, grad_two, 15)
     result(one_v, grad_one, 16)
     for copy in results:
@@ -683,7 +684,7 @@
         pltpu.SemaphoreType.DMA((3,)), pltpu.SemaphoreType.DMA((12,)),
         pltpu.SemaphoreType.DMA((2,)), pltpu.SemaphoreType.DMA((2,)),
         pltpu.SemaphoreType.DMA((8,)), pltpu.SemaphoreType.DMA((8,)),
-        pltpu.SemaphoreType.DMA((96,)), pltpu.SemaphoreType.DMA((96,)),
+        pltpu.SemaphoreType.DMA((108,)), pltpu.SemaphoreType.DMA((108,)),
     ]
     codes = np.concatenate(
         [np.arange(N)] + [N + SLOTS * code + np.arange(SLOTS) for code in ORDER]

time: 94 us -> 95.4 us (1.015)
  Pallas kernels: 93 us -> 94.4 us
    pallas_call x1, Pallas kernels: 91.1 us -> 92.6 us  [on_device(): pl.pallas_call(step_body, name='step', in_specs=[hbm] * 10, out_specs=[hb...]
where the time goes in v9:
time: 95.4 us; the launch traced here: 95.2 us
  Pallas kernels  94.4 us (99%)
    pallas_call x1, Pallas kernels, on_device(): pl.pallas_call(step_body, name='step', in_specs=[hbm] * 10, out_specs=[hb...  92.6 us

profile of v9, /device:TPU:0, one launch (start us, length us, event | category | flops | bytes accessed | tf_op | source)
XLA Modules:
  0.0 95.2 jit_solution(1375095439005887938)
XLA Ops:
  0.6 92.6 %step.1 = (f32[349,256]{1,0:T(8,128)}, f32[1,128]{1,0:T(1,128)}, f32[36,512]{1,0:T(8,128)}, f32[36,349]{1,0:T(8,128)}) custom-call(bf16[256,512]{1,0:T(8,128)(2,1)} %own_hbm.1, bf16[9,512,512]{2,1,0:T(8,128)(2,1)} %w_one_hbm.1, bf16[349,8,512]{2,1,0:T(8,128)(2,1)} %bitcast.8, bf16[349,512]{1,0:T(8,128)(2,1)} %bitcast.9, s32[8,2,256]{2,1,0:T(2,128)} %src_hbm.1, ...), custom_call_target="tpu_custom_call" | custom-call | tf_op jit(solution)/shard_map/step/pallas_call | solution.py:692
  93.2 1.8 %finish.1 = (f32[349,256]{1,0:T(8,128)}, f32[1,1]{1,0:T(1,128)}, f32[36,512]{1,0:T(8,128)}, f32[36,349]{1,0:T(8,128)}) custom-call(f32[349,256]{1,0:T(8,128)} %get-tuple-element.12.a, f32[1,128]{1,0:T(1,128)} %get-tuple-element.13.b, f32[36,512]{1,0:T(8,128)} %get-tuple-element.14.c, f32[36,349]{1,0:T(8,128)} %get-tuple-element.15.d), custom_call_target="tpu_custom_call" | custom-call | tf_op jit(solution)/shard_map/finish/pallas_call | solution.py:707
